TPU v7x, 32 devices: a whole 2x2x4 slice. The times are simulated.
32 devices in a mesh: row: 8 (over y, x, core), col: 4 (over z).
Axes of the slice: x: 2, y: 2, z: 4, core: 2. Of those that a mesh axis runs over, the one named last changes fastest.
Arguments:
- residual: bfloat16 [8, 4, 2048, 512], P('row', 'col'), may hold values from -6 to 6
- self_tiles: bfloat16 [8, 4, 2048, 2048], P('row', 'col'), may hold values from -0.09375 to 0.09375
- side_tiles: bfloat16 [8, 4, 2048, 2048], P('row', 'col'), may hold values from -0.09375 to 0.09375
- row_cluster_basis: bfloat16 [8, 4, 2048, 32], P('row', 'col'), may hold values from -0.125 to 0.125
- column_cluster_basis: bfloat16 [8, 4, 2048, 32], P('row', 'col'), may hold values from -1 to 1
- couplings: bfloat16 [8, 4, 64, 32, 32], P('row', 'col'), may hold values from -0.1875 to 0.1875
- near_side: int32 [8, 4], P('row', 'col'), may hold values from -1 to 1
- adm_targets: int32 [8, 4, 64], P('row', 'col'), may hold values from 0 to 31, as said below
- adm_ranks: int32 [8, 4, 64], P('row', 'col'), may hold values from 8 to 32
- adm_count: int32 [8, 4], P('row', 'col'), may hold values from 1 to 64
Outputs:
- gradient: float32 [8, 4, 2048, 512], P('row', 'col')
Inputs may be any that keep to these rules, and one draw needn't show every extreme that they name: `near_side`: -1 or +1 names the cluster row before or after around the loop of 8 rows; 0 means no such tile. Each entry of adm_targets for the block row of linear index i is the linear index of a cluster other than i; slot 0 names i - 1 or i + 1, counted round the 32 clusters; targets may repeat.
All inputs are finite; a program needn't handle non-finite values.
Results may differ from a plain program's by a relative error of at most 0.0033.
Values may be sent and summed in bfloat16 or wider, within the bound.
No kernel may reach another device: no remote copies, remote signals or barrier semaphores. Data moves between devices by JAX's collectives and lax.ppermute only.
A program may use at most 128 MiB of HBM per device.

v0:
```python
import jax
import jax.numpy as jnp
from jax import lax
from jax.sharding import PartitionSpec as P


def with_halo(block, sides, width):
    for axis, dim in sides:
        count = lax.axis_size(axis)
        forward = [(i, i + 1) for i in range(count - 1)]
        forward.append((count - 1, 0))
        backward = [(target, source) for source, target in forward]
        low = lax.ppermute(
            lax.slice_in_dim(block, block.shape[dim] - width, None, axis=dim), axis, forward
        )
        high = lax.ppermute(lax.slice_in_dim(block, 0, width, axis=dim), axis, backward)
        block = jnp.concatenate([low, block, high], axis=dim)
    return block


def contract(tile, values):
    return lax.dot_general(
        tile, values, (((0,), (0,)), ((), ())), preferred_element_type=jnp.float32
    )


def on_device(
    residual,
    self_tiles,
    side_tiles,
    row_cluster_basis,
    column_cluster_basis,
    couplings,
    near_side,
    adm_targets,
    adm_ranks,
    adm_count,
):
    slot_count = couplings.shape[2]
    rank_dimension = couplings.shape[3]
    cluster_groups = lax.axis_size("row") * lax.axis_size("col")
    local_rows = residual[0, 0]
    coefficient_table = contract(row_cluster_basis[0, 0], local_rows).astype(jnp.bfloat16)
    rank_index = jnp.arange(rank_dimension, dtype=jnp.int32)
    slot_index = jnp.arange(slot_count, dtype=jnp.int32)
    keep_mask = (rank_index[None, :] < adm_ranks[0, 0][:, None]) & (slot_index < adm_count[0, 0])[
        :, None
    ]
    keep_float = keep_mask.astype(jnp.float32)
    masked = couplings[0, 0].astype(jnp.float32) * keep_float[:, :, None] * keep_float[:, None, :]
    onehot = (
        adm_targets[0, 0][:, None] == jnp.arange(cluster_groups, dtype=jnp.int32)[None, :]
    ).astype(jnp.float32)
    coupled_blocks = lax.dot_general(
        onehot,
        masked.reshape(slot_count, rank_dimension * rank_dimension),
        (((0,), (0,)), ((), ())),
        precision=lax.Precision.HIGHEST,
        preferred_element_type=jnp.float32,
    )
    coupled_blocks = coupled_blocks.reshape(cluster_groups, rank_dimension, rank_dimension)
    padded = with_halo(residual, (("row", 0),), 1)
    side_offset = near_side[0, 0]
    neighbour = lax.dynamic_index_in_dim(padded, side_offset + 1, 0, keepdims=False)[0]
    own_part = contract(self_tiles[0, 0], local_rows)
    side_part = contract(side_tiles[0, 0], neighbour) * (side_offset != 0).astype(jnp.float32)
    received = lax.all_to_all(
        coupled_blocks, ("row", "col"), split_axis=0, concat_axis=0, tiled=True
    )
    dual_sums = jnp.einsum(
        "cab,can->bn",
        received,
        lax.all_gather(coefficient_table[None], ("row", "col"), axis=0, tiled=True).astype(
            jnp.float32
        ),
        precision=lax.Precision.HIGHEST,
    )
    dual_vector = dual_sums.astype(jnp.bfloat16)
    distant_part = jnp.dot(
        column_cluster_basis[0, 0], dual_vector, preferred_element_type=jnp.float32
    )
    gradient = own_part + side_part + distant_part
    return gradient[None, None]


def solution(mesh):
    placed = (
        P("row", "col", None, None),
        P("row", "col", None, None),
        P("row", "col", None, None),
        P("row", "col", None, None),
        P("row", "col", None, None),
        P("row", "col", None, None, None),
        P("row", "col"),
        P("row", "col", None),
        P("row", "col", None),
        P("row", "col"),
    )
    return jax.shard_map(
        on_device,
        mesh=mesh,
        in_specs=placed,
        out_specs=P("row", "col", None, None),
        check_vma=False,
    )
```

profile of v0, /device:TPU:1, one launch (start us, length us, event | category | flops | bytes accessed | tf_op | source)
XLA Modules:
  0.0 91.6 jit_solution(10351635145926286116)
XLA Ops:
  6.5 0.0 copy-start
  6.5 0.0 copy-start.1
  6.5 0.0 all-gather.3.cloned.1.call-start
  6.5 2.6 %collective-permute-start = (bf16[1,1,2048,512]{3,2,1,0:T(8,128)(2,1)}, bf16[1,1,2048,512]{3,2,1,0:T(8,128)(2,1)}, u32[]{:S(2)}, u32[]{:S(2)}) collective-permute-start(bf16[1,1,2048,512]{3,2,1,0:T(8,128)(2,1)} %param.10), channel_id=1, source_target_pairs={{0,4},{4,8},{8,12},{12,16},{16,20},{20,24},{24,28},{28,0},{1,5},{5... | collective-permute-start | bytes 6291464 | tf_op jit(solution)/shard_map/ppermute | solution.py:13
  9.1 0.0 collective-permute-start.1
  9.1 2.8 %fusion.15 = bf16[32,512]{1,0:T(8,128)(2,1)} fusion(bf16[1,1,2048,512]{3,2,1,0:T(8,128)(2,1)} %param.10, bf16[1,1,2048,32]{2,3,1,0:T(8,128)(2,1)} %param.13), kind=kOutput, calls=%fused_computation.18 | convolution fusion | flops 67125248 | bytes 2260992 | tf_op jit(solution)/shard_map/dot_general | solution.py:22
  11.9 0.0 all-gather.3.cloned.1.call-update
  12.6 0.7 fusion.28
  13.2 1.0 %fusion.18 = f32[64,1024]{0,1:T(8,128)S(1)} fusion(bf16[1,1,64,32,32]{2,4,3,1,0:T(8,128)(2,1)} %param.15, f32[64,32]{0,1:T(8,128)S(1)} %fusion.28), kind=kLoop, calls=%fused_computation.20 | loop fusion | flops 196608 | bytes 401408 | tf_op jit(solution)/shard_map/mul | solution.py:50
  14.2 2.0 %fusion.24 = f32[32,32,32]{2,0,1:T(8,128)S(1)} fusion(f32[32,32,64]{2,1,0:T(8,128)S(1)} %bitcast.65, s32[64]{0:T(128)} %bitcast.67), kind=kOutput, calls=%fused_computation.27 | convolution fusion | flops 25169920 | bytes 393472 | tf_op jit(solution)/shard_map/dot_general | solution.py:54
  16.3 0.3 copy.14
  16.6 0.9 reshape.99
  17.5 6.2 %all-to-all-start = ((f32[32,1,1024]{2,1,0:T(1,128)}), f32[32,1,1024]{2,1,0:T(1,128)S(1)}, u32[]{:S(2)}, u32[]{:S(2)}) async-start(f32[32,1,1024]{2,1,0:T(1,128)} %reshape.99), calls=%async_computation | async-start | bytes 262144 | tf_op jit(solution)/shard_map/all_to_all | solution.py:67
  23.8 0.0 copy-done.1
  23.8 9.7 %fusion.2 = f32[2048,512]{1,0:T(8,128)} fusion(bf16[1,1,2048,2048]{3,2,1,0:T(8,128)(2,1)} %param.11, bf16[1,1,2048,512]{3,2,1,0:T(8,128)(2,1)S(1)} %copy-done.1), kind=kOutput, calls=%fused_computation.2 | convolution fusion | flops 4294967296 | bytes 14680064 | tf_op jit(solution)/shard_map/dot_general | solution.py:22
  34.2 26.9 %all-to-all-done = f32[32,1,1024]{2,1,0:T(1,128)S(1)} async-done(((f32[32,1,1024]{2,1,0:T(1,128)}), f32[32,1,1024]{2,1,0:T(1,128)S(1)}, u32[]{:S(2)}, u32[]{:S(2)}) %all-to-all-start) | async-done | bytes 131104 | tf_op jit(solution)/shard_map/all_to_all | solution.py:67
  61.1 0.6 broadcast.48
  61.7 1.0 %reduce = f32[32,1024]{1,0:T(8,128)S(1)} reduce(f32[32,1,1024]{2,1,0:T(1,128)S(1)} %all-to-all-done, f32[]{:T(128)} %broadcast.48), dimensions={1}, to_apply=%all_to_all.3.reduce_sub_computation | reduce | bytes 262148 | tf_op jit(solution)/shard_map/all_to_all | solution.py:67
  62.7 0.2 reshape.100
  62.8 7.0 %all-gather.3.cloned.1.call-done = bf16[1024,512]{1,0:T(8,128)(2,1)} async-done(((bf16[32,512]{1,0:T(8,128)(2,1)}), bf16[1024,512]{1,0:T(8,128)(2,1)}) %all-gather.3.cloned.1.call-update) | async-done | bytes 1048592 | tf_op jit(solution)/shard_map/all_gather | solution.py:73
  69.8 1.8 %fusion.14 = bf16[32,512]{1,0:T(8,128)(2,1)S(1)} fusion(f32[32,32,32]{2,1,0:T(8,128)S(1)} %reshape.100, bf16[32,32,512]{2,1,0:T(8,128)(2,1)} %bitcast.66), kind=kOutput, calls=%fused_computation.17 | convolution fusion | flops 201342976 | bytes 1212416 | tf_op jit(solution)/shard_map/cab,can->bn/dot_general | solution.py:70
  71.6 0.0 copy-done
  71.6 0.7 fusion.19
  72.4 0.0 collective-permute-done
  72.4 0.0 collective-permute-done.1
  72.4 12.3 %fusion.4 = f32[1,1,2048,512]{3,2,1,0:T(8,128)} fusion(f32[512,2048]{0,1:T(8,128)S(1)} %fusion.19, f32[2048,512]{1,0:T(8,128)} %fusion.2, bf16[1,1,2048,2048]{3,2,1,0:T(8,128)(2,1)} %param.12, s32[]{:T(128)S(6)} %select_n.4, bf16[1,1,2048,512]{3,2,1,0:T(8,128)(2,1)} %collective-permute-done, bf16[1,1,2048,512]{3,2,1,0:T(8,128)(2,1)S(1)} %copy-done.1, ...), kind=kOutput, calls=%fused_computation.8 | convolution fusion | flops 4300210176 | bytes 27262984 | tf_op jit(solution)/shard_map/dot_general | solution.py:22
  (1 shorter events, 0.0 us)
Async XLA Ops:
  6.5 65.1 %copy-start = (bf16[1,1,2048,32]{2,3,1,0:T(8,128)(2,1)S(1)}, bf16[1,1,2048,32]{2,3,1,0:T(8,128)(2,1)}, u32[]{:S(2)}) copy-start(bf16[1,1,2048,32]{2,3,1,0:T(8,128)(2,1)} %param.14) | copy-start | bytes 393220
  6.5 17.2 %copy-start.1 = (bf16[1,1,2048,512]{3,2,1,0:T(8,128)(2,1)S(1)}, bf16[1,1,2048,512]{3,2,1,0:T(8,128)(2,1)}, u32[]{:S(2)}) copy-start(bf16[1,1,2048,512]{3,2,1,0:T(8,128)(2,1)} %param.10) | copy-start | bytes 6291460
  6.5 63.3 %all-gather.3.cloned.1.call-start = ((), (), s32[]{:S(2)}) async-start(), calls=%async_computation.1 | async-start | bytes 1081344 | tf_op jit(solution)/shard_map/all_gather | solution.py:73
  6.5 65.9 %collective-permute-start = (bf16[1,1,2048,512]{3,2,1,0:T(8,128)(2,1)}, bf16[1,1,2048,512]{3,2,1,0:T(8,128)(2,1)}, u32[]{:S(2)}, u32[]{:S(2)}) collective-permute-start(bf16[1,1,2048,512]{3,2,1,0:T(8,128)(2,1)} %param.10), channel_id=1, source_target_pairs={{0,4},{4,8},{8,12},{12,16},{16,20},{20,24},{24,28},{28,0},{1,5},{5... | collective-permute-start | bytes 6291464 | tf_op jit(solution)/shard_map/ppermute | solution.py:13
  9.1 63.3 %collective-permute-start.1 = (bf16[1,1,2048,512]{3,2,1,0:T(8,128)(2,1)}, bf16[1,1,2048,512]{3,2,1,0:T(8,128)(2,1)}, u32[]{:S(2)}, u32[]{:S(2)}) collective-permute-start(bf16[1,1,2048,512]{3,2,1,0:T(8,128)(2,1)} %param.10), channel_id=1, source_target_pairs={{4,0},{8,4},{12,8},{16,12},{20,16},{24,20},{28,24},{0,28},{5,1},{9... | collective-permute-start | bytes 6291464 | tf_op jit(solution)/shard_map/ppermute | solution.py:16
  17.5 43.5 %all-to-all-start = ((f32[32,1,1024]{2,1,0:T(1,128)}), f32[32,1,1024]{2,1,0:T(1,128)S(1)}, u32[]{:S(2)}, u32[]{:S(2)}) async-start(f32[32,1,1024]{2,1,0:T(1,128)} %reshape.99), calls=%async_computation | async-start | bytes 262144 | tf_op jit(solution)/shard_map/all_to_all | solution.py:67
Sparse Core Ops, SparseCore 0:
  12.0 57.7 all-gather.2
where the time goes:
time: 92.1 us; the launch traced here: 91.6 us
  waiting for transfers between devices  33.9 us (37%)
  matrix products  29.4 us (32%)
  between operations  14.8 us (16%)
  starting transfers between devices  8.84 us (10%)
  other arithmetic  2.67 us (3%)
  local copies, waits for them, and re-layouts  1.98 us (2%)
    all_to_all x1, waiting for transfers between devices, on_device(): lax.all_to_all(coupled_blocks, ('row', 'col'), split_axis=0, concat_axis=...  26.9 us
    dot_general x3, matrix products, contract(): lax.dot_general(tile, values, (((0,), (0,)), ((), ())), preferred_element...  24.8 us
    all_gather x1, waiting for transfers between devices, on_device(): lax.all_gather(coefficient_table[None], ('row', 'col'), axis=0, tiled=True)  6.99 us
    all_to_all x1, starting transfers between devices, on_device(): lax.all_to_all(coupled_blocks, ('row', 'col'), split_axis=0, concat_axis=...  6.24 us
    ppermute x1, starting transfers between devices, with_halo(): lax.ppermute(lax.slice_in_dim(block, block.shape[dim] - width, None, axis...  2.59 us
    dot_general x1, matrix products, on_device(): lax.dot_general(onehot, masked.reshape(slot_count, rank_dimension * rank_...  2.04 us
  transfers between devices with their start and end apart: 4, of which 2 were waited for; matrix products, arithmetic and copies ran while one was open for 24% of the time, Pallas kernels for 0%

commit v1 on v0

v1 whole, which is shorter than its diff:
```python
import jax
import jax.numpy as jnp
from jax import lax
from jax.sharding import PartitionSpec as P

CHUNKS = 8


def contract(tile, values):
    return lax.dot_general(
        tile, values, (((0,), (0,)), ((), ())), preferred_element_type=jnp.float32
    )


def dual_of(coefficients, couplings, targets, ranks, count):
    rows, cols = lax.axis_size("row"), lax.axis_size("col")
    slots, rank, _ = couplings.shape
    rank_index = jnp.arange(rank, dtype=jnp.int32)
    slot_index = jnp.arange(slots, dtype=jnp.int32)
    keep = (rank_index[None, :] < ranks[:, None]) & (slot_index < count)[:, None]
    keep = keep.astype(jnp.bfloat16)
    masked = couplings * keep[:, :, None] * keep[:, None, :]
    onehot = (targets[:, None] == jnp.arange(rows * cols, dtype=jnp.int32)[None, :]).astype(
        jnp.bfloat16
    )
    blocks = contract(onehot, masked.reshape(slots, rank * rank)).astype(jnp.bfloat16)
    blocks = blocks.reshape(rows, cols, rank, rank).transpose(1, 2, 0, 3)
    blocks = blocks.reshape(cols, rank, rows * rank)
    packed = jnp.concatenate(
        [jnp.broadcast_to(coefficients[None], (cols,) + coefficients.shape), blocks], axis=2
    )
    me = lax.axis_index("col")
    held = [lax.dynamic_index_in_dim(packed, me, 0, keepdims=False)]
    for shift in range(1, cols):
        outgoing = lax.dynamic_index_in_dim(packed, (me + shift) % cols, 0, keepdims=False)
        held.append(
            lax.ppermute(outgoing, "col", [(i, (i + shift) % cols) for i in range(cols)])
        )
    held = jnp.concatenate(held, axis=0)
    width = coefficients.shape[1]
    partial = contract(held[:, width:], held[:, :width])
    bits = rows.bit_length() - 1
    current = partial.reshape((2,) * bits + (rank, width))
    mine = lax.axis_index("row")
    left = list(range(bits))[::-1]
    for bit in [0] + list(range(bits - 1, 0, -1)):
        axis = left.index(bit)
        left.remove(bit)
        low = lax.index_in_dim(current, 0, axis, keepdims=False)
        high = lax.index_in_dim(current, 1, axis, keepdims=False)
        upper = (mine >> bit) & 1 == 1
        outgoing = jnp.where(upper, low, high).astype(jnp.bfloat16)
        kept = jnp.where(upper, high, low)
        incoming = lax.ppermute(outgoing, "row", [(i, i ^ (1 << bit)) for i in range(rows)])
        current = kept + incoming.astype(jnp.float32)
    return current.astype(jnp.bfloat16)


def on_device(
    residual,
    self_tiles,
    side_tiles,
    row_cluster_basis,
    column_cluster_basis,
    couplings,
    near_side,
    adm_targets,
    adm_ranks,
    adm_count,
):
    rows = lax.axis_size("row")
    local = residual[0, 0]
    points = local.shape[0]
    size = points // CHUNKS
    near_pairs = [(i, i ^ 1) for i in range(rows)]
    far_pairs = [(i, (i - 1) % rows if i % 2 == 0 else (i + 1) % rows) for i in range(rows)]
    side_offset = near_side[0, 0]
    near_offset = 1 - 2 * (lax.axis_index("row") % 2)
    use_near = side_offset == near_offset
    use_far = side_offset == -near_offset

    far = []
    for c in range(CHUNKS):
        piece = lax.slice_in_dim(local, c * size, (c + 1) * size)
        far.append(lax.ppermute(piece, "row", far_pairs))
    near = lax.ppermute(local, "row", near_pairs)
    coefficients = contract(row_cluster_basis[0, 0], local).astype(jnp.bfloat16)
    dual = dual_of(
        coefficients, couplings[0, 0], adm_targets[0, 0], adm_ranks[0, 0], adm_count[0, 0]
    )
    total = contract(self_tiles[0, 0], local)
    zero = jnp.zeros((), jnp.bfloat16)
    for c in range(CHUNKS):
        here = lax.slice_in_dim(near, c * size, (c + 1) * size)
        values = jnp.where(use_far, far[c], jnp.where(use_near, here, zero))
        tile = lax.slice_in_dim(side_tiles[0, 0], c * size, (c + 1) * size)
        total = lax.optimization_barrier(total)
        total = total + contract(tile, values)
        if c == CHUNKS - 2:
            total = lax.optimization_barrier(total)
            total = total + jnp.dot(
                column_cluster_basis[0, 0], dual, preferred_element_type=jnp.float32
            )
    return total[None, None]


def solution(mesh):
    placed = (
        P("row", "col", None, None),
        P("row", "col", None, None),
        P("row", "col", None, None),
        P("row", "col", None, None),
        P("row", "col", None, None),
        P("row", "col", None, None, None),
        P("row", "col"),
        P("row", "col", None),
        P("row", "col", None),
        P("row", "col"),
    )

    return jax.shard_map(
        on_device,
        mesh=mesh,
        in_specs=placed,
        out_specs=P("row", "col", None, None),
        check_vma=False,
    )
```

time: 92.1 us -> 78.4 us (0.85)
  the two profiles are of different devices: /device:TPU:1 before, /device:TPU:0 now
where the time goes in v1:
time: 78.4 us; the launch traced here: 78 us
  matrix products  30.3 us (39%)
  starting transfers between devices  17.7 us (23%)
  waiting for transfers between devices  16 us (20%)
  other arithmetic  8.97 us (11%)
  local copies, waits for them, and re-layouts  3.12 us (4%)
  between operations  1.82 us (2%)
    dot_general x12, matrix products, contract(): lax.dot_general(tile, values, (((0,), (0,)), ((), ())), preferred_element...  29.6 us
    ppermute x8, starting transfers between devices, on_device(): far.append(lax.ppermute(piece, 'row', far_pairs))  9.14 us
    ppermute x3, waiting for transfers between devices, dual_of(): lax.ppermute(outgoing, 'row', [(i, i ^ 1 << bit) for i in range(rows)])  7.21 us
    ppermute x3, starting transfers between devices, dual_of(): lax.ppermute(outgoing, 'col', [(i, (i + shift) % cols) for i in range(col...  6.14 us
    add x6, other arithmetic, on_device(): total = total + contract(tile, values)  6.14 us
    ppermute x3, waiting for transfers between devices, dual_of(): lax.ppermute(outgoing, 'col', [(i, (i + shift) % cols) for i in range(col...  4.88 us
    ppermute x8, waiting for transfers between devices, on_device(): far.append(lax.ppermute(piece, 'row', far_pairs))  3.9 us
    ppermute x3, starting transfers between devices, dual_of(): lax.ppermute(outgoing, 'row', [(i, i ^ 1 << bit) for i in range(rows)])  1.73 us
  transfers between devices with their start and end apart: 15, of which 7 were waited for; matrix products, arithmetic and copies ran while one was open for 41% of the time, Pallas kernels for 0%

profile of v1, /device:TPU:0, one launch (start us, length us, event | category | flops | bytes accessed | tf_op | source)
XLA Modules:
  0.0 78.0 jit_solution(9303713568215496868)
XLA Ops:
  4.0 2.1 %convolution_convert_fusion.1 = bf16[32,512]{1,0:T(8,128)(2,1)S(1)} fusion(bf16[1,1,2048,32]{2,3,1,0:T(8,128)(2,1)} %param.13, bf16[1,1,2048,512]{3,2,1,0:T(8,128)(2,1)} %param.10), kind=kOutput, calls=%fused_computation.13 | convolution fusion | flops 67125248 | bytes 2260992 | tf_op jit(solution)/shard_map/dot_general | solution.py:10
  6.2 5.1 %collective-permute-start.10 = (bf16[32,768]{1,0:T(8,128)(2,1)S(1)}, bf16[32,768]{1,0:T(8,128)(2,1)S(1)}, u32[]{:S(2)}, u32[]{:S(2)}) collective-permute-start(bf16[32,768]{1,0:T(8,128)(2,1)S(1)} %get-tuple-element.16), channel_id=1, source_target_pairs={{0,3},{1,0},{2,1},{3,2},{4,7},{5,4},{6,5},{7,6},{8,11},{9,8},{10,9... | collective-permute-start | bytes 147464 | tf_op jit(solution)/shard_map/ppermute | solution.py:37
  11.3 1.0 %collective-permute-start.8 = (bf16[32,768]{1,0:T(8,128)(2,1)S(1)}, bf16[32,768]{1,0:T(8,128)(2,1)S(1)}, u32[]{:S(2)}, u32[]{:S(2)}) collective-permute-start(bf16[32,768]{1,0:T(8,128)(2,1)S(1)} %get-tuple-element.14), channel_id=1, source_target_pairs={{0,1},{1,2},{2,3},{3,0},{4,5},{5,6},{6,7},{7,4},{8,9},{9,10},{10,1... | collective-permute-start | bytes 147464 | tf_op jit(solution)/shard_map/ppermute | solution.py:37
  12.3 1.0 %collective-permute-done.10 = bf16[32,768]{1,0:T(8,128)(2,1)S(1)} collective-permute-done((bf16[32,768]{1,0:T(8,128)(2,1)S(1)}, bf16[32,768]{1,0:T(8,128)(2,1)S(1)}, u32[]{:S(2)}, u32[]{:S(2)}) %collective-permute-start.10) | collective-permute-done | bytes 49184 | tf_op jit(solution)/shard_map/ppermute | solution.py:37
  13.3 2.9 %collective-permute-done.9 = bf16[32,768]{1,0:T(8,128)(2,1)S(1)} collective-permute-done((bf16[32,768]{1,0:T(8,128)(2,1)S(1)}, bf16[32,768]{1,0:T(8,128)(2,1)S(1)}, u32[]{:S(2)}, u32[]{:S(2)}) %collective-permute-start.9) | collective-permute-done | bytes 49184 | tf_op jit(solution)/shard_map/ppermute | solution.py:37
  17.5 1.3 %collective-permute-done.11 = bf16[2,2,32,512]{3,2,1,0:T(8,128)(2,1)S(1)} collective-permute-done((bf16[2,2,32,512]{3,2,1,0:T(8,128)(2,1)S(1)}, bf16[2,2,32,512]{3,2,1,0:T(8,128)(2,1)S(1)}, u32[]{:S(2)}, u32[]{:S(2)}) %collective-permute-start.11) | collective-permute-done | bytes 131104 | tf_op jit(solution)/shard_map/ppermute | solution.py:54
  19.0 1.6 %collective-permute-start.12 = (bf16[2,32,512]{2,1,0:T(8,128)(2,1)S(1)}, bf16[2,32,512]{2,1,0:T(8,128)(2,1)S(1)}, u32[]{:S(2)}, u32[]{:S(2)}) collective-permute-start(bf16[2,32,512]{2,1,0:T(8,128)(2,1)S(1)} %fusion.73), channel_id=1, source_target_pairs={{0,16},{4,20},{8,24},{12,28},{16,0},{20,4},{24,8},{28,12},{1,17},{... | collective-permute-start | bytes 196616 | tf_op jit(solution)/shard_map/ppermute | solution.py:54
  20.5 1.3 %slice_bitcast_fusion = (bf16[256,512]{1,0:T(8,128)(2,1)}, bf16[256,512]{1,0:T(8,128)(2,1)}, bf16[256,512]{1,0:T(8,128)(2,1)}, bf16[256,512]{1,0:T(8,128)(2,1)},...) fusion(bf16[1,1,2048,512]{3,2,1,0:T(8,128)(2,1)S(1)} %copy-done.3), kind=kLoop, calls=%fused_computation.66 | loop fusion | bytes 4194304 | tf_op jit(solution)/shard_map/slice | solution.py:84
  23.5 1.0 %collective-permute-start.2 = (bf16[256,512]{1,0:T(8,128)(2,1)}, bf16[256,512]{1,0:T(8,128)(2,1)S(1)}, u32[]{:S(2)}, u32[]{:S(2)}) collective-permute-start(bf16[256,512]{1,0:T(8,128)(2,1)} %get-tuple-element.10), channel_id=1, source_target_pairs={{0,28},{4,8},{8,4},{12,16},{16,12},{20,24},{24,20},{28,0},{1,29},{... | collective-permute-start | bytes 786440 | tf_op jit(solution)/shard_map/ppermute | solution.py:85
  24.5 1.6 %collective-permute-start.3 = (bf16[256,512]{1,0:T(8,128)(2,1)}, bf16[256,512]{1,0:T(8,128)(2,1)S(1)}, u32[]{:S(2)}, u32[]{:S(2)}) collective-permute-start(bf16[256,512]{1,0:T(8,128)(2,1)} %get-tuple-element.9), channel_id=1, source_target_pairs={{0,28},{4,8},{8,4},{12,16},{16,12},{20,24},{24,20},{28,0},{1,29},{... | collective-permute-start | bytes 786440 | tf_op jit(solution)/shard_map/ppermute | solution.py:85
  26.3 9.7 %fusion = f32[2048,512]{1,0:T(8,128)} fusion(bf16[1,1,2048,2048]{3,2,1,0:T(8,128)(2,1)} %param.11, bf16[1,1,2048,512]{3,2,1,0:T(8,128)(2,1)S(1)} %copy-done.3), kind=kOutput, calls=%fused_computation | convolution fusion | flops 4294967296 | bytes 14680064 | tf_op jit(solution)/shard_map/dot_general | solution.py:10
  36.7 5.9 %collective-permute-done.13 = bf16[32,512]{1,0:T(8,128)(2,1)S(1)} collective-permute-done((bf16[32,512]{1,0:T(8,128)(2,1)S(1)}, bf16[32,512]{1,0:T(8,128)(2,1)S(1)}, u32[]{:S(2)}, u32[]{:S(2)}) %collective-permute-start.13) | collective-permute-done | bytes 32800 | tf_op jit(solution)/shard_map/ppermute | solution.py:54
  43.4 2.7 %collective-permute-start.5 = (bf16[256,512]{1,0:T(8,128)(2,1)}, bf16[256,512]{1,0:T(8,128)(2,1)S(1)}, u32[]{:S(2)}, u32[]{:S(2)}) collective-permute-start(bf16[256,512]{1,0:T(8,128)(2,1)} %get-tuple-element.7), channel_id=1, source_target_pairs={{0,28},{4,8},{8,4},{12,16},{16,12},{20,24},{24,20},{28,0},{1,29},{... | collective-permute-start | bytes 786440 | tf_op jit(solution)/shard_map/ppermute | solution.py:85
  46.2 2.1 %bitcast_add_fusion.8 = f32[2048,512]{1,0:T(8,128)S(1)} fusion(f32[2048,512]{1,0:T(8,128)S(1)} %copy-done.2, bf16[1,1,2048,2048]{3,2,1,0:T(8,128)(2,1)} %param.12, bf16[256,512]{1,0:T(8,128)(2,1)S(1)} %collective-permute-done, bf16[2048,512]{1,0:T(8,128)(2,1)} %collective-permute-done.1, pred[]{:T(512)S(6)} %eq.38, pred[]{:T(512)S(6)} %eq.37), kind=kOutput, calls=%fused_computation.11 | convolution fusion | flops 538181632 | bytes 9961474 | tf_op jit(solution)/shard_map/dot_general | solution.py:10
  48.3 2.7 %collective-permute-start.7 = (bf16[256,512]{1,0:T(8,128)(2,1)S(1)}, bf16[256,512]{1,0:T(8,128)(2,1)S(1)}, u32[]{:S(2)}, u32[]{:S(2)}) collective-permute-start(bf16[256,512]{1,0:T(8,128)(2,1)S(1)} %copy-done.5), channel_id=1, source_target_pairs={{0,28},{4,8},{8,4},{12,16},{16,12},{20,24},{24,20},{28,0},{1,29},{... | collective-permute-start | bytes 786440 | tf_op jit(solution)/shard_map/ppermute | solution.py:85
  51.0 2.2 %fusion.14 = f32[512,2048]{0,1:T(8,128)S(1)} fusion(bf16[1,1,2048,2048]{3,2,1,0:T(8,128)(2,1)} %param.12, bf16[256,512]{1,0:T(8,128)(2,1)S(1)} %collective-permute-done.2, bf16[2048,512]{1,0:T(8,128)(2,1)} %collective-permute-done.1, pred[]{:T(512)S(6)} %eq.38, pred[]{:T(512)S(6)} %eq.37), kind=kOutput, calls=%fused_computation.25 | convolution fusion | flops 537133056 | bytes 5767170 | tf_op jit(solution)/shard_map/dot_general | solution.py:10
  53.2 1.1 %bitcast_add_fusion.7 = f32[2048,512]{1,0:T(8,128)S(1)} fusion(f32[2048,512]{1,0:T(8,128)S(1)} %bitcast_add_fusion.8, f32[512,2048]{0,1:T(8,128)S(1)} %fusion.14), kind=kLoop, calls=%fused_computation.10 | loop fusion | flops 1048576 | bytes 12582912 | tf_op jit(solution)/shard_map/add | solution.py:98
  54.4 1.1 %slice-done.1 = s8[4194304]{0:T(1024)(128)(4,1)S(1)} async-done(((s8[8388608]{0:T(1024)(128)(4,1)}), s8[4194304]{0:T(1024)(128)(4,1)S(1)}, s32[]{:S(2)}) %slice-start.1) | async-done | bytes 4194328
  55.5 1.7 %fusion.12 = f32[512,2048]{0,1:T(8,128)S(1)} fusion(bf16[1,1,2048,2048]{3,2,1,0:T(8,128)(2,1)S(1)} %bitcast.138, bf16[256,512]{1,0:T(8,128)(2,1)S(1)} %collective-permute-done.3, bf16[2048,512]{1,0:T(8,128)(2,1)} %collective-permute-done.1, pred[]{:T(512)S(6)} %eq.38, pred[]{:T(512)S(6)} %eq.37), kind=kOutput, calls=%fused_computation.23 | convolution fusion | flops 537133056 | bytes 5767170 | tf_op jit(solution)/shard_map/dot_general | solution.py:10
  57.3 1.0 %bitcast_add_fusion.6 = f32[2048,512]{1,0:T(8,128)S(1)} fusion(f32[2048,512]{1,0:T(8,128)S(1)} %bitcast_add_fusion.7, f32[512,2048]{0,1:T(8,128)S(1)} %fusion.12), kind=kLoop, calls=%fused_computation.9 | loop fusion | flops 1048576 | bytes 12582912 | tf_op jit(solution)/shard_map/add | solution.py:98
  58.3 1.7 %fusion.10 = f32[512,2048]{0,1:T(8,128)S(1)} fusion(bf16[1,1,2048,2048]{3,2,1,0:T(8,128)(2,1)S(1)} %bitcast.138, bf16[256,512]{1,0:T(8,128)(2,1)S(1)} %collective-permute-done.4, bf16[2048,512]{1,0:T(8,128)(2,1)} %collective-permute-done.1, pred[]{:T(512)S(6)} %eq.38, pred[]{:T(512)S(6)} %eq.37), kind=kOutput, calls=%fused_computation.21 | convolution fusion | flops 537133056 | bytes 5767170 | tf_op jit(solution)/shard_map/dot_general | solution.py:10
  60.0 1.0 %bitcast_add_fusion.5 = f32[2048,512]{1,0:T(8,128)S(1)} fusion(f32[2048,512]{1,0:T(8,128)S(1)} %bitcast_add_fusion.6, f32[512,2048]{0,1:T(8,128)S(1)} %fusion.10), kind=kLoop, calls=%fused_computation.8 | loop fusion | flops 1048576 | bytes 12582912 | tf_op jit(solution)/shard_map/add | solution.py:98
  61.1 1.7 %fusion.8 = f32[512,2048]{0,1:T(8,128)S(1)} fusion(bf16[1,1,2048,2048]{3,2,1,0:T(8,128)(2,1)S(1)} %bitcast.138, bf16[256,512]{1,0:T(8,128)(2,1)S(1)} %collective-permute-done.5, bf16[2048,512]{1,0:T(8,128)(2,1)} %collective-permute-done.1, pred[]{:T(512)S(6)} %eq.38, pred[]{:T(512)S(6)} %eq.37), kind=kOutput, calls=%fused_computation.19 | convolution fusion | flops 537133056 | bytes 5767170 | tf_op jit(solution)/shard_map/dot_general | solution.py:10
  62.8 1.0 %bitcast_add_fusion.4 = f32[2048,512]{1,0:T(8,128)S(1)} fusion(f32[2048,512]{1,0:T(8,128)S(1)} %bitcast_add_fusion.5, f32[512,2048]{0,1:T(8,128)S(1)} %fusion.8), kind=kLoop, calls=%fused_computation.7 | loop fusion | flops 1048576 | bytes 12582912 | tf_op jit(solution)/shard_map/add | solution.py:98
  63.8 1.7 %fusion.6 = f32[512,2048]{0,1:T(8,128)S(1)} fusion(bf16[1,1,2048,2048]{3,2,1,0:T(8,128)(2,1)S(1)} %bitcast.138, bf16[256,512]{1,0:T(8,128)(2,1)S(1)} %collective-permute-done.6, bf16[2048,512]{1,0:T(8,128)(2,1)} %collective-permute-done.1, pred[]{:T(512)S(6)} %eq.38, pred[]{:T(512)S(6)} %eq.37), kind=kOutput, calls=%fused_computation.17 | convolution fusion | flops 537133056 | bytes 5767170 | tf_op jit(solution)/shard_map/dot_general | solution.py:10
  65.5 1.0 %bitcast_add_fusion.3 = f32[2048,512]{1,0:T(8,128)S(1)} fusion(f32[2048,512]{1,0:T(8,128)S(1)} %bitcast_add_fusion.4, f32[512,2048]{0,1:T(8,128)S(1)} %fusion.6), kind=kLoop, calls=%fused_computation.6 | loop fusion | flops 1048576 | bytes 12582912 | tf_op jit(solution)/shard_map/add | solution.py:98
  66.6 2.6 %collective-permute-done.7 = bf16[256,512]{1,0:T(8,128)(2,1)S(1)} collective-permute-done((bf16[256,512]{1,0:T(8,128)(2,1)S(1)}, bf16[256,512]{1,0:T(8,128)(2,1)S(1)}, u32[]{:S(2)}, u32[]{:S(2)}) %collective-permute-start.7) | collective-permute-done | bytes 262176 | tf_op jit(solution)/shard_map/ppermute | solution.py:85
  69.2 1.7 %fusion.4 = f32[512,2048]{0,1:T(8,128)S(1)} fusion(bf16[1,1,2048,2048]{3,2,1,0:T(8,128)(2,1)S(1)} %bitcast.138, bf16[256,512]{1,0:T(8,128)(2,1)S(1)} %collective-permute-done.7, bf16[2048,512]{1,0:T(8,128)(2,1)} %collective-permute-done.1, pred[]{:T(512)S(6)} %eq.38, pred[]{:T(512)S(6)} %eq.37), kind=kOutput, calls=%fused_computation.15 | convolution fusion | flops 537133056 | bytes 5767170 | tf_op jit(solution)/shard_map/dot_general | solution.py:10
  70.9 1.0 %bitcast_add_fusion.2 = f32[2048,512]{1,0:T(8,128)S(1)} fusion(f32[2048,512]{1,0:T(8,128)S(1)} %bitcast_add_fusion.3, f32[512,2048]{0,1:T(8,128)S(1)} %fusion.4), kind=kLoop, calls=%fused_computation.5 | loop fusion | flops 1048576 | bytes 12582912 | tf_op jit(solution)/shard_map/add | solution.py:98
  71.9 1.0 %bitcast_add_fusion.1 = f32[2048,512]{1,0:T(8,128)S(1)} fusion(f32[2048,512]{1,0:T(8,128)S(1)} %bitcast_add_fusion.2, f32[512,2048]{0,1:T(8,128)S(1)} %fusion.62), kind=kLoop, calls=%fused_computation.4 | loop fusion | flops 1048576 | bytes 12582912 | tf_op jit(solution)/shard_map/add | solution.py:101
  72.9 1.3 %collective-permute-done.14 = bf16[256,512]{1,0:T(8,128)(2,1)S(1)} collective-permute-done((bf16[256,512]{1,0:T(8,128)(2,1)S(1)}, bf16[256,512]{1,0:T(8,128)(2,1)S(1)}, u32[]{:S(2)}, u32[]{:S(2)}) %collective-permute-start.14) | collective-permute-done | bytes 262176 | tf_op jit(solution)/shard_map/ppermute | solution.py:85
  74.2 3.7 %fusion.2 = f32[1,1,2048,512]{3,2,1,0:T(8,128)} fusion(f32[2048,512]{1,0:T(8,128)S(1)} %bitcast_add_fusion.1, bf16[1,1,2048,2048]{3,2,1,0:T(8,128)(2,1)S(1)} %bitcast.138, bf16[256,512]{1,0:T(8,128)(2,1)S(1)} %collective-permute-done.14, bf16[2048,512]{1,0:T(8,128)(2,1)} %collective-permute-done.1, pred[]{:T(512)S(6)} %eq.38, pred[]{:T(512)S(6)} %eq.37), kind=kOutput, calls=%fused_computation.3 | convolution fusion | flops 538181632 | bytes 9961474 | tf_op jit(solution)/shard_map/dot_general | solution.py:10
  (51 shorter events, 7.2 us)
Async XLA Ops:
  0.0 42.6 %copy-start = (bf16[1,1,2048,32]{2,3,1,0:T(8,128)(2,1)S(1)}, bf16[1,1,2048,32]{2,3,1,0:T(8,128)(2,1)}, u32[]{:S(2)}) copy-start(bf16[1,1,2048,32]{2,3,1,0:T(8,128)(2,1)} %param.14) | copy-start | bytes 393220
  0.0 20.5 %copy-start.3 = (bf16[1,1,2048,512]{3,2,1,0:T(8,128)(2,1)S(1)}, bf16[1,1,2048,512]{3,2,1,0:T(8,128)(2,1)}, u32[]{:S(2)}) copy-start(bf16[1,1,2048,512]{3,2,1,0:T(8,128)(2,1)} %param.10) | copy-start | bytes 6291460
  6.2 7.2 %collective-permute-start.10 = (bf16[32,768]{1,0:T(8,128)(2,1)S(1)}, bf16[32,768]{1,0:T(8,128)(2,1)S(1)}, u32[]{:S(2)}, u32[]{:S(2)}) collective-permute-start(bf16[32,768]{1,0:T(8,128)(2,1)S(1)} %get-tuple-element.16), channel_id=1, source_target_pairs={{0,3},{1,0},{2,1},{3,2},{4,7},{5,4},{6,5},{7,6},{8,11},{9,8},{10,9... | collective-permute-start | bytes 147464 | tf_op jit(solution)/shard_map/ppermute | solution.py:37
  11.3 5.0 %collective-permute-start.9 = (bf16[32,768]{1,0:T(8,128)(2,1)S(1)}, bf16[32,768]{1,0:T(8,128)(2,1)S(1)}, u32[]{:S(2)}, u32[]{:S(2)}) collective-permute-start(bf16[32,768]{1,0:T(8,128)(2,1)S(1)} %get-tuple-element.15), channel_id=1, source_target_pairs={{0,2},{1,3},{2,0},{3,1},{4,6},{5,7},{6,4},{7,5},{8,10},{9,11},{10,... | collective-permute-start | bytes 147464 | tf_op jit(solution)/shard_map/ppermute | solution.py:37
  11.3 5.9 %collective-permute-start.8 = (bf16[32,768]{1,0:T(8,128)(2,1)S(1)}, bf16[32,768]{1,0:T(8,128)(2,1)S(1)}, u32[]{:S(2)}, u32[]{:S(2)}) collective-permute-start(bf16[32,768]{1,0:T(8,128)(2,1)S(1)} %get-tuple-element.14), channel_id=1, source_target_pairs={{0,1},{1,2},{2,3},{3,0},{4,5},{5,6},{6,7},{7,4},{8,9},{9,10},{10,1... | collective-permute-start | bytes 147464 | tf_op jit(solution)/shard_map/ppermute | solution.py:37
  17.5 1.4 %collective-permute-start.11 = (bf16[2,2,32,512]{3,2,1,0:T(8,128)(2,1)S(1)}, bf16[2,2,32,512]{3,2,1,0:T(8,128)(2,1)S(1)}, u32[]{:S(2)}, u32[]{:S(2)}) collective-permute-start(bf16[2,2,32,512]{3,2,1,0:T(8,128)(2,1)S(1)} %fusion.59), channel_id=1, source_target_pairs={{0,4},{4,0},{8,12},{12,8},{16,20},{20,16},{24,28},{28,24},{1,5},{5... | collective-permute-start | bytes 393224 | tf_op jit(solution)/shard_map/ppermute | solution.py:54
  19.0 7.2 %collective-permute-start.12 = (bf16[2,32,512]{2,1,0:T(8,128)(2,1)S(1)}, bf16[2,32,512]{2,1,0:T(8,128)(2,1)S(1)}, u32[]{:S(2)}, u32[]{:S(2)}) collective-permute-start(bf16[2,32,512]{2,1,0:T(8,128)(2,1)S(1)} %fusion.73), channel_id=1, source_target_pairs={{0,16},{4,20},{8,24},{12,28},{16,0},{20,4},{24,8},{28,12},{1,17},{... | collective-permute-start | bytes 196616 | tf_op jit(solution)/shard_map/ppermute | solution.py:54
  21.9 21.5 %collective-permute-start = (bf16[256,512]{1,0:T(8,128)(2,1)}, bf16[256,512]{1,0:T(8,128)(2,1)S(1)}, u32[]{:S(2)}, u32[]{:S(2)}) collective-permute-start(bf16[256,512]{1,0:T(8,128)(2,1)} %get-tuple-element.11), channel_id=1, source_target_pairs={{0,28},{4,8},{8,4},{12,16},{16,12},{20,24},{24,20},{28,0},{1,29},{... | collective-permute-start | bytes 786440 | tf_op jit(solution)/shard_map/ppermute | solution.py:85
  22.8 23.3 %collective-permute-start.1 = (bf16[2048,512]{1,0:T(8,128)(2,1)S(1)}, bf16[2048,512]{1,0:T(8,128)(2,1)}, u32[]{:S(2)}, u32[]{:S(2)}) collective-permute-start(bf16[2048,512]{1,0:T(8,128)(2,1)S(1)} %bitcast.139), channel_id=1, source_target_pairs={{0,4},{4,0},{8,12},{12,8},{16,20},{20,16},{24,28},{28,24},{1,5},{5... | collective-permute-start | bytes 6291464 | tf_op jit(solution)/shard_map/ppermute | solution.py:86
  23.5 24.8 %collective-permute-start.2 = (bf16[256,512]{1,0:T(8,128)(2,1)}, bf16[256,512]{1,0:T(8,128)(2,1)S(1)}, u32[]{:S(2)}, u32[]{:S(2)}) collective-permute-start(bf16[256,512]{1,0:T(8,128)(2,1)} %get-tuple-element.10), channel_id=1, source_target_pairs={{0,28},{4,8},{8,4},{12,16},{16,12},{20,24},{24,20},{28,0},{1,29},{... | collective-permute-start | bytes 786440 | tf_op jit(solution)/shard_map/ppermute | solution.py:85
  24.5 29.7 %collective-permute-start.3 = (bf16[256,512]{1,0:T(8,128)(2,1)}, bf16[256,512]{1,0:T(8,128)(2,1)S(1)}, u32[]{:S(2)}, u32[]{:S(2)}) collective-permute-start(bf16[256,512]{1,0:T(8,128)(2,1)} %get-tuple-element.9), channel_id=1, source_target_pairs={{0,28},{4,8},{8,4},{12,16},{16,12},{20,24},{24,20},{28,0},{1,29},{... | collective-permute-start | bytes 786440 | tf_op jit(solution)/shard_map/ppermute | solution.py:85
  26.2 16.4 %collective-permute-start.13 = (bf16[32,512]{1,0:T(8,128)(2,1)S(1)}, bf16[32,512]{1,0:T(8,128)(2,1)S(1)}, u32[]{:S(2)}, u32[]{:S(2)}) collective-permute-start(bf16[32,512]{1,0:T(8,128)(2,1)S(1)} %fusion.90), channel_id=1, source_target_pairs={{0,8},{4,12},{8,0},{12,4},{16,24},{20,28},{24,16},{28,20},{1,9},{5... | collective-permute-start | bytes 98312 | tf_op jit(solution)/shard_map/ppermute | solution.py:54
  36.0 10.1 %copy-start.6 = (bf16[256,512]{1,0:T(8,128)(2,1)S(1)}, bf16[256,512]{1,0:T(8,128)(2,1)}, u32[]{:S(2)}) copy-start(bf16[256,512]{1,0:T(8,128)(2,1)} %get-tuple-element.6) | copy-start | bytes 786436
  36.7 9.5 %copy-start.2 = (f32[2048,512]{1,0:T(8,128)S(1)}, f32[2048,512]{1,0:T(8,128)}, u32[]{:S(2)}) copy-start(f32[2048,512]{1,0:T(8,128)} %fusion) | copy-start | bytes 12582916
  42.6 15.7 %collective-permute-start.4 = (bf16[256,512]{1,0:T(8,128)(2,1)}, bf16[256,512]{1,0:T(8,128)(2,1)S(1)}, u32[]{:S(2)}, u32[]{:S(2)}) collective-permute-start(bf16[256,512]{1,0:T(8,128)(2,1)} %get-tuple-element.8), channel_id=1, source_target_pairs={{0,28},{4,8},{8,4},{12,16},{16,12},{20,24},{24,20},{28,0},{1,29},{... | collective-permute-start | bytes 786440 | tf_op jit(solution)/shard_map/ppermute | solution.py:85
  43.4 17.7 %collective-permute-start.5 = (bf16[256,512]{1,0:T(8,128)(2,1)}, bf16[256,512]{1,0:T(8,128)(2,1)S(1)}, u32[]{:S(2)}, u32[]{:S(2)}) collective-permute-start(bf16[256,512]{1,0:T(8,128)(2,1)} %get-tuple-element.7), channel_id=1, source_target_pairs={{0,28},{4,8},{8,4},{12,16},{16,12},{20,24},{24,20},{28,0},{1,29},{... | collective-permute-start | bytes 786440 | tf_op jit(solution)/shard_map/ppermute | solution.py:85
  46.1 2.2 %copy-start.5 = (bf16[256,512]{1,0:T(8,128)(2,1)S(1)}, bf16[256,512]{1,0:T(8,128)(2,1)}, u32[]{:S(2)}) copy-start(bf16[256,512]{1,0:T(8,128)(2,1)} %get-tuple-element.12) | copy-start | bytes 786436
  46.1 17.7 %collective-permute-start.6 = (bf16[256,512]{1,0:T(8,128)(2,1)S(1)}, bf16[256,512]{1,0:T(8,128)(2,1)S(1)}, u32[]{:S(2)}, u32[]{:S(2)}) collective-permute-start(bf16[256,512]{1,0:T(8,128)(2,1)S(1)} %copy-done.6), channel_id=1, source_target_pairs={{0,28},{4,8},{8,4},{12,16},{16,12},{20,24},{24,20},{28,0},{1,29},{... | collective-permute-start | bytes 786440 | tf_op jit(solution)/shard_map/ppermute | solution.py:85
  48.3 20.9 %collective-permute-start.7 = (bf16[256,512]{1,0:T(8,128)(2,1)S(1)}, bf16[256,512]{1,0:T(8,128)(2,1)S(1)}, u32[]{:S(2)}, u32[]{:S(2)}) collective-permute-start(bf16[256,512]{1,0:T(8,128)(2,1)S(1)} %copy-done.5), channel_id=1, source_target_pairs={{0,28},{4,8},{8,4},{12,16},{16,12},{20,24},{24,20},{28,0},{1,29},{... | collective-permute-start | bytes 786440 | tf_op jit(solution)/shard_map/ppermute | solution.py:85
  51.0 3.4 %slice-start = ((s8[8388608]{0:T(1024)(128)(4,1)}), s8[4194304]{0:T(1024)(128)(4,1)S(1)}, s32[]{:S(2)}) async-start(s8[8388608]{0:T(1024)(128)(4,1)} %bitcast.137), calls=%async_computation | async-start | bytes 8388608
  53.2 1.1 %copy-start.4 = (bf16[256,512]{1,0:T(8,128)(2,1)S(1)}, bf16[256,512]{1,0:T(8,128)(2,1)}, u32[]{:S(2)}) copy-start(bf16[256,512]{1,0:T(8,128)(2,1)} %get-tuple-element.5) | copy-start | bytes 786436
  53.2 2.3 %slice-start.1 = ((s8[8388608]{0:T(1024)(128)(4,1)}), s8[4194304]{0:T(1024)(128)(4,1)S(1)}, s32[]{:S(2)}) async-start(s8[8388608]{0:T(1024)(128)(4,1)} %bitcast.137), calls=%async_computation.1 | async-start | bytes 8388608
  54.3 19.9 %collective-permute-start.14 = (bf16[256,512]{1,0:T(8,128)(2,1)S(1)}, bf16[256,512]{1,0:T(8,128)(2,1)S(1)}, u32[]{:S(2)}, u32[]{:S(2)}) collective-permute-start(bf16[256,512]{1,0:T(8,128)(2,1)S(1)} %copy-done.4), channel_id=1, source_target_pairs={{0,28},{4,8},{8,4},{12,16},{16,12},{20,24},{24,20},{28,0},{1,29},{... | collective-permute-start | bytes 786440 | tf_op jit(solution)/shard_map/ppermute | solution.py:85
  71.9 6.1 %copy-start.1 = (bf16[1,1,2048,32]{2,3,1,0:T(8,128)(2,1)S(1)}, bf16[1,1,2048,32]{2,3,1,0:T(8,128)(2,1)}, u32[]{:S(2)}) copy-start(bf16[1,1,2048,32]{2,3,1,0:T(8,128)(2,1)} %param.14) | copy-start | bytes 393220

commit v2 on v1

v2 whole, which is shorter than its diff:
```python
import jax
import jax.numpy as jnp
from jax import lax
from jax.experimental import pallas as pl
from jax.experimental.pallas import tpu as pltpu
from jax.sharding import PartitionSpec as P

BLOCK = 512
GRANT = 20 * 1024 * 1024


def contract(tile, values):
    return lax.dot_general(
        tile, values, (((0,), (0,)), ((), ())), preferred_element_type=jnp.float32
    )


def in_vmem(value):
    return pltpu.with_memory_space_constraint(value, pltpu.VMEM)


def in_hbm(value):
    return pltpu.with_memory_space_constraint(value, pltpu.HBM)


def whole():
    return pl.BlockSpec(memory_space=pltpu.VMEM)


def grant():
    return pltpu.CompilerParams(vmem_limit_bytes=GRANT)


def split_rows(values, bounds, keep):
    columns = values.shape[1]

    def kernel(values_ref, *rest):
        outs, held, sems = rest[: len(bounds)], rest[len(bounds) : -1], rest[-1]
        held = outs if keep else held
        reads = [
            pltpu.make_async_copy(values_ref.at[pl.ds(start, size)], ref, sems.at[c])
            for c, ((start, size), ref) in enumerate(zip(bounds, held))
        ]
        for read in reads:
            read.start()
        writes = []
        for c, read in enumerate(reads):
            read.wait()
            if not keep:
                write = pltpu.make_async_copy(held[c], outs[c], sems.at[c + len(bounds)])
                write.start()
                writes.append(write)
        for write in writes:
            write.wait()

    shapes = [(size, columns) for _, size in bounds]
    space = pltpu.VMEM if keep else pltpu.HBM
    scratch = [] if keep else [pltpu.VMEM(shape, values.dtype) for shape in shapes]
    return pl.pallas_call(
        kernel,
        in_specs=[pl.BlockSpec(memory_space=pltpu.HBM)],
        out_specs=[pl.BlockSpec(memory_space=space) for _ in bounds],
        out_shape=[space(shape, values.dtype) for shape in shapes],
        scratch_shapes=scratch + [pltpu.SemaphoreType.DMA((2 * len(bounds),))],
        compiler_params=grant(),
    )(in_hbm(values))


def own_product(tile, values, part, parts, total=None):
    points, columns = tile.shape[1], values.shape[1]
    block = min(BLOCK, points // parts)
    steps = points // parts // block
    first = part * steps

    def kernel(tile_ref, values_ref, *rest):
        rest[-1][...] = contract(tile_ref[...], values_ref[...])

    in_specs = [
        pl.BlockSpec((tile.shape[0], block), lambda i: (0, first + i)),
        whole(),
    ]
    arguments = [in_hbm(tile), in_vmem(values)]
    if total is not None:
        in_specs.append(pl.BlockSpec(memory_space=pltpu.HBM))
        arguments.append(in_hbm(total))
    return pl.pallas_call(
        kernel,
        grid=(steps,),
        in_specs=in_specs,
        out_specs=pl.BlockSpec((block, columns), lambda i: (first + i, 0)),
        out_shape=pltpu.HBM((points, columns), jnp.float32),
        input_output_aliases={} if total is None else {2: 0},
        compiler_params=grant(),
        cost_estimate=pl.CostEstimate(
            flops=2 * tile.size * columns // parts,
            bytes_accessed=4 * tile.size // parts,
            transcendentals=0,
        ),
    )(*arguments)


def step_rows(block):
    return pl.ds(pl.multiple_of(pl.program_id(0) * block, block), block)


def choose(which_ref, far_refs, near_ref, values_ref):
    @pl.when(which_ref[0] == 2)
    def _():
        row = 0
        for far_ref in far_refs:
            values_ref[row : row + far_ref.shape[0], :] = far_ref[...]
            row += far_ref.shape[0]

    @pl.when(which_ref[0] == 1)
    def _():
        values_ref[...] = near_ref[...]

    @pl.when(which_ref[0] == 0)
    def _():
        values_ref[...] = jnp.zeros_like(values_ref)


def prepare_last(tile, near, start, size):
    points, columns = tile.shape[1], near.shape[1]
    block = min(BLOCK, points)
    at = start // size

    def kernel(tile_ref, near_ref, flipped_ref, kept_ref):
        flipped_ref[step_rows(block), :] = tile_ref[...].T

        @pl.when(pl.program_id(0) == 0)
        def _():
            kept_ref[...] = near_ref[...]

    return pl.pallas_call(
        kernel,
        grid=(points // block,),
        in_specs=[
            pl.BlockSpec((size, block), lambda i: (at, i)),
            pl.BlockSpec((size, columns), lambda i: (at, 0)),
        ],
        out_specs=[whole(), whole()],
        out_shape=[
            pltpu.VMEM((points, size), tile.dtype),
            pltpu.VMEM((size, columns), near.dtype),
        ],
        compiler_params=grant(),
    )(in_hbm(tile), in_hbm(near))


def add_rows(total, tile, far, near, which, start, extra):
    points, columns = total.shape
    size = sum(piece.shape[0] for piece in far)
    block = min(BLOCK, points)
    at = start // size
    count = len(far)

    def kernel(which_ref, total_ref, tile_ref, near_ref, *rest):
        out_ref, values_ref = rest[-2:]
        basis_ref, kept_ref, incoming_ref = rest[count:-2]
        here = step_rows(block)

        @pl.when(pl.program_id(0) == 0)
        def _():
            choose(which_ref, rest[:count], near_ref, values_ref)

        dual = (kept_ref[...] + incoming_ref[...].astype(jnp.float32)).astype(jnp.bfloat16)
        result = total_ref[...] + contract(tile_ref[...], values_ref[...])
        out_ref[here, :] = result + contract(basis_ref[:, here], dual)

    in_specs = [
        pl.BlockSpec(memory_space=pltpu.SMEM),
        pl.BlockSpec((block, columns), lambda i: (i, 0)),
        pl.BlockSpec((size, block), lambda i: (at, i)),
        pl.BlockSpec((size, columns), lambda i: (at, 0)),
    ]
    in_specs += [pl.BlockSpec(piece.shape, lambda i: (0, 0)) for piece in far]
    in_specs += [whole() for _ in extra]
    return pl.pallas_call(
        kernel,
        grid=(points // block,),
        in_specs=in_specs,
        out_specs=whole(),
        out_shape=pltpu.VMEM((points, columns), jnp.float32),
        compiler_params=grant(),
        scratch_shapes=[pltpu.VMEM((size, columns), jnp.bfloat16)],
        cost_estimate=pl.CostEstimate(
            flops=2 * size * points * columns,
            bytes_accessed=2 * size * points + 8 * total.size,
            transcendentals=0,
        ),
    )(
        which,
        in_hbm(total),
        in_hbm(tile),
        in_hbm(near),
        *[in_hbm(piece) for piece in far],
        *[in_vmem(value) for value in extra],
    )


def add_last(total, flipped, far, near, which):
    points, columns = total.shape
    size = far.shape[0]
    block = min(BLOCK // 2, points)
    steps = points // block

    def kernel(which_ref, total_ref, flipped_ref, far_ref, near_ref, out_ref, *scratch):
        values_ref, staged_ref, sems = scratch
        choose(which_ref, [far_ref], near_ref, values_ref)
        copies = []
        for step in range(steps):
            rows = pl.ds(step * block, block)
            staged_ref[rows, :] = total_ref[rows, :] + jnp.dot(
                flipped_ref[rows, :], values_ref[...], preferred_element_type=jnp.float32
            )
            copy = pltpu.make_async_copy(staged_ref.at[rows], out_ref.at[rows], sems.at[step])
            copy.start()
            copies.append(copy)
        for copy in copies:
            copy.wait()

    return pl.pallas_call(
        kernel,
        in_specs=[pl.BlockSpec(memory_space=pltpu.SMEM)] + [whole() for _ in range(4)],
        out_specs=pl.BlockSpec(memory_space=pltpu.HBM),
        out_shape=jax.ShapeDtypeStruct((points, columns), jnp.float32),
        compiler_params=grant(),
        scratch_shapes=[
            pltpu.VMEM((size, columns), jnp.bfloat16),
            pltpu.VMEM((points, columns), jnp.float32),
            pltpu.SemaphoreType.DMA((steps,)),
        ],
        cost_estimate=pl.CostEstimate(
            flops=2 * size * points * columns,
            bytes_accessed=2 * size * points + 8 * total.size,
            transcendentals=0,
        ),
    )(which, in_vmem(total), in_vmem(flipped), in_vmem(far), in_vmem(near))


def coupling_blocks(couplings, targets, ranks, count, rows, cols):
    slots, rank, _ = couplings.shape
    rank_index = jnp.arange(rank, dtype=jnp.int32)
    slot_index = jnp.arange(slots, dtype=jnp.int32)
    keep = (rank_index[None, :] < ranks[:, None]) & (slot_index < count)[:, None]
    keep = keep.astype(jnp.bfloat16)
    masked = couplings * keep[:, :, None] * keep[:, None, :]
    onehot = (targets[:, None] == jnp.arange(rows * cols, dtype=jnp.int32)[None, :]).astype(
        jnp.bfloat16
    )
    blocks = contract(onehot, masked.reshape(slots, rank * rank)).astype(jnp.bfloat16)
    blocks = blocks.reshape(rows, cols, rank, rank).transpose(1, 2, 0, 3)
    return blocks.reshape(cols, rank, rows * rank)


def dual_of(coefficients, blocks, rows, cols):
    rank, width = coefficients.shape
    packed = jnp.concatenate(
        [jnp.broadcast_to(coefficients[None], (cols,) + coefficients.shape), blocks], axis=2
    )
    me = lax.axis_index("col")
    held = [lax.dynamic_index_in_dim(packed, me, 0, keepdims=False)]
    for shift in range(1, cols):
        outgoing = lax.dynamic_index_in_dim(packed, (me + shift) % cols, 0, keepdims=False)
        held.append(lax.ppermute(outgoing, "col", [(i, (i + shift) % cols) for i in range(cols)]))
    held = jnp.concatenate(held, axis=0)
    partial = contract(held[:, width:], held[:, :width])
    bits = rows.bit_length() - 1
    current = partial.reshape((2,) * bits + (rank, width))
    mine = lax.axis_index("row")
    left = list(range(bits))[::-1]
    order = [0] + list(range(bits - 1, 0, -1))
    for place, bit in enumerate(order):
        axis = left.index(bit)
        left.remove(bit)
        low = lax.index_in_dim(current, 0, axis, keepdims=False)
        high = lax.index_in_dim(current, 1, axis, keepdims=False)
        upper = (mine >> bit) & 1 == 1
        outgoing = jnp.where(upper, low, high).astype(jnp.bfloat16)
        kept = jnp.where(upper, high, low)
        incoming = lax.ppermute(outgoing, "row", [(i, i ^ (1 << bit)) for i in range(rows)])
        if place < bits - 1:
            current = kept + incoming.astype(jnp.float32)
    return kept, incoming


def on_device(
    residual,
    self_tiles,
    side_tiles,
    row_cluster_basis,
    column_cluster_basis,
    couplings,
    near_side,
    adm_targets,
    adm_ranks,
    adm_count,
):
    rows, cols = lax.axis_size("row"), lax.axis_size("col")
    local = residual[0, 0]
    points = local.shape[0]
    near_pairs = [(i, i ^ 1) for i in range(rows)]
    far_pairs = [(i, (i - 1) % rows if i % 2 == 0 else (i + 1) % rows) for i in range(rows)]
    side_offset = near_side[0, 0]
    near_offset = 1 - 2 * (lax.axis_index("row") % 2)
    which = jnp.where(
        side_offset == 0, 0, jnp.where(side_offset == near_offset, 1, 2)
    ).astype(jnp.int32).reshape(1)

    unit = points // 8
    bounds = [(0, unit), (unit, 5 * unit), (6 * unit, 2 * unit)]
    pieces = split_rows(local, bounds[:1], True)
    pieces += split_rows(local, bounds[1:], False)
    far = []
    for piece in pieces:
        far.append(lax.ppermute(piece, "row", far_pairs))
    near = lax.ppermute(local, "row", near_pairs)
    coefficients = contract(row_cluster_basis[0, 0], local).astype(jnp.bfloat16)
    blocks = coupling_blocks(
        couplings[0, 0], adm_targets[0, 0], adm_ranks[0, 0], adm_count[0, 0], rows, cols
    )
    kept, incoming = dual_of(coefficients, blocks, rows, cols)
    total = own_product(self_tiles[0, 0], local, 0, 2)
    total = own_product(self_tiles[0, 0], local, 1, 2, total)
    side = side_tiles[0, 0]
    flipped, near_last = prepare_last(side, near, *bounds[2])
    extra = (column_cluster_basis[0, 0].T, kept, incoming)
    total = add_rows(total, side, far[:2], near, which, bounds[0][0], extra)
    total = add_last(total, flipped, far[2], near_last, which)
    return total[None, None]


def solution(mesh):
    placed = (
        P("row", "col", None, None),
        P("row", "col", None, None),
        P("row", "col", None, None),
        P("row", "col", None, None),
        P("row", "col", None, None),
        P("row", "col", None, None, None),
        P("row", "col"),
        P("row", "col", None),
        P("row", "col", None),
        P("row", "col"),
    )

    return jax.shard_map(
        on_device,
        mesh=mesh,
        in_specs=placed,
        out_specs=P("row", "col", None, None),
        check_vma=False,
    )
```

time: 78.4 us -> 73.2 us (0.934)
  the two profiles are of different devices: /device:TPU:0 before, /device:TPU:1 now
where the time goes in v2:
time: 73.2 us; the launch traced here: 72.8 us
  Pallas kernels  27.3 us (37%)
  waiting for transfers between devices  26.3 us (36%)
  starting transfers between devices  12.6 us (17%)
  matrix products  2.53 us (3%)
  other arithmetic  1.69 us (2%)
  between operations  1.68 us (2%)
    ppermute x3, waiting for transfers between devices, on_device(): far.append(lax.ppermute(piece, 'row', far_pairs))  13.5 us
    ppermute x3, waiting for transfers between devices, dual_of(): lax.ppermute(outgoing, 'row', [(i, i ^ 1 << bit) for i in range(rows)])  12.9 us
    pallas_call x2, Pallas kernels, own_product(): pl.pallas_call(kernel, grid=(steps,), in_specs=in_specs, out_specs=pl.Blo...  10.2 us
    pallas_call x1, Pallas kernels, add_rows(): pl.pallas_call(kernel, grid=(points // block,), in_specs=in_specs, out_sp...  8.16 us
    ppermute x3, starting transfers between devices, dual_of(): lax.ppermute(outgoing, 'col', [(i, (i + shift) % cols) for i in range(col...  6.08 us
    ppermute x3, starting transfers between devices, on_device(): far.append(lax.ppermute(piece, 'row', far_pairs))  3.96 us
    pallas_call x2, Pallas kernels, split_rows(): pl.pallas_call(kernel, in_specs=[pl.BlockSpec(memory_space=pltpu.HBM)], o...  3.54 us
    pallas_call x1, Pallas kernels, prepare_last(): pl.pallas_call(kernel, grid=(points // block,), in_specs=[pl.BlockSpec((s...  2.96 us
  transfers between devices with their start and end apart: 10, of which 2 were waited for; matrix products, arithmetic and copies ran while one was open for 7% of the time, Pallas kernels for 34%

profile of v2, /device:TPU:1, one launch (start us, length us, event | category | flops | bytes accessed | tf_op | source)
XLA Modules:
  0.0 72.8 jit_solution(11301298303312857138)
XLA Ops:
  0.0 0.1 collective-permute-start
  0.8 0.1 copy-done
  0.9 2.0 %convolution_convert_fusion.1 = bf16[32,512]{1,0:T(8,128)(2,1)S(1)} fusion(bf16[1,1,2048,32]{2,3,1,0:T(8,128)(2,1)S(1)} %copy-done, bf16[1,1,2048,512]{3,2,1,0:T(8,128)(2,1)} %param.10), kind=kOutput, calls=%fused_computation.1 | convolution fusion | flops 67125248 | bytes 2260992 | tf_op jit(solution)/shard_map/dot_general | solution.py:13
  3.0 0.1 bitcast_multiply_fusion
  3.1 0.3 convolution_convert_fusion
  3.4 0.2 reshape.110
  3.5 0.2 copy.18
  3.7 0.2 reshape.111
  4.0 2.7 %collective-permute-start.3 = (bf16[32,768]{1,0:T(8,128)(2,1)S(1)}, bf16[32,768]{1,0:T(8,128)(2,1)S(1)}, u32[]{:S(2)}, u32[]{:S(2)}) collective-permute-start(bf16[32,768]{1,0:T(8,128)(2,1)S(1)} %get-tuple-element.14), channel_id=1, source_target_pairs={{0,1},{1,2},{2,3},{3,0},{4,5},{5,6},{6,7},{7,4},{8,9},{9,10},{10,1... | collective-permute-start | bytes 147464 | tf_op jit(solution)/shard_map/ppermute | solution.py:266
  6.7 2.3 %collective-permute-start.4 = (bf16[32,768]{1,0:T(8,128)(2,1)S(1)}, bf16[32,768]{1,0:T(8,128)(2,1)S(1)}, u32[]{:S(2)}, u32[]{:S(2)}) collective-permute-start(bf16[32,768]{1,0:T(8,128)(2,1)S(1)} %get-tuple-element.15), channel_id=1, source_target_pairs={{0,2},{1,3},{2,0},{3,1},{4,6},{5,7},{6,4},{7,5},{8,10},{9,11},{10,... | collective-permute-start | bytes 147464 | tf_op jit(solution)/shard_map/ppermute | solution.py:266
  9.0 1.1 %collective-permute-start.5 = (bf16[32,768]{1,0:T(8,128)(2,1)S(1)}, bf16[32,768]{1,0:T(8,128)(2,1)S(1)}, u32[]{:S(2)}, u32[]{:S(2)}) collective-permute-start(bf16[32,768]{1,0:T(8,128)(2,1)S(1)} %get-tuple-element.16), channel_id=1, source_target_pairs={{0,3},{1,0},{2,1},{3,2},{4,7},{5,4},{6,5},{7,6},{8,11},{9,8},{10,9... | collective-permute-start | bytes 147464 | tf_op jit(solution)/shard_map/ppermute | solution.py:266
  10.1 2.6 %shard_map.103 = (bf16[1280,512]{1,0:T(8,128)(2,1)}, bf16[512,512]{1,0:T(8,128)(2,1)}) custom-call(bf16[2048,512]{1,0:T(8,128)(2,1)} %bitcast.72), custom_call_target="tpu_custom_call" | custom-call | tf_op jit(solution)/shard_map/pallas_call | solution.py:59
  12.6 0.0 copy-start.1
  12.6 2.1 %collective-permute-start.2 = (bf16[1280,512]{1,0:T(8,128)(2,1)}, bf16[1280,512]{1,0:T(8,128)(2,1)}, u32[]{:S(2)}, u32[]{:S(2)}) collective-permute-start(bf16[1280,512]{1,0:T(8,128)(2,1)} %get-tuple-element.9), channel_id=1, source_target_pairs={{0,28},{4,8},{8,4},{12,16},{16,12},{20,24},{24,20},{28,0},{1,29},{... | collective-permute-start | bytes 3932168 | tf_op jit(solution)/shard_map/ppermute | solution.py:317
  14.8 1.0 %shard_map.102 = bf16[256,512]{1,0:T(8,128)(2,1)S(1)} custom-call(bf16[2048,512]{1,0:T(8,128)(2,1)} %bitcast.73), custom_call_target="tpu_custom_call" | custom-call | tf_op jit(solution)/shard_map/pallas_call | solution.py:59
  15.8 0.0 collective-permute-done.3
  15.8 0.2 collective-permute-start.1
  16.0 1.6 %collective-permute-start.9 = (bf16[512,512]{1,0:T(8,128)(2,1)}, bf16[512,512]{1,0:T(8,128)(2,1)S(1)}, u32[]{:S(2)}, u32[]{:S(2)}) collective-permute-start(bf16[512,512]{1,0:T(8,128)(2,1)} %get-tuple-element.11), channel_id=1, source_target_pairs={{0,28},{4,8},{8,4},{12,16},{16,12},{20,24},{24,20},{28,0},{1,29},{... | collective-permute-start | bytes 1572872 | tf_op jit(solution)/shard_map/ppermute | solution.py:317
  17.6 0.2 fusion.1
  17.9 1.4 %collective-permute-start.6 = (bf16[2,2,32,512]{3,2,1,0:T(8,128)(2,1)S(1)}, bf16[2,2,32,512]{3,2,1,0:T(8,128)(2,1)S(1)}, u32[]{:S(2)}, u32[]{:S(2)}) collective-permute-start(bf16[2,2,32,512]{3,2,1,0:T(8,128)(2,1)S(1)} %fusion), channel_id=1, source_target_pairs={{0,4},{4,0},{8,12},{12,8},{16,20},{20,16},{24,28},{28,24},{1,5},{5... | collective-permute-start | bytes 393224 | tf_op jit(solution)/shard_map/ppermute | solution.py:282
  19.3 5.1 %shard_map.100.rest_0_ = f32[2048,512]{1,0:T(8,128)} custom-call(bf16[2048,2048]{1,0:T(8,128)(2,1)} %bitcast.77, bf16[2048,512]{1,0:T(8,128)(2,1)S(1)} %bitcast.74), custom_call_target="tpu_custom_call" | custom-call | flops 2147483648 | bytes 8388608 | tf_op jit(solution)/shard_map/pallas_call | solution.py:86
  24.5 0.6 fusion.4
  25.1 0.2 collective-permute-start.7
  25.4 5.1 %shard_map.101.total_ref = f32[2048,512]{1,0:T(8,128)} custom-call(bf16[2048,2048]{1,0:T(8,128)(2,1)} %bitcast.78, bf16[2048,512]{1,0:T(8,128)(2,1)S(1)} %bitcast.75, f32[2048,512]{1,0:T(8,128)} %shard_map.100.rest_0_), custom_call_target="tpu_custom_call", output_to_operand_aliasing={{}: (2, {})} | custom-call | flops 2147483648 | bytes 8388608 | tf_op jit(solution)/shard_map/pallas_call | solution.py:86
  31.2 0.9 %bitcast_add_fusion.1 = f32[2,32,512]{2,1,0:T(8,128)S(1)} fusion(bf16[2,32,512]{2,1,0:T(8,128)(2,1)} %collective-permute-done.7, f32[2,2,32,512]{3,2,1,0:T(8,128)S(1)} %bitcast_add_fusion, pred[]{:T(512)S(6)} %eq.40), kind=kLoop, calls=%fused_computation.23 | loop fusion | flops 98304 | bytes 458753 | tf_op jit(solution)/shard_map/add | solution.py:284
  32.0 0.8 %collective-permute-start.8 = (bf16[32,512]{1,0:T(8,128)(2,1)S(1)}, bf16[32,512]{1,0:T(8,128)(2,1)S(1)}, u32[]{:S(2)}, u32[]{:S(2)}) collective-permute-start(bf16[32,512]{1,0:T(8,128)(2,1)S(1)} %fusion.20), channel_id=1, source_target_pairs={{0,8},{4,12},{8,0},{12,4},{16,24},{20,28},{24,16},{28,20},{1,9},{5... | collective-permute-start | bytes 98312 | tf_op jit(solution)/shard_map/ppermute | solution.py:282
  32.9 0.0 copy-start.2
  32.9 3.0 %shard_map.105 = (bf16[2048,512]{1,0:T(8,128)(2,1)S(1)}, bf16[512,512]{1,0:T(8,128)(2,1)S(1)}) custom-call(bf16[2048,2048]{1,0:T(8,128)(2,1)} %bitcast.79, bf16[2048,512]{1,0:T(8,128)(2,1)} %collective-permute-done.near_ref), custom_call_target="tpu_custom_call" | custom-call | tf_op jit(solution)/shard_map/pallas_call | solution.py:135
  35.9 13.5 %collective-permute-done.1.rest_0_ = bf16[256,512]{1,0:T(8,128)(2,1)S(1)} collective-permute-done((bf16[256,512]{1,0:T(8,128)(2,1)S(1)}, bf16[256,512]{1,0:T(8,128)(2,1)S(1)}, u32[]{:S(2)}, u32[]{:S(2)}) %collective-permute-start.1) | collective-permute-done | bytes 262176 | tf_op jit(solution)/shard_map/ppermute | solution.py:317
  49.3 12.8 %collective-permute-done.8.rest_4_ = bf16[32,512]{1,0:T(8,128)(2,1)S(1)} collective-permute-done((bf16[32,512]{1,0:T(8,128)(2,1)S(1)}, bf16[32,512]{1,0:T(8,128)(2,1)S(1)}, u32[]{:S(2)}, u32[]{:S(2)}) %collective-permute-start.8) | collective-permute-done | bytes 32800 | tf_op jit(solution)/shard_map/ppermute | solution.py:282
  62.2 8.2 %shard_map.104.total_ref = f32[2048,512]{1,0:T(8,128)S(1)} custom-call(s32[1]{0:T(128)} %bitcast.1.which_ref, f32[2048,512]{1,0:T(8,128)} %shard_map.101.total_ref, bf16[2048,2048]{1,0:T(8,128)(2,1)} %bitcast.80, bf16[2048,512]{1,0:T(8,128)(2,1)} %collective-permute-done.near_ref, bf16[256,512]{1,0:T(8,128)(2,1)} %copy-done.3, ...), custom_call_target="tpu_custom_call" | custom-call | flops 3221225472 | bytes 14680064 | tf_op jit(solution)/shard_map/pallas_call | solution.py:179
  70.4 2.4 %shard_map.106 = f32[2048,512]{1,0:T(8,128)} custom-call(s32[1]{0:T(128)} %bitcast.1.which_ref, f32[2048,512]{1,0:T(8,128)S(1)} %shard_map.104.total_ref, bf16[2048,512]{1,0:T(8,128)(2,1)S(1)} %get-tuple-element.10.flipped_ref, bf16[512,512]{1,0:T(8,128)(2,1)S(1)} %collective-permute-done.9.far_ref, bf16[512,512]{1,0:T(8,128)(2,1)S(1)} %get-tuple-element.12.near_ref), custom_call_target="tpu_custom_call" | custom-call | flops 1073741824 | bytes 10485760 | tf_op jit(solution)/shard_map/pallas_call | solution.py:223
  (26 shorter events, 0.2 us)
Async XLA Ops:
  0.0 0.9 %copy-start = (bf16[1,1,2048,32]{2,3,1,0:T(8,128)(2,1)S(1)}, bf16[1,1,2048,32]{2,3,1,0:T(8,128)(2,1)}, u32[]{:S(2)}) copy-start(bf16[1,1,2048,32]{2,3,1,0:T(8,128)(2,1)} %param.13) | copy-start | bytes 393220
  0.0 2.9 %copy-start.6 = (s32[1,1,64]{2,1,0:T(1,128)S(1)}, s32[1,1,64]{2,1,0:T(1,128)}, u32[]{:S(2)}) copy-start(s32[1,1,64]{2,1,0:T(1,128)} %param.18) | copy-start | bytes 772
  0.0 3.0 %copy-start.4 = (bf16[1,1,64,32,32]{2,4,3,1,0:T(8,128)(2,1)S(1)}, bf16[1,1,64,32,32]{2,4,3,1,0:T(8,128)(2,1)}, u32[]{:S(2)}) copy-start(bf16[1,1,64,32,32]{2,4,3,1,0:T(8,128)(2,1)} %param.15) | copy-start | bytes 393220
  0.0 3.0 %copy-start.5 = (s32[1,1,64]{2,1,0:T(1,128)S(1)}, s32[1,1,64]{2,1,0:T(1,128)}, u32[]{:S(2)}) copy-start(s32[1,1,64]{2,1,0:T(1,128)} %param.17) | copy-start | bytes 772
  0.0 32.9 %collective-permute-start = (bf16[2048,512]{1,0:T(8,128)(2,1)}, bf16[2048,512]{1,0:T(8,128)(2,1)}, u32[]{:S(2)}, u32[]{:S(2)}) collective-permute-start(bf16[2048,512]{1,0:T(8,128)(2,1)} %bitcast.71), channel_id=1, source_target_pairs={{0,4},{4,0},{8,12},{12,8},{16,20},{20,16},{24,28},{28,24},{1,5},{5... | collective-permute-start | bytes 6291464 | tf_op jit(solution)/shard_map/ppermute | solution.py:318
  4.0 11.8 %collective-permute-start.3 = (bf16[32,768]{1,0:T(8,128)(2,1)S(1)}, bf16[32,768]{1,0:T(8,128)(2,1)S(1)}, u32[]{:S(2)}, u32[]{:S(2)}) collective-permute-start(bf16[32,768]{1,0:T(8,128)(2,1)S(1)} %get-tuple-element.14), channel_id=1, source_target_pairs={{0,1},{1,2},{2,3},{3,0},{4,5},{5,6},{6,7},{7,4},{8,9},{9,10},{10,1... | collective-permute-start | bytes 147464 | tf_op jit(solution)/shard_map/ppermute | solution.py:266
  6.7 9.3 %collective-permute-start.4 = (bf16[32,768]{1,0:T(8,128)(2,1)S(1)}, bf16[32,768]{1,0:T(8,128)(2,1)S(1)}, u32[]{:S(2)}, u32[]{:S(2)}) collective-permute-start(bf16[32,768]{1,0:T(8,128)(2,1)S(1)} %get-tuple-element.15), channel_id=1, source_target_pairs={{0,2},{1,3},{2,0},{3,1},{4,6},{5,7},{6,4},{7,5},{8,10},{9,11},{10,... | collective-permute-start | bytes 147464 | tf_op jit(solution)/shard_map/ppermute | solution.py:266
  9.0 8.6 %collective-permute-start.5 = (bf16[32,768]{1,0:T(8,128)(2,1)S(1)}, bf16[32,768]{1,0:T(8,128)(2,1)S(1)}, u32[]{:S(2)}, u32[]{:S(2)}) collective-permute-start(bf16[32,768]{1,0:T(8,128)(2,1)S(1)} %get-tuple-element.16), channel_id=1, source_target_pairs={{0,3},{1,0},{2,1},{3,2},{4,7},{5,4},{6,5},{7,6},{8,11},{9,8},{10,9... | collective-permute-start | bytes 147464 | tf_op jit(solution)/shard_map/ppermute | solution.py:266
  12.6 6.7 %copy-start.1 = (bf16[1,1,2048,512]{3,2,1,0:T(8,128)(2,1)S(1)}, bf16[1,1,2048,512]{3,2,1,0:T(8,128)(2,1)}, u32[]{:S(2)}) copy-start(bf16[1,1,2048,512]{3,2,1,0:T(8,128)(2,1)} %param.10) | copy-start | bytes 6291460
  12.6 49.5 %collective-permute-start.2 = (bf16[1280,512]{1,0:T(8,128)(2,1)}, bf16[1280,512]{1,0:T(8,128)(2,1)}, u32[]{:S(2)}, u32[]{:S(2)}) collective-permute-start(bf16[1280,512]{1,0:T(8,128)(2,1)} %get-tuple-element.9), channel_id=1, source_target_pairs={{0,28},{4,8},{8,4},{12,16},{16,12},{20,24},{24,20},{28,0},{1,29},{... | collective-permute-start | bytes 3932168 | tf_op jit(solution)/shard_map/ppermute | solution.py:317
  15.8 33.6 %collective-permute-start.1 = (bf16[256,512]{1,0:T(8,128)(2,1)S(1)}, bf16[256,512]{1,0:T(8,128)(2,1)S(1)}, u32[]{:S(2)}, u32[]{:S(2)}) collective-permute-start(bf16[256,512]{1,0:T(8,128)(2,1)S(1)} %shard_map.102), channel_id=1, source_target_pairs={{0,28},{4,8},{8,4},{12,16},{16,12},{20,24},{24,20},{28,0},{1,29},{... | collective-permute-start | bytes 786440 | tf_op jit(solution)/shard_map/ppermute | solution.py:317
  16.0 54.4 %collective-permute-start.9 = (bf16[512,512]{1,0:T(8,128)(2,1)}, bf16[512,512]{1,0:T(8,128)(2,1)S(1)}, u32[]{:S(2)}, u32[]{:S(2)}) collective-permute-start(bf16[512,512]{1,0:T(8,128)(2,1)} %get-tuple-element.11), channel_id=1, source_target_pairs={{0,28},{4,8},{8,4},{12,16},{16,12},{20,24},{24,20},{28,0},{1,29},{... | collective-permute-start | bytes 1572872 | tf_op jit(solution)/shard_map/ppermute | solution.py:317
  17.9 6.6 %collective-permute-start.6 = (bf16[2,2,32,512]{3,2,1,0:T(8,128)(2,1)S(1)}, bf16[2,2,32,512]{3,2,1,0:T(8,128)(2,1)S(1)}, u32[]{:S(2)}, u32[]{:S(2)}) collective-permute-start(bf16[2,2,32,512]{3,2,1,0:T(8,128)(2,1)S(1)} %fusion), channel_id=1, source_target_pairs={{0,4},{4,0},{8,12},{12,8},{16,20},{20,16},{24,28},{28,24},{1,5},{5... | collective-permute-start | bytes 393224 | tf_op jit(solution)/shard_map/ppermute | solution.py:282
  25.1 6.0 %collective-permute-start.7 = (bf16[2,32,512]{2,1,0:T(8,128)(2,1)}, bf16[2,32,512]{2,1,0:T(8,128)(2,1)}, u32[]{:S(2)}, u32[]{:S(2)}) collective-permute-start(bf16[2,32,512]{2,1,0:T(8,128)(2,1)} %fusion.4), channel_id=1, source_target_pairs={{0,16},{4,20},{8,24},{12,28},{16,0},{20,4},{24,8},{28,12},{1,17},{... | collective-permute-start | bytes 196616 | tf_op jit(solution)/shard_map/ppermute | solution.py:282
  32.0 30.1 %collective-permute-start.8 = (bf16[32,512]{1,0:T(8,128)(2,1)S(1)}, bf16[32,512]{1,0:T(8,128)(2,1)S(1)}, u32[]{:S(2)}, u32[]{:S(2)}) collective-permute-start(bf16[32,512]{1,0:T(8,128)(2,1)S(1)} %fusion.20), channel_id=1, source_target_pairs={{0,8},{4,12},{8,0},{12,4},{16,24},{20,28},{24,16},{28,20},{1,9},{5... | collective-permute-start | bytes 98312 | tf_op jit(solution)/shard_map/ppermute | solution.py:282
  32.9 29.3 %copy-start.2 = (bf16[1,1,2048,32]{2,3,1,0:T(8,128)(2,1)S(1)}, bf16[1,1,2048,32]{2,3,1,0:T(8,128)(2,1)}, u32[]{:S(2)}) copy-start(bf16[1,1,2048,32]{2,3,1,0:T(8,128)(2,1)} %param.14) | copy-start | bytes 393220
  49.3 12.9 %copy-start.3 = (bf16[256,512]{1,0:T(8,128)(2,1)}, bf16[256,512]{1,0:T(8,128)(2,1)S(1)}, u32[]{:S(2)}) copy-start(bf16[256,512]{1,0:T(8,128)(2,1)S(1)} %collective-permute-done.1.rest_0_) | copy-start | bytes 786436

commit v3 on v2

--- a/solution.py
+++ b/solution.py
@@ -31,36 +31,33 @@
     return pltpu.CompilerParams(vmem_limit_bytes=GRANT)
 
 
-def split_rows(values, bounds, keep):
-    columns = values.shape[1]
-
+def split(values, bounds):
     def kernel(values_ref, *rest):
         outs, held, sems = rest[: len(bounds)], rest[len(bounds) : -1], rest[-1]
-        held = outs if keep else held
         reads = [
-            pltpu.make_async_copy(values_ref.at[pl.ds(start, size)], ref, sems.at[c])
-            for c, ((start, size), ref) in enumerate(zip(bounds, held))
+            pltpu.make_async_copy(
+                values_ref.at[pl.ds(row, size), pl.ds(column, width)], ref, sems.at[c]
+            )
+            for c, ((row, size, column, width), ref) in enumerate(zip(bounds, held))
         ]
         for read in reads:
             read.start()
         writes = []
         for c, read in enumerate(reads):
             read.wait()
-            if not keep:
-                write = pltpu.make_async_copy(held[c], outs[c], sems.at[c + len(bounds)])
-                write.start()
-                writes.append(write)
+            write = pltpu.make_async_copy(held[c], outs[c], sems.at[c + len(bounds)])
+            write.start()
+            writes.append(write)
         for write in writes:
             write.wait()
 
-    shapes = [(size, columns) for _, size in bounds]
-    space = pltpu.VMEM if keep else pltpu.HBM
-    scratch = [] if keep else [pltpu.VMEM(shape, values.dtype) for shape in shapes]
+    shapes = [(size, width) for _, size, _, width in bounds]
+    scratch = [pltpu.VMEM(shape, values.dtype) for shape in shapes]
     return pl.pallas_call(
         kernel,
         in_specs=[pl.BlockSpec(memory_space=pltpu.HBM)],
-        out_specs=[pl.BlockSpec(memory_space=space) for _ in bounds],
-        out_shape=[space(shape, values.dtype) for shape in shapes],
+        out_specs=[pl.BlockSpec(memory_space=pltpu.HBM) for _ in bounds],
+        out_shape=[pltpu.HBM(shape, values.dtype) for shape in shapes],
         scratch_shapes=scratch + [pltpu.SemaphoreType.DMA((2 * len(bounds),))],
         compiler_params=grant(),
     )(in_hbm(values))
@@ -199,44 +196,53 @@
     )
 
 
-def add_last(total, flipped, far, near, which):
+def add_last(total, flipped, far, near, which, column, out=None):
     points, columns = total.shape
-    size = far.shape[0]
+    size, width = far.shape
     block = min(BLOCK // 2, points)
     steps = points // block
-
-    def kernel(which_ref, total_ref, flipped_ref, far_ref, near_ref, out_ref, *scratch):
-        values_ref, staged_ref, sems = scratch
-        choose(which_ref, [far_ref], near_ref, values_ref)
+    here = pl.ds(column, width)
+
+    def kernel(which_ref, total_ref, flipped_ref, far_ref, near_ref, *rest):
+        out_ref, values_ref, staged_ref, sems = rest[-4:]
+        choose(which_ref, [far_ref], near_ref.at[:, here], values_ref)
         copies = []
         for step in range(steps):
             rows = pl.ds(step * block, block)
-            staged_ref[rows, :] = total_ref[rows, :] + jnp.dot(
+            staged_ref[rows, :] = total_ref[rows, here] + jnp.dot(
                 flipped_ref[rows, :], values_ref[...], preferred_element_type=jnp.float32
             )
-            copy = pltpu.make_async_copy(staged_ref.at[rows], out_ref.at[rows], sems.at[step])
+            copy = pltpu.make_async_copy(
+                staged_ref.at[rows], out_ref.at[rows, here], sems.at[step]
+            )
             copy.start()
             copies.append(copy)
         for copy in copies:
             copy.wait()
 
-    return pl.pallas_call(
-        kernel,
-        in_specs=[pl.BlockSpec(memory_space=pltpu.SMEM)] + [whole() for _ in range(4)],
+    arguments = [which] + [in_vmem(value) for value in (total, flipped, far, near)]
+    in_specs = [pl.BlockSpec(memory_space=pltpu.SMEM)] + [whole() for _ in range(4)]
+    if out is not None:
+        arguments.append(in_hbm(out))
+        in_specs.append(pl.BlockSpec(memory_space=pltpu.HBM))
+    return pl.pallas_call(
+        kernel,
+        in_specs=in_specs,
         out_specs=pl.BlockSpec(memory_space=pltpu.HBM),
         out_shape=jax.ShapeDtypeStruct((points, columns), jnp.float32),
+        input_output_aliases={} if out is None else {5: 0},
         compiler_params=grant(),
         scratch_shapes=[
-            pltpu.VMEM((size, columns), jnp.bfloat16),
-            pltpu.VMEM((points, columns), jnp.float32),
+            pltpu.VMEM((size, width), jnp.bfloat16),
+            pltpu.VMEM((points, width), jnp.float32),
             pltpu.SemaphoreType.DMA((steps,)),
         ],
         cost_estimate=pl.CostEstimate(
-            flops=2 * size * points * columns,
-            bytes_accessed=2 * size * points + 8 * total.size,
+            flops=2 * size * points * width,
+            bytes_accessed=2 * size * points + 8 * points * width,
             transcendentals=0,
         ),
-    )(which, in_vmem(total), in_vmem(flipped), in_vmem(far), in_vmem(near))
+    )(*arguments)
 
 
 def coupling_blocks(couplings, targets, ranks, count, rows, cols):
@@ -249,9 +255,11 @@
     onehot = (targets[:, None] == jnp.arange(rows * cols, dtype=jnp.int32)[None, :]).astype(
         jnp.bfloat16
     )
-    blocks = contract(onehot, masked.reshape(slots, rank * rank)).astype(jnp.bfloat16)
-    blocks = blocks.reshape(rows, cols, rank, rank).transpose(1, 2, 0, 3)
-    return blocks.reshape(cols, rank, rows * rank)
+    sums = contract(onehot, masked.reshape(slots, rank * rank))
+    high = lax.reduce_precision(sums, 8, 7)
+    parts = [high.astype(jnp.bfloat16), (sums - high).astype(jnp.bfloat16)]
+    blocks = jnp.stack(parts).reshape(2, rows, cols, rank, rank).transpose(2, 3, 0, 1, 4)
+    return blocks.reshape(cols, rank, 2 * rows * rank)
 
 
 def dual_of(coefficients, blocks, rows, cols):
@@ -265,7 +273,9 @@
         outgoing = lax.dynamic_index_in_dim(packed, (me + shift) % cols, 0, keepdims=False)
         held.append(lax.ppermute(outgoing, "col", [(i, (i + shift) % cols) for i in range(cols)]))
     held = jnp.concatenate(held, axis=0)
-    partial = contract(held[:, width:], held[:, :width])
+    half = width + rows * rank
+    partial = contract(held[:, width:half], held[:, :width])
+    partial = partial + contract(held[:, half:], held[:, :width])
     bits = rows.bit_length() - 1
     current = partial.reshape((2,) * bits + (rank, width))
     mine = lax.axis_index("row")
@@ -277,11 +287,13 @@
         low = lax.index_in_dim(current, 0, axis, keepdims=False)
         high = lax.index_in_dim(current, 1, axis, keepdims=False)
         upper = (mine >> bit) & 1 == 1
-        outgoing = jnp.where(upper, low, high).astype(jnp.bfloat16)
+        outgoing = jnp.where(upper, low, high)
         kept = jnp.where(upper, high, low)
+        if place == bits - 1:
+            outgoing = outgoing.astype(jnp.bfloat16)
         incoming = lax.ppermute(outgoing, "row", [(i, i ^ (1 << bit)) for i in range(rows)])
         if place < bits - 1:
-            current = kept + incoming.astype(jnp.float32)
+            current = kept + incoming
     return kept, incoming
 
 
@@ -309,9 +321,14 @@
     ).astype(jnp.int32).reshape(1)
 
     unit = points // 8
-    bounds = [(0, unit), (unit, 5 * unit), (6 * unit, 2 * unit)]
-    pieces = split_rows(local, bounds[:1], True)
-    pieces += split_rows(local, bounds[1:], False)
+    width = local.shape[1]
+    early = width * 3 // 4
+    bounds = [
+        (unit, 5 * unit, 0, width),
+        (6 * unit, 2 * unit, 0, early),
+        (6 * unit, 2 * unit, early, width - early),
+    ]
+    pieces = [lax.slice_in_dim(local, 0, unit), *split(local, bounds)]
     far = []
     for piece in pieces:
         far.append(lax.ppermute(piece, "row", far_pairs))
@@ -324,11 +341,12 @@
     total = own_product(self_tiles[0, 0], local, 0, 2)
     total = own_product(self_tiles[0, 0], local, 1, 2, total)
     side = side_tiles[0, 0]
-    flipped, near_last = prepare_last(side, near, *bounds[2])
+    flipped, near_last = prepare_last(side, near, 6 * unit, 2 * unit)
     extra = (column_cluster_basis[0, 0].T, kept, incoming)
-    total = add_rows(total, side, far[:2], near, which, bounds[0][0], extra)
-    total = add_last(total, flipped, far[2], near_last, which)
-    return total[None, None]
+    total = add_rows(total, side, far[:2], near, which, 0, extra)
+    out = add_last(total, flipped, far[2], near_last, which, 0)
+    out = add_last(total, flipped, far[3], near_last, which, early, out)
+    return out[None, None]
 
 
 def solution(mesh):

time: 73.2 us -> 79.6 us (1.087)
  starting transfers between devices: 12.6 us -> 16.3 us
  local copies, waits for them, and re-layouts: 0.64 us -> 3.53 us
  other arithmetic: 1.69 us -> 3.82 us
  waiting for transfers between devices: 26.3 us -> 24.5 us
    ppermute x3 -> x4, waiting for transfers between devices: 13.5 us -> 0.01 us  [on_device(): far.append(lax.ppermute(piece, 'row', far_pairs))]
    ppermute x3, waiting for transfers between devices: 12.9 us -> 22 us  [dual_of(): lax.ppermute(outgoing, 'row', [(i, i ^ 1 << bit) for i in range(rows)])]
    ppermute x3, starting transfers between devices: 2.5 us -> 5.59 us  [dual_of(): lax.ppermute(outgoing, 'row', [(i, i ^ 1 << bit) for i in range(rows)])]
    ppermute x3, waiting for transfers between devices: 0.01 us -> 2.44 us  [dual_of(): lax.ppermute(outgoing, 'col', [(i, (i + shift) % cols) for i in range(col...]
    unnamed x14 -> x12, local copies, waits for them, and re-layouts: 0.1 us -> 1.61 us
    ppermute x1, starting transfers between devices: 0.07 us -> 1.51 us  [on_device(): near = lax.ppermute(local, 'row', near_pairs)]
    mul x1, other arithmetic: 0.05 us -> 1.13 us  [coupling_blocks(): masked = couplings * keep[:, :, None] * keep[:, None, :]]
    dot_general x3 -> x4, matrix products: 2.53 us -> 1.89 us  [contract(): lax.dot_general(tile, values, (((0,), (0,)), ((), ())), preferred_element...]
  transfers between devices with their start and end apart: 10 -> 11, of which waited for: 2 -> 2; matrix products, arithmetic and copies ran while one was open for 7% -> 4% of each run, Pallas kernels for 34% -> 33%
where the time goes in v3:
time: 79.6 us; the launch traced here: 79.2 us
  Pallas kernels  27.6 us (35%)
  waiting for transfers between devices  24.5 us (31%)
  starting transfers between devices  16.3 us (20%)
  other arithmetic  3.82 us (5%)
  local copies, waits for them, and re-layouts  3.53 us (4%)
  matrix products  1.89 us (2%)
  between operations  1.62 us (2%)
    ppermute x3, waiting for transfers between devices, dual_of(): lax.ppermute(outgoing, 'row', [(i, i ^ 1 << bit) for i in range(rows)])  22 us
    pallas_call x2, Pallas kernels, own_product(): pl.pallas_call(kernel, grid=(steps,), in_specs=in_specs, out_specs=pl.Blo...  10.2 us
    pallas_call x1, Pallas kernels, add_rows(): pl.pallas_call(kernel, grid=(points // block,), in_specs=in_specs, out_sp...  8.16 us
    ppermute x3, starting transfers between devices, dual_of(): lax.ppermute(outgoing, 'row', [(i, i ^ 1 << bit) for i in range(rows)])  5.59 us
    ppermute x3, starting transfers between devices, dual_of(): lax.ppermute(outgoing, 'col', [(i, (i + shift) % cols) for i in range(col...  5.54 us
    ppermute x4, starting transfers between devices, on_device(): far.append(lax.ppermute(piece, 'row', far_pairs))  3.66 us
    pallas_call x2, Pallas kernels, add_last(): pl.pallas_call(kernel, in_specs=in_specs, out_specs=pl.BlockSpec(memory_s...  3.65 us
    pallas_call x1, Pallas kernels, prepare_last(): pl.pallas_call(kernel, grid=(points // block,), in_specs=[pl.BlockSpec((s...  2.93 us
  transfers between devices with their start and end apart: 11, of which 2 were waited for; matrix products, arithmetic and copies ran while one was open for 4% of the time, Pallas kernels for 33%

profile of v3, /device:TPU:1, one launch (start us, length us, event | category | flops | bytes accessed | tf_op | source)
XLA Modules:
  0.0 79.2 jit_solution(1364173569387189783)
XLA Ops:
  0.7 0.7 fusion.33
  1.4 1.1 %bitcast_multiply_fusion = bf16[64,1024]{0,1:T(8,128)(2,1)S(1)} fusion(bf16[1,1,64,32,32]{2,4,3,1,0:T(8,128)(2,1)} %param.15, bf16[64,32]{0,1:T(8,128)(2,1)S(1)} %fusion.33), kind=kLoop, calls=%fused_computation.15 | loop fusion | flops 131072 | bytes 266240 | tf_op jit(solution)/shard_map/mul | solution.py:254
  2.5 0.9 %reduce-precision_convert_fusion = (bf16[32,1024]{1,0:T(8,128)(2,1)S(1)}, bf16[32,1024]{1,0:T(8,128)(2,1)S(1)}) fusion(bf16[64,1024]{0,1:T(8,128)(2,1)S(1)} %bitcast_multiply_fusion, s32[64]{0:T(128)} %bitcast.79), kind=kOutput, calls=%fused_computation.20 | convolution fusion | flops 4329472 | bytes 262400 | tf_op jit(solution)/shard_map/dot_general | solution.py:13
  3.8 0.2 stack.10
  4.3 0.4 reshape.111
  4.8 0.5 convolution_convert_fusion
  5.3 2.2 %collective-permute-start.3 = (bf16[32,1024]{1,0:T(8,128)(2,1)S(1)}, bf16[32,1024]{1,0:T(8,128)(2,1)S(1)}, u32[]{:S(2)}, u32[]{:S(2)}) collective-permute-start(bf16[32,1024]{1,0:T(8,128)(2,1)S(1)} %get-tuple-element.16), channel_id=1, source_target_pairs={{0,1},{1,2},{2,3},{3,0},{4,5},{5,6},{6,7},{7,4},{8,9},{9,10},{10,1... | collective-permute-start | bytes 196616 | tf_op jit(solution)/shard_map/ppermute | solution.py:274
  7.5 2.3 %collective-permute-start.4 = (bf16[32,1024]{1,0:T(8,128)(2,1)S(1)}, bf16[32,1024]{1,0:T(8,128)(2,1)S(1)}, u32[]{:S(2)}, u32[]{:S(2)}) collective-permute-start(bf16[32,1024]{1,0:T(8,128)(2,1)S(1)} %get-tuple-element.17), channel_id=1, source_target_pairs={{0,2},{1,3},{2,0},{3,1},{4,6},{5,7},{6,4},{7,5},{8,10},{9,11},{10,... | collective-permute-start | bytes 196616 | tf_op jit(solution)/shard_map/ppermute | solution.py:274
  9.8 1.1 %collective-permute-start.5 = (bf16[32,1024]{1,0:T(8,128)(2,1)S(1)}, bf16[32,1024]{1,0:T(8,128)(2,1)S(1)}, u32[]{:S(2)}, u32[]{:S(2)}) collective-permute-start(bf16[32,1024]{1,0:T(8,128)(2,1)S(1)} %get-tuple-element.18), channel_id=1, source_target_pairs={{0,3},{1,0},{2,1},{3,2},{4,7},{5,4},{6,5},{7,6},{8,11},{9,8},{10,9... | collective-permute-start | bytes 196616 | tf_op jit(solution)/shard_map/ppermute | solution.py:274
  10.9 1.5 %collective-permute-start = (bf16[2048,512]{1,0:T(8,128)(2,1)S(1)}, bf16[2048,512]{1,0:T(8,128)(2,1)}, u32[]{:S(2)}, u32[]{:S(2)}) collective-permute-start(bf16[2048,512]{1,0:T(8,128)(2,1)S(1)} %bitcast.69), channel_id=1, source_target_pairs={{0,4},{4,0},{8,12},{12,8},{16,20},{20,16},{24,28},{28,24},{1,5},{5... | collective-permute-start | bytes 6291464 | tf_op jit(solution)/shard_map/ppermute | solution.py:335
  12.4 2.4 %collective-permute-done.4 = bf16[32,1024]{1,0:T(8,128)(2,1)S(1)} collective-permute-done((bf16[32,1024]{1,0:T(8,128)(2,1)S(1)}, bf16[32,1024]{1,0:T(8,128)(2,1)S(1)}, u32[]{:S(2)}, u32[]{:S(2)}) %collective-permute-start.4) | collective-permute-done | bytes 65568 | tf_op jit(solution)/shard_map/ppermute | solution.py:274
  14.9 0.2 fusion.2
  15.1 0.3 convolution_add_fusion
  15.4 0.8 select_bitcast_fusion
  16.1 0.9 %collective-permute-start.6 = (f32[2,2,32,512]{3,2,1,0:T(8,128)}, f32[2,2,32,512]{3,2,1,0:T(8,128)}, u32[]{:S(2)}, u32[]{:S(2)}) collective-permute-start(f32[2,2,32,512]{3,2,1,0:T(8,128)} %select_bitcast_fusion), channel_id=1, source_target_pairs={{0,4},{4,0},{8,12},{12,8},{16,20},{20,16},{24,28},{28,24},{1,5},{5... | collective-permute-start | bytes 786440 | tf_op jit(solution)/shard_map/ppermute | solution.py:294
  17.1 0.7 slice_bitcast_fusion.2
  17.8 1.1 %collective-permute-start.1 = (bf16[256,512]{1,0:T(8,128)(2,1)}, bf16[256,512]{1,0:T(8,128)(2,1)S(1)}, u32[]{:S(2)}, u32[]{:S(2)}) collective-permute-start(bf16[256,512]{1,0:T(8,128)(2,1)} %slice_bitcast_fusion.2), channel_id=1, source_target_pairs={{0,28},{4,8},{8,4},{12,16},{16,12},{20,24},{24,20},{28,0},{1,29},{... | collective-permute-start | bytes 786440 | tf_op jit(solution)/shard_map/ppermute | solution.py:334
  18.9 2.6 %shard_map.102 = (bf16[1280,512]{1,0:T(8,128)(2,1)}, bf16[512,384]{1,0:T(8,128)(2,1)}, bf16[512,128]{1,0:T(8,128)(2,1)}) custom-call(bf16[2048,512]{1,0:T(8,128)(2,1)} %bitcast.68), custom_call_target="tpu_custom_call" | custom-call | tf_op jit(solution)/shard_map/pallas_call | solution.py:56
  21.5 0.7 collective-permute-start.10
  22.2 1.1 %collective-permute-start.2 = (bf16[1280,512]{1,0:T(8,128)(2,1)}, bf16[1280,512]{1,0:T(8,128)(2,1)}, u32[]{:S(2)}, u32[]{:S(2)}) collective-permute-start(bf16[1280,512]{1,0:T(8,128)(2,1)} %get-tuple-element.10), channel_id=1, source_target_pairs={{0,28},{4,8},{8,4},{12,16},{16,12},{20,24},{24,20},{28,0},{1,29},{... | collective-permute-start | bytes 3932168 | tf_op jit(solution)/shard_map/ppermute | solution.py:334
  24.0 1.6 %copy-done.2 = bf16[1,1,2048,512]{3,2,1,0:T(8,128)(2,1)S(1)} copy-done((bf16[1,1,2048,512]{3,2,1,0:T(8,128)(2,1)S(1)}, bf16[1,1,2048,512]{3,2,1,0:T(8,128)(2,1)}, u32[]{:S(2)}) %copy-start.2) | copy-done | bytes 2097176
  25.6 5.1 %shard_map.100.rest_0_ = f32[2048,512]{1,0:T(8,128)} custom-call(bf16[2048,2048]{1,0:T(8,128)(2,1)} %bitcast.73, bf16[2048,512]{1,0:T(8,128)(2,1)S(1)} %bitcast.70), custom_call_target="tpu_custom_call" | custom-call | flops 2147483648 | bytes 8388608 | tf_op jit(solution)/shard_map/pallas_call | solution.py:83
  30.7 1.0 %bitcast_add_fusion = f32[2,2,32,512]{3,2,1,0:T(8,128)S(1)} fusion(f32[2,2,32,512]{3,2,1,0:T(8,128)} %collective-permute-done.6, f32[2,2,2,32,512]{4,3,2,1,0:T(8,128)S(1)} %bitcast.78, pred[]{:T(512)S(6)} %eq.41), kind=kLoop, calls=%fused_computation.14 | loop fusion | flops 131072 | bytes 1048577 | tf_op jit(solution)/shard_map/add | solution.py:296
  31.8 1.3 %collective-permute-start.7 = (f32[2,32,512]{2,1,0:T(8,128)S(1)}, f32[2,32,512]{2,1,0:T(8,128)S(1)}, u32[]{:S(2)}, u32[]{:S(2)}) collective-permute-start(f32[2,32,512]{2,1,0:T(8,128)S(1)} %select_bitcast_fusion.1), channel_id=1, source_target_pairs={{0,16},{4,20},{8,24},{12,28},{16,0},{20,4},{24,8},{28,12},{1,17},{... | collective-permute-start | bytes 393224 | tf_op jit(solution)/shard_map/ppermute | solution.py:294
  33.1 5.1 %shard_map.101.total_ref = f32[2048,512]{1,0:T(8,128)} custom-call(bf16[2048,2048]{1,0:T(8,128)(2,1)} %bitcast.74, bf16[2048,512]{1,0:T(8,128)(2,1)S(1)} %bitcast.71, f32[2048,512]{1,0:T(8,128)} %shard_map.100.rest_0_), custom_call_target="tpu_custom_call", output_to_operand_aliasing={{}: (2, {})} | custom-call | flops 2147483648 | bytes 8388608 | tf_op jit(solution)/shard_map/pallas_call | solution.py:83
  38.2 3.4 %collective-permute-start.8 = (bf16[32,512]{1,0:T(8,128)(2,1)S(1)}, bf16[32,512]{1,0:T(8,128)(2,1)S(1)}, u32[]{:S(2)}, u32[]{:S(2)}) collective-permute-start(bf16[32,512]{1,0:T(8,128)(2,1)S(1)} %fusion.27), channel_id=1, source_target_pairs={{0,8},{4,12},{8,0},{12,4},{16,24},{20,28},{24,16},{28,20},{1,9},{5... | collective-permute-start | bytes 98312 | tf_op jit(solution)/shard_map/ppermute | solution.py:294
  41.6 0.8 collective-permute-start.9
  42.4 22.0 %collective-permute-done.8.rest_4_ = bf16[32,512]{1,0:T(8,128)(2,1)S(1)} collective-permute-done((bf16[32,512]{1,0:T(8,128)(2,1)S(1)}, bf16[32,512]{1,0:T(8,128)(2,1)S(1)}, u32[]{:S(2)}, u32[]{:S(2)}) %collective-permute-start.8) | collective-permute-done | bytes 32800 | tf_op jit(solution)/shard_map/ppermute | solution.py:294
  64.4 8.2 %shard_map.103.total_ref = f32[2048,512]{1,0:T(8,128)S(1)} custom-call(s32[1]{0:T(128)} %bitcast.1.which_ref, f32[2048,512]{1,0:T(8,128)} %shard_map.101.total_ref, bf16[2048,2048]{1,0:T(8,128)(2,1)} %bitcast.75, bf16[2048,512]{1,0:T(8,128)(2,1)} %collective-permute-done.near_ref, bf16[256,512]{1,0:T(8,128)(2,1)} %copy-done.4, ...), custom_call_target="tpu_custom_call" | custom-call | flops 3221225472 | bytes 14680064 | tf_op jit(solution)/shard_map/pallas_call | solution.py:176
  72.6 2.9 %shard_map.104 = (bf16[2048,512]{1,0:T(8,128)(2,1)S(1)}, bf16[512,512]{1,0:T(8,128)(2,1)S(1)}) custom-call(bf16[2048,2048]{1,0:T(8,128)(2,1)} %bitcast.76, bf16[2048,512]{1,0:T(8,128)(2,1)} %collective-permute-done.near_ref), custom_call_target="tpu_custom_call" | custom-call | tf_op jit(solution)/shard_map/pallas_call | solution.py:132
  75.5 2.2 %shard_map.105.rest_0_ = f32[2048,512]{1,0:T(8,128)} custom-call(s32[1]{0:T(128)} %bitcast.1.which_ref, f32[2048,512]{1,0:T(8,128)S(1)} %shard_map.103.total_ref, bf16[2048,512]{1,0:T(8,128)(2,1)S(1)} %get-tuple-element.11.flipped_ref, bf16[512,384]{1,0:T(8,128)(2,1)S(1)} %collective-permute-done.10.far_ref, bf16[512,512]{1,0:T(8,128)(2,1)S(1)} %get-tuple-element.13.near_ref), custom_call_target="tpu_custom_call" | custom-call | flops 805306368 | bytes 8388608 | tf_op jit(solution)/shard_map/pallas_call | solution.py:228
  77.7 1.5 %shard_map.106 = f32[2048,512]{1,0:T(8,128)} custom-call(s32[1]{0:T(128)} %bitcast.1.which_ref, f32[2048,512]{1,0:T(8,128)S(1)} %shard_map.103.total_ref, bf16[2048,512]{1,0:T(8,128)(2,1)S(1)} %get-tuple-element.11.flipped_ref, bf16[512,128]{1,0:T(8,128)(2,1)S(1)} %collective-permute-done.9.far_ref, ...), custom_call_target="tpu_custom_call", output_to_operand_aliasing={{}: (5, {})} | custom-call | flops 268435456 | bytes 4194304 | tf_op jit(solution)/shard_map/pallas_call | solution.py:228
  (32 shorter events, 0.9 us)
Async XLA Ops:
  0.0 4.8 %copy-start = (bf16[1,1,2048,32]{2,3,1,0:T(8,128)(2,1)S(1)}, bf16[1,1,2048,32]{2,3,1,0:T(8,128)(2,1)}, u32[]{:S(2)}) copy-start(bf16[1,1,2048,32]{2,3,1,0:T(8,128)(2,1)} %param.13) | copy-start | bytes 393220
  1.4 3.5 %copy-start.1 = (bf16[1,1,2048,512]{3,2,1,0:T(8,128)(2,1)S(1)}, bf16[1,1,2048,512]{3,2,1,0:T(8,128)(2,1)}, u32[]{:S(2)}) copy-start(bf16[1,1,2048,512]{3,2,1,0:T(8,128)(2,1)} %param.10) | copy-start | bytes 6291460
  5.3 7.1 %collective-permute-start.3 = (bf16[32,1024]{1,0:T(8,128)(2,1)S(1)}, bf16[32,1024]{1,0:T(8,128)(2,1)S(1)}, u32[]{:S(2)}, u32[]{:S(2)}) collective-permute-start(bf16[32,1024]{1,0:T(8,128)(2,1)S(1)} %get-tuple-element.16), channel_id=1, source_target_pairs={{0,1},{1,2},{2,3},{3,0},{4,5},{5,6},{6,7},{7,4},{8,9},{9,10},{10,1... | collective-permute-start | bytes 196616 | tf_op jit(solution)/shard_map/ppermute | solution.py:274
  7.5 7.3 %collective-permute-start.4 = (bf16[32,1024]{1,0:T(8,128)(2,1)S(1)}, bf16[32,1024]{1,0:T(8,128)(2,1)S(1)}, u32[]{:S(2)}, u32[]{:S(2)}) collective-permute-start(bf16[32,1024]{1,0:T(8,128)(2,1)S(1)} %get-tuple-element.17), channel_id=1, source_target_pairs={{0,2},{1,3},{2,0},{3,1},{4,6},{5,7},{6,4},{7,5},{8,10},{9,11},{10,... | collective-permute-start | bytes 196616 | tf_op jit(solution)/shard_map/ppermute | solution.py:274
  9.8 5.0 %collective-permute-start.5 = (bf16[32,1024]{1,0:T(8,128)(2,1)S(1)}, bf16[32,1024]{1,0:T(8,128)(2,1)S(1)}, u32[]{:S(2)}, u32[]{:S(2)}) collective-permute-start(bf16[32,1024]{1,0:T(8,128)(2,1)S(1)} %get-tuple-element.18), channel_id=1, source_target_pairs={{0,3},{1,0},{2,1},{3,2},{4,7},{5,4},{6,5},{7,6},{8,11},{9,8},{10,9... | collective-permute-start | bytes 196616 | tf_op jit(solution)/shard_map/ppermute | solution.py:274
  10.9 53.5 %collective-permute-start = (bf16[2048,512]{1,0:T(8,128)(2,1)S(1)}, bf16[2048,512]{1,0:T(8,128)(2,1)}, u32[]{:S(2)}, u32[]{:S(2)}) collective-permute-start(bf16[2048,512]{1,0:T(8,128)(2,1)S(1)} %bitcast.69), channel_id=1, source_target_pairs={{0,4},{4,0},{8,12},{12,8},{16,20},{20,16},{24,28},{28,24},{1,5},{5... | collective-permute-start | bytes 6291464 | tf_op jit(solution)/shard_map/ppermute | solution.py:335
  16.1 14.5 %collective-permute-start.6 = (f32[2,2,32,512]{3,2,1,0:T(8,128)}, f32[2,2,32,512]{3,2,1,0:T(8,128)}, u32[]{:S(2)}, u32[]{:S(2)}) collective-permute-start(f32[2,2,32,512]{3,2,1,0:T(8,128)} %select_bitcast_fusion), channel_id=1, source_target_pairs={{0,4},{4,0},{8,12},{12,8},{16,20},{20,16},{24,28},{28,24},{1,5},{5... | collective-permute-start | bytes 786440 | tf_op jit(solution)/shard_map/ppermute | solution.py:294
  17.8 23.8 %collective-permute-start.1 = (bf16[256,512]{1,0:T(8,128)(2,1)}, bf16[256,512]{1,0:T(8,128)(2,1)S(1)}, u32[]{:S(2)}, u32[]{:S(2)}) collective-permute-start(bf16[256,512]{1,0:T(8,128)(2,1)} %slice_bitcast_fusion.2), channel_id=1, source_target_pairs={{0,28},{4,8},{8,4},{12,16},{16,12},{20,24},{24,20},{28,0},{1,29},{... | collective-permute-start | bytes 786440 | tf_op jit(solution)/shard_map/ppermute | solution.py:334
  21.5 54.0 %collective-permute-start.10 = (bf16[512,384]{1,0:T(8,128)(2,1)}, bf16[512,384]{1,0:T(8,128)(2,1)S(1)}, u32[]{:S(2)}, u32[]{:S(2)}) collective-permute-start(bf16[512,384]{1,0:T(8,128)(2,1)} %get-tuple-element.14), channel_id=1, source_target_pairs={{0,28},{4,8},{8,4},{12,16},{16,12},{20,24},{24,20},{28,0},{1,29},{... | collective-permute-start | bytes 1179656 | tf_op jit(solution)/shard_map/ppermute | solution.py:334
  22.2 42.2 %collective-permute-start.2 = (bf16[1280,512]{1,0:T(8,128)(2,1)}, bf16[1280,512]{1,0:T(8,128)(2,1)}, u32[]{:S(2)}, u32[]{:S(2)}) collective-permute-start(bf16[1280,512]{1,0:T(8,128)(2,1)} %get-tuple-element.10), channel_id=1, source_target_pairs={{0,28},{4,8},{8,4},{12,16},{16,12},{20,24},{24,20},{28,0},{1,29},{... | collective-permute-start | bytes 3932168 | tf_op jit(solution)/shard_map/ppermute | solution.py:334
  24.0 1.6 %copy-start.2 = (bf16[1,1,2048,512]{3,2,1,0:T(8,128)(2,1)S(1)}, bf16[1,1,2048,512]{3,2,1,0:T(8,128)(2,1)}, u32[]{:S(2)}) copy-start(bf16[1,1,2048,512]{3,2,1,0:T(8,128)(2,1)} %param.10) | copy-start | bytes 6291460
  31.7 9.9 %copy-start.5 = (bf16[512,128]{1,0:T(8,128)(2,1)S(1)}, bf16[512,128]{1,0:T(8,128)(2,1)}, u32[]{:S(2)}) copy-start(bf16[512,128]{1,0:T(8,128)(2,1)} %get-tuple-element.12) | copy-start | bytes 393220
  31.7 32.7 %copy-start.3 = (bf16[1,1,2048,32]{2,3,1,0:T(8,128)(2,1)S(1)}, bf16[1,1,2048,32]{2,3,1,0:T(8,128)(2,1)}, u32[]{:S(2)}) copy-start(bf16[1,1,2048,32]{2,3,1,0:T(8,128)(2,1)} %param.14) | copy-start | bytes 393220
  31.8 6.4 %collective-permute-start.7 = (f32[2,32,512]{2,1,0:T(8,128)S(1)}, f32[2,32,512]{2,1,0:T(8,128)S(1)}, u32[]{:S(2)}, u32[]{:S(2)}) collective-permute-start(f32[2,32,512]{2,1,0:T(8,128)S(1)} %select_bitcast_fusion.1), channel_id=1, source_target_pairs={{0,16},{4,20},{8,24},{12,28},{16,0},{20,4},{24,8},{28,12},{1,17},{... | collective-permute-start | bytes 393224 | tf_op jit(solution)/shard_map/ppermute | solution.py:294
  38.2 26.2 %collective-permute-start.8 = (bf16[32,512]{1,0:T(8,128)(2,1)S(1)}, bf16[32,512]{1,0:T(8,128)(2,1)S(1)}, u32[]{:S(2)}, u32[]{:S(2)}) collective-permute-start(bf16[32,512]{1,0:T(8,128)(2,1)S(1)} %fusion.27), channel_id=1, source_target_pairs={{0,8},{4,12},{8,0},{12,4},{16,24},{20,28},{24,16},{28,20},{1,9},{5... | collective-permute-start | bytes 98312 | tf_op jit(solution)/shard_map/ppermute | solution.py:294
  41.6 22.8 %copy-start.4 = (bf16[256,512]{1,0:T(8,128)(2,1)}, bf16[256,512]{1,0:T(8,128)(2,1)S(1)}, u32[]{:S(2)}) copy-start(bf16[256,512]{1,0:T(8,128)(2,1)S(1)} %collective-permute-done.1.rest_0_) | copy-start | bytes 786436
  41.6 36.1 %collective-permute-start.9 = (bf16[512,128]{1,0:T(8,128)(2,1)S(1)}, bf16[512,128]{1,0:T(8,128)(2,1)S(1)}, u32[]{:S(2)}, u32[]{:S(2)}) collective-permute-start(bf16[512,128]{1,0:T(8,128)(2,1)S(1)} %copy-done.5), channel_id=1, source_target_pairs={{0,28},{4,8},{8,4},{12,16},{16,12},{20,24},{24,20},{28,0},{1,29},{... | collective-permute-start | bytes 393224 | tf_op jit(solution)/shard_map/ppermute | solution.py:334

commit v4 on v3

--- a/solution.py
+++ b/solution.py
@@ -100,13 +100,10 @@
     return pl.ds(pl.multiple_of(pl.program_id(0) * block, block), block)
 
 
-def choose(which_ref, far_refs, near_ref, values_ref):
+def choose(which_ref, fetch, near_ref, values_ref):
     @pl.when(which_ref[0] == 2)
     def _():
-        row = 0
-        for far_ref in far_refs:
-            values_ref[row : row + far_ref.shape[0], :] = far_ref[...]
-            row += far_ref.shape[0]
+        fetch()
 
     @pl.when(which_ref[0] == 1)
     def _():
@@ -117,83 +114,96 @@
         values_ref[...] = jnp.zeros_like(values_ref)
 
 
-def prepare_last(tile, near, start, size):
-    points, columns = tile.shape[1], near.shape[1]
+def stage(tile, near, total, start):
+    rows, points = tile.shape
+    size = rows - start
     block = min(BLOCK, points)
-    at = start // size
-
-    def kernel(tile_ref, near_ref, flipped_ref, kept_ref):
-        flipped_ref[step_rows(block), :] = tile_ref[...].T
+
+    def kernel(tile_ref, near_ref, total_ref, first_ref, flipped_ref, near_out, total_out, *scratch):
+        last_ref, sems = scratch
+        copies = [
+            pltpu.make_async_copy(tile_ref.at[pl.ds(start, size)], last_ref, sems.at[0]),
+            pltpu.make_async_copy(tile_ref.at[pl.ds(0, start)], first_ref, sems.at[1]),
+            pltpu.make_async_copy(total_ref, total_out, sems.at[2]),
+            pltpu.make_async_copy(near_ref, near_out, sems.at[3]),
+        ]
+        for copy in copies:
+            copy.start()
+        copies[0].wait()
+        for at in range(0, points, block):
+            flipped_ref[at : at + block, :] = last_ref[:, at : at + block].T
+        for copy in copies[1:]:
+            copy.wait()
+
+    return pl.pallas_call(
+        kernel,
+        in_specs=[pl.BlockSpec(memory_space=pltpu.HBM) for _ in range(3)],
+        out_specs=[whole() for _ in range(4)],
+        out_shape=[
+            pltpu.VMEM((start, points), tile.dtype),
+            pltpu.VMEM((points, size), tile.dtype),
+            pltpu.VMEM(near.shape, near.dtype),
+            pltpu.VMEM(total.shape, total.dtype),
+        ],
+        compiler_params=grant(),
+        scratch_shapes=[
+            pltpu.VMEM((size, points), tile.dtype),
+            pltpu.SemaphoreType.DMA((4,)),
+        ],
+    )(in_hbm(tile), in_hbm(near), in_hbm(total))
+
+
+def add_rows(total, tile, far, near, which, extra):
+    points, columns = total.shape
+    size = tile.shape[0]
+    block = min(BLOCK, points)
+    count = len(far)
+
+    def kernel(which_ref, total_ref, tile_ref, near_ref, *rest):
+        out_ref, values_ref, sems = rest[-3:]
+        basis_ref, kept_ref, incoming_ref = rest[count:-3]
+        here = step_rows(block)
+
+        def fetch():
+            row, copies = 0, []
+            for c, far_ref in enumerate(rest[:count]):
+                rows = pl.ds(row, far_ref.shape[0])
+                copies.append(pltpu.make_async_copy(far_ref, values_ref.at[rows], sems.at[c]))
+                copies[-1].start()
+                row += far_ref.shape[0]
+            for copy in copies:
+                copy.wait()
 
         @pl.when(pl.program_id(0) == 0)
         def _():
-            kept_ref[...] = near_ref[...]
-
-    return pl.pallas_call(
-        kernel,
-        grid=(points // block,),
-        in_specs=[
-            pl.BlockSpec((size, block), lambda i: (at, i)),
-            pl.BlockSpec((size, columns), lambda i: (at, 0)),
-        ],
-        out_specs=[whole(), whole()],
-        out_shape=[
-            pltpu.VMEM((points, size), tile.dtype),
-            pltpu.VMEM((size, columns), near.dtype),
-        ],
-        compiler_params=grant(),
-    )(in_hbm(tile), in_hbm(near))
-
-
-def add_rows(total, tile, far, near, which, start, extra):
-    points, columns = total.shape
-    size = sum(piece.shape[0] for piece in far)
-    block = min(BLOCK, points)
-    at = start // size
-    count = len(far)
-
-    def kernel(which_ref, total_ref, tile_ref, near_ref, *rest):
-        out_ref, values_ref = rest[-2:]
-        basis_ref, kept_ref, incoming_ref = rest[count:-2]
-        here = step_rows(block)
-
-        @pl.when(pl.program_id(0) == 0)
-        def _():
-            choose(which_ref, rest[:count], near_ref, values_ref)
+            choose(which_ref, fetch, near_ref.at[:size], values_ref)
 
         dual = (kept_ref[...] + incoming_ref[...].astype(jnp.float32)).astype(jnp.bfloat16)
-        result = total_ref[...] + contract(tile_ref[...], values_ref[...])
+        result = total_ref[here, :] + contract(tile_ref[:, here], values_ref[...])
         out_ref[here, :] = result + contract(basis_ref[:, here], dual)
 
-    in_specs = [
-        pl.BlockSpec(memory_space=pltpu.SMEM),
-        pl.BlockSpec((block, columns), lambda i: (i, 0)),
-        pl.BlockSpec((size, block), lambda i: (at, i)),
-        pl.BlockSpec((size, columns), lambda i: (at, 0)),
-    ]
-    in_specs += [pl.BlockSpec(piece.shape, lambda i: (0, 0)) for piece in far]
-    in_specs += [whole() for _ in extra]
+    arguments = [which] + [in_vmem(value) for value in (total, tile, near)]
+    arguments += [in_hbm(piece) for piece in far] + [in_vmem(value) for value in extra]
+    in_specs = [pl.BlockSpec(memory_space=pltpu.SMEM)] + [whole() for _ in range(3)]
+    in_specs += [pl.BlockSpec(memory_space=pltpu.HBM) for _ in far] + [whole() for _ in extra]
     return pl.pallas_call(
         kernel,
         grid=(points // block,),
         in_specs=in_specs,
         out_specs=whole(),
         out_shape=pltpu.VMEM((points, columns), jnp.float32),
-        compiler_params=grant(),
-        scratch_shapes=[pltpu.VMEM((size, columns), jnp.bfloat16)],
+        input_output_aliases={1: 0},
+        compiler_params=grant(),
+        scratch_shapes=[
+            pltpu.VMEM((size, columns), jnp.bfloat16),
+            pltpu.SemaphoreType.DMA((count,)),
+        ],
         cost_estimate=pl.CostEstimate(
             flops=2 * size * points * columns,
-            bytes_accessed=2 * size * points + 8 * total.size,
+            bytes_accessed=2 * size * columns,
             transcendentals=0,
         ),
-    )(
-        which,
-        in_hbm(total),
-        in_hbm(tile),
-        in_hbm(near),
-        *[in_hbm(piece) for piece in far],
-        *[in_vmem(value) for value in extra],
-    )
+    )(*arguments)
 
 
 def add_last(total, flipped, far, near, which, column, out=None):
@@ -205,7 +215,11 @@
 
     def kernel(which_ref, total_ref, flipped_ref, far_ref, near_ref, *rest):
         out_ref, values_ref, staged_ref, sems = rest[-4:]
-        choose(which_ref, [far_ref], near_ref.at[:, here], values_ref)
+
+        def fetch():
+            values_ref[...] = far_ref[...]
+
+        choose(which_ref, fetch, near_ref.at[points - size :, here], values_ref)
         copies = []
         for step in range(steps):
             rows = pl.ds(step * block, block)
@@ -341,11 +355,11 @@
     total = own_product(self_tiles[0, 0], local, 0, 2)
     total = own_product(self_tiles[0, 0], local, 1, 2, total)
     side = side_tiles[0, 0]
-    flipped, near_last = prepare_last(side, near, 6 * unit, 2 * unit)
+    first, flipped, near, total = stage(side, near, total, 6 * unit)
     extra = (column_cluster_basis[0, 0].T, kept, incoming)
-    total = add_rows(total, side, far[:2], near, which, 0, extra)
-    out = add_last(total, flipped, far[2], near_last, which, 0)
-    out = add_last(total, flipped, far[3], near_last, which, early, out)
+    total = add_rows(total, first, far[:2], near, which, extra)
+    out = add_last(total, flipped, far[2], near, which, 0)
+    out = add_last(total, flipped, far[3], near, which, early, out)
     return out[None, None]
 
 

time: 79.6 us -> 73.4 us (0.922)
  waiting for transfers between devices: 24.5 us -> 17 us
  Pallas kernels: 27.6 us -> 29.3 us
  matrix products: 1.89 us -> 3.48 us
  starting transfers between devices: 16.3 us -> 15.2 us
    ppermute x3, waiting for transfers between devices: 22 us -> 10.7 us  [dual_of(): lax.ppermute(outgoing, 'row', [(i, i ^ 1 << bit) for i in range(rows)])]
    ppermute x4, waiting for transfers between devices: 0.01 us -> 6.25 us  [on_device(): far.append(lax.ppermute(piece, 'row', far_pairs))]
    ppermute x3, waiting for transfers between devices: 2.44 us -> 0.01 us  [dual_of(): lax.ppermute(outgoing, 'col', [(i, (i + shift) % cols) for i in range(col...]
    pallas_call x1, Pallas kernels: 2.93 us -> 5.28 us  [stage(): pl.pallas_call(kernel, in_specs=[pl.BlockSpec(memory_space=pltpu.HBM) for...]
    pallas_call x1, Pallas kernels: 8.16 us -> 6.2 us  [add_rows(): pl.pallas_call(kernel, grid=(points // block,), in_specs=in_specs, out_sp...]
    ppermute x3, starting transfers between devices: 5.59 us -> 3.76 us  [dual_of(): lax.ppermute(outgoing, 'row', [(i, i ^ 1 << bit) for i in range(rows)])]
    dot_general x4, matrix products: 1.89 us -> 3.48 us  [contract(): lax.dot_general(tile, values, (((0,), (0,)), ((), ())), preferred_element...]
    unnamed x12 -> x10, local copies, waits for them, and re-layouts: 1.61 us -> 0.02 us
  transfers between devices with their start and end apart: 11 -> 11, of which waited for: 2 -> 3; matrix products, arithmetic and copies ran while one was open for 4% -> 5% of each run, Pallas kernels for 33% -> 38%
where the time goes in v4:
time: 73.4 us; the launch traced here: 73.1 us
  Pallas kernels  29.3 us (40%)
  waiting for transfers between devices  17 us (23%)
  starting transfers between devices  15.2 us (21%)
  other arithmetic  3.63 us (5%)
  matrix products  3.48 us (5%)
  local copies, waits for them, and re-layouts  2.88 us (4%)
  between operations  1.6 us (2%)
    pallas_call x2, Pallas kernels, own_product(): pl.pallas_call(kernel, grid=(steps,), in_specs=in_specs, out_specs=pl.Blo...  11.6 us
    ppermute x3, waiting for transfers between devices, dual_of(): lax.ppermute(outgoing, 'row', [(i, i ^ 1 << bit) for i in range(rows)])  10.7 us
    ppermute x4, waiting for transfers between devices, on_device(): far.append(lax.ppermute(piece, 'row', far_pairs))  6.25 us
    pallas_call x1, Pallas kernels, add_rows(): pl.pallas_call(kernel, grid=(points // block,), in_specs=in_specs, out_sp...  6.2 us
    ppermute x3, starting transfers between devices, dual_of(): lax.ppermute(outgoing, 'col', [(i, (i + shift) % cols) for i in range(col...  5.54 us
    pallas_call x1, Pallas kernels, stage(): pl.pallas_call(kernel, in_specs=[pl.BlockSpec(memory_space=pltpu.HBM) for...  5.28 us
    ppermute x4, starting transfers between devices, on_device(): far.append(lax.ppermute(piece, 'row', far_pairs))  4.33 us
    ppermute x3, starting transfers between devices, dual_of(): lax.ppermute(outgoing, 'row', [(i, i ^ 1 << bit) for i in range(rows)])  3.76 us
  transfers between devices with their start and end apart: 11, of which 3 were waited for; matrix products, arithmetic and copies ran while one was open for 5% of the time, Pallas kernels for 38%

profile of v4, /device:TPU:1, one launch (start us, length us, event | category | flops | bytes accessed | tf_op | source)
XLA Modules:
  0.0 73.1 jit_solution(11094218703794594493)
XLA Ops:
  0.7 0.7 fusion.33
  1.4 1.0 %bitcast_multiply_fusion = bf16[64,1024]{0,1:T(8,128)(2,1)S(1)} fusion(bf16[1,1,64,32,32]{2,4,3,1,0:T(8,128)(2,1)} %param.15, bf16[64,32]{0,1:T(8,128)(2,1)S(1)} %fusion.33), kind=kLoop, calls=%fused_computation.15 | loop fusion | flops 131072 | bytes 266240 | tf_op jit(solution)/shard_map/mul | solution.py:268
  2.4 0.9 %reduce-precision_convert_fusion = (bf16[32,1024]{1,0:T(8,128)(2,1)S(1)}, bf16[32,1024]{1,0:T(8,128)(2,1)S(1)}) fusion(bf16[64,1024]{0,1:T(8,128)(2,1)S(1)} %bitcast_multiply_fusion, s32[64]{0:T(128)} %bitcast.74), kind=kOutput, calls=%fused_computation.20 | convolution fusion | flops 4329472 | bytes 262400 | tf_op jit(solution)/shard_map/dot_general | solution.py:13
  3.3 0.2 stack.9
  3.7 0.2 stack.10
  4.2 0.4 reshape.111
  4.7 2.0 %convolution_convert_fusion = bf16[32,512]{1,0:T(8,128)(2,1)S(1)} fusion(bf16[1,1,2048,32]{2,3,1,0:T(8,128)(2,1)S(1)} %copy-done, bf16[1,1,2048,512]{3,2,1,0:T(8,128)(2,1)} %param.10), kind=kOutput, calls=%fused_computation.1 | convolution fusion | flops 67125248 | bytes 2260992 | tf_op jit(solution)/shard_map/dot_general | solution.py:13
  6.8 2.2 %collective-permute-start.3 = (bf16[32,1024]{1,0:T(8,128)(2,1)S(1)}, bf16[32,1024]{1,0:T(8,128)(2,1)S(1)}, u32[]{:S(2)}, u32[]{:S(2)}) collective-permute-start(bf16[32,1024]{1,0:T(8,128)(2,1)S(1)} %get-tuple-element.20), channel_id=1, source_target_pairs={{0,1},{1,2},{2,3},{3,0},{4,5},{5,6},{6,7},{7,4},{8,9},{9,10},{10,1... | collective-permute-start | bytes 196616 | tf_op jit(solution)/shard_map/ppermute | solution.py:288
  8.9 2.3 %collective-permute-start.4 = (bf16[32,1024]{1,0:T(8,128)(2,1)S(1)}, bf16[32,1024]{1,0:T(8,128)(2,1)S(1)}, u32[]{:S(2)}, u32[]{:S(2)}) collective-permute-start(bf16[32,1024]{1,0:T(8,128)(2,1)S(1)} %get-tuple-element.21), channel_id=1, source_target_pairs={{0,2},{1,3},{2,0},{3,1},{4,6},{5,7},{6,4},{7,5},{8,10},{9,11},{10,... | collective-permute-start | bytes 196616 | tf_op jit(solution)/shard_map/ppermute | solution.py:288
  11.3 1.1 %collective-permute-start.5 = (bf16[32,1024]{1,0:T(8,128)(2,1)S(1)}, bf16[32,1024]{1,0:T(8,128)(2,1)S(1)}, u32[]{:S(2)}, u32[]{:S(2)}) collective-permute-start(bf16[32,1024]{1,0:T(8,128)(2,1)S(1)} %get-tuple-element.22), channel_id=1, source_target_pairs={{0,3},{1,0},{2,1},{3,2},{4,7},{5,4},{6,5},{7,6},{8,11},{9,8},{10,9... | collective-permute-start | bytes 196616 | tf_op jit(solution)/shard_map/ppermute | solution.py:288
  12.3 1.5 %collective-permute-start = (bf16[2048,512]{1,0:T(8,128)(2,1)}, bf16[2048,512]{1,0:T(8,128)(2,1)S(1)}, u32[]{:S(2)}, u32[]{:S(2)}) collective-permute-start(bf16[2048,512]{1,0:T(8,128)(2,1)} %bitcast.3.values_ref), channel_id=1, source_target_pairs={{0,4},{4,0},{8,12},{12,8},{16,20},{20,16},{24,28},{28,24},{1,5},{5... | collective-permute-start | bytes 6291464 | tf_op jit(solution)/shard_map/ppermute | solution.py:349
  13.8 2.6 %shard_map.103 = (bf16[1280,512]{1,0:T(8,128)(2,1)}, bf16[512,384]{1,0:T(8,128)(2,1)}, bf16[512,128]{1,0:T(8,128)(2,1)}) custom-call(bf16[2048,512]{1,0:T(8,128)(2,1)} %bitcast.3.values_ref), custom_call_target="tpu_custom_call" | custom-call | tf_op jit(solution)/shard_map/pallas_call | solution.py:56
  16.4 1.2 %collective-permute-start.2 = (bf16[1280,512]{1,0:T(8,128)(2,1)}, bf16[1280,512]{1,0:T(8,128)(2,1)}, u32[]{:S(2)}, u32[]{:S(2)}) collective-permute-start(bf16[1280,512]{1,0:T(8,128)(2,1)} %get-tuple-element.15), channel_id=1, source_target_pairs={{0,28},{4,8},{8,4},{12,16},{16,12},{20,24},{24,20},{28,0},{1,29},{... | collective-permute-start | bytes 3932168 | tf_op jit(solution)/shard_map/ppermute | solution.py:348
  17.7 0.2 fusion.2
  17.9 0.3 convolution_add_fusion
  18.2 0.7 select_bitcast_fusion
  18.9 1.5 %collective-permute-start.6 = (f32[2,2,32,512]{3,2,1,0:T(8,128)}, f32[2,2,32,512]{3,2,1,0:T(8,128)}, u32[]{:S(2)}, u32[]{:S(2)}) collective-permute-start(f32[2,2,32,512]{3,2,1,0:T(8,128)} %select_bitcast_fusion), channel_id=1, source_target_pairs={{0,4},{4,0},{8,12},{12,8},{16,20},{20,16},{24,28},{28,24},{1,5},{5... | collective-permute-start | bytes 786440 | tf_op jit(solution)/shard_map/ppermute | solution.py:308
  20.4 1.7 %slice_bitcast_fusion.2 = bf16[256,512]{1,0:T(8,128)(2,1)} fusion(bf16[1,1,2048,512]{3,2,1,0:T(8,128)(2,1)} %param.10), kind=kLoop, calls=%fused_computation.18 | loop fusion | bytes 524288 | tf_op jit(solution)/shard_map/slice | solution.py:345
  22.2 1.6 %collective-permute-start.10 = (bf16[512,384]{1,0:T(8,128)(2,1)}, bf16[512,384]{1,0:T(8,128)(2,1)S(1)}, u32[]{:S(2)}, u32[]{:S(2)}) collective-permute-start(bf16[512,384]{1,0:T(8,128)(2,1)} %get-tuple-element.18), channel_id=1, source_target_pairs={{0,28},{4,8},{8,4},{12,16},{16,12},{20,24},{24,20},{28,0},{1,29},{... | collective-permute-start | bytes 1179656 | tf_op jit(solution)/shard_map/ppermute | solution.py:348
  24.4 5.8 %shard_map.100.rest_0_ = f32[2048,512]{1,0:T(8,128)} custom-call(bf16[2048,2048]{1,0:T(8,128)(2,1)} %bitcast.69, bf16[2048,512]{1,0:T(8,128)(2,1)} %bitcast.3.values_ref), custom_call_target="tpu_custom_call" | custom-call | flops 2147483648 | bytes 8388608 | tf_op jit(solution)/shard_map/pallas_call | solution.py:83
  30.2 1.0 %bitcast_add_fusion = f32[2,2,32,512]{3,2,1,0:T(8,128)S(1)} fusion(f32[2,2,32,512]{3,2,1,0:T(8,128)} %collective-permute-done.6, f32[2,2,2,32,512]{4,3,2,1,0:T(8,128)S(1)} %bitcast.73, pred[]{:T(512)S(6)} %eq.41), kind=kLoop, calls=%fused_computation.14 | loop fusion | flops 131072 | bytes 1048577 | tf_op jit(solution)/shard_map/add | solution.py:310
  31.3 0.3 collective-permute-start.7
  31.6 5.8 %shard_map.101.total_ref = f32[2048,512]{1,0:T(8,128)} custom-call(bf16[2048,2048]{1,0:T(8,128)(2,1)} %bitcast.70, bf16[2048,512]{1,0:T(8,128)(2,1)} %bitcast.3.values_ref, f32[2048,512]{1,0:T(8,128)} %shard_map.100.rest_0_), custom_call_target="tpu_custom_call", output_to_operand_aliasing={{}: (2, {})} | custom-call | flops 2147483648 | bytes 8388608 | tf_op jit(solution)/shard_map/pallas_call | solution.py:83
  37.3 1.1 %collective-permute-done.7 = f32[2,32,512]{2,1,0:T(8,128)S(1)} collective-permute-done((f32[2,32,512]{2,1,0:T(8,128)S(1)}, f32[2,32,512]{2,1,0:T(8,128)S(1)}, u32[]{:S(2)}, u32[]{:S(2)}) %collective-permute-start.7) | collective-permute-done | bytes 131104 | tf_op jit(solution)/shard_map/ppermute | solution.py:308
  38.4 2.0 %collective-permute-start.8 = (bf16[32,512]{1,0:T(8,128)(2,1)S(1)}, bf16[32,512]{1,0:T(8,128)(2,1)S(1)}, u32[]{:S(2)}, u32[]{:S(2)}) collective-permute-start(bf16[32,512]{1,0:T(8,128)(2,1)S(1)} %fusion.27), channel_id=1, source_target_pairs={{0,8},{4,12},{8,0},{12,4},{16,24},{20,28},{24,16},{28,20},{1,9},{5... | collective-permute-start | bytes 98312 | tf_op jit(solution)/shard_map/ppermute | solution.py:308
  40.5 1.4 %collective-permute-start.9 = (bf16[512,128]{1,0:T(8,128)(2,1)S(1)}, bf16[512,128]{1,0:T(8,128)(2,1)S(1)}, u32[]{:S(2)}, u32[]{:S(2)}) collective-permute-start(bf16[512,128]{1,0:T(8,128)(2,1)S(1)} %copy-done.4), channel_id=1, source_target_pairs={{0,28},{4,8},{8,4},{12,16},{16,12},{20,24},{24,20},{28,0},{1,29},{... | collective-permute-start | bytes 393224 | tf_op jit(solution)/shard_map/ppermute | solution.py:348
  41.9 5.3 %shard_map.102 = (bf16[1536,2048]{1,0:T(8,128)(2,1)S(1)}, bf16[2048,512]{1,0:T(8,128)(2,1)S(1)}, bf16[2048,512]{1,0:T(8,128)(2,1)S(1)}, f32[2048,512]{1,0:T(8,128)S(1)}) custom-call(bf16[2048,2048]{1,0:T(8,128)(2,1)} %bitcast.71, bf16[2048,512]{1,0:T(8,128)(2,1)} %copy-done.2, f32[2048,512]{1,0:T(8,128)} %shard_map.101.total_ref), custom_call_target="tpu_custom_call" | custom-call | tf_op jit(solution)/shard_map/pallas_call | solution.py:138
  47.2 6.2 %collective-permute-done.1.rest_0_ = bf16[256,512]{1,0:T(8,128)(2,1)S(1)} collective-permute-done((bf16[256,512]{1,0:T(8,128)(2,1)}, bf16[256,512]{1,0:T(8,128)(2,1)S(1)}, u32[]{:S(2)}, u32[]{:S(2)}) %collective-permute-start.1) | collective-permute-done | bytes 262176 | tf_op jit(solution)/shard_map/ppermute | solution.py:348
  53.4 9.7 %collective-permute-done.8.rest_4_ = bf16[32,512]{1,0:T(8,128)(2,1)S(1)} collective-permute-done((bf16[32,512]{1,0:T(8,128)(2,1)S(1)}, bf16[32,512]{1,0:T(8,128)(2,1)S(1)}, u32[]{:S(2)}, u32[]{:S(2)}) %collective-permute-start.8) | collective-permute-done | bytes 32800 | tf_op jit(solution)/shard_map/ppermute | solution.py:308
  63.1 6.2 %shard_map.104.total_ref = f32[2048,512]{1,0:T(8,128)S(1)} custom-call(s32[1]{0:T(128)} %bitcast.1.which_ref, f32[2048,512]{1,0:T(8,128)S(1)} %get-tuple-element.12.total_ref, bf16[1536,2048]{1,0:T(8,128)(2,1)S(1)} %get-tuple-element.13.tile_ref, bf16[2048,512]{1,0:T(8,128)(2,1)S(1)} %get-tuple-element.14.near_ref, ...), custom_call_target="tpu_custom_call", output_to_operand_aliasing={{}: (1, {})} | custom-call | flops 3221225472 | bytes 1572864 | tf_op jit(solution)/shard_map/pallas_call | solution.py:189
  69.3 2.2 %shard_map.105.rest_0_ = f32[2048,512]{1,0:T(8,128)} custom-call(s32[1]{0:T(128)} %bitcast.1.which_ref, f32[2048,512]{1,0:T(8,128)S(1)} %shard_map.104.total_ref, bf16[2048,512]{1,0:T(8,128)(2,1)S(1)} %get-tuple-element.16.flipped_ref, bf16[512,384]{1,0:T(8,128)(2,1)S(1)} %collective-permute-done.10.far_ref, bf16[2048,512]{1,0:T(8,128)(2,1)S(1)} %get-tuple-element.14.near_ref), custom_call_target="tpu_custom_call" | custom-call | flops 805306368 | bytes 8388608 | tf_op jit(solution)/shard_map/pallas_call | solution.py:242
  71.6 1.5 %shard_map.106 = f32[2048,512]{1,0:T(8,128)} custom-call(s32[1]{0:T(128)} %bitcast.1.which_ref, f32[2048,512]{1,0:T(8,128)S(1)} %shard_map.104.total_ref, bf16[2048,512]{1,0:T(8,128)(2,1)S(1)} %get-tuple-element.16.flipped_ref, bf16[512,128]{1,0:T(8,128)(2,1)S(1)} %collective-permute-done.9.far_ref, ...), custom_call_target="tpu_custom_call", output_to_operand_aliasing={{}: (5, {})} | custom-call | flops 268435456 | bytes 4194304 | tf_op jit(solution)/shard_map/pallas_call | solution.py:242
  (30 shorter events, 0.8 us)
Async XLA Ops:
  0.0 4.7 %copy-start = (bf16[1,1,2048,32]{2,3,1,0:T(8,128)(2,1)S(1)}, bf16[1,1,2048,32]{2,3,1,0:T(8,128)(2,1)}, u32[]{:S(2)}) copy-start(bf16[1,1,2048,32]{2,3,1,0:T(8,128)(2,1)} %param.13) | copy-start | bytes 393220
  6.8 10.8 %collective-permute-start.3 = (bf16[32,1024]{1,0:T(8,128)(2,1)S(1)}, bf16[32,1024]{1,0:T(8,128)(2,1)S(1)}, u32[]{:S(2)}, u32[]{:S(2)}) collective-permute-start(bf16[32,1024]{1,0:T(8,128)(2,1)S(1)} %get-tuple-element.20), channel_id=1, source_target_pairs={{0,1},{1,2},{2,3},{3,0},{4,5},{5,6},{6,7},{7,4},{8,9},{9,10},{10,1... | collective-permute-start | bytes 196616 | tf_op jit(solution)/shard_map/ppermute | solution.py:288
  8.9 8.7 %collective-permute-start.4 = (bf16[32,1024]{1,0:T(8,128)(2,1)S(1)}, bf16[32,1024]{1,0:T(8,128)(2,1)S(1)}, u32[]{:S(2)}, u32[]{:S(2)}) collective-permute-start(bf16[32,1024]{1,0:T(8,128)(2,1)S(1)} %get-tuple-element.21), channel_id=1, source_target_pairs={{0,2},{1,3},{2,0},{3,1},{4,6},{5,7},{6,4},{7,5},{8,10},{9,11},{10,... | collective-permute-start | bytes 196616 | tf_op jit(solution)/shard_map/ppermute | solution.py:288
  11.3 6.4 %collective-permute-start.5 = (bf16[32,1024]{1,0:T(8,128)(2,1)S(1)}, bf16[32,1024]{1,0:T(8,128)(2,1)S(1)}, u32[]{:S(2)}, u32[]{:S(2)}) collective-permute-start(bf16[32,1024]{1,0:T(8,128)(2,1)S(1)} %get-tuple-element.22), channel_id=1, source_target_pairs={{0,3},{1,0},{2,1},{3,2},{4,7},{5,4},{6,5},{7,6},{8,11},{9,8},{10,9... | collective-permute-start | bytes 196616 | tf_op jit(solution)/shard_map/ppermute | solution.py:288
  12.3 28.1 %collective-permute-start = (bf16[2048,512]{1,0:T(8,128)(2,1)}, bf16[2048,512]{1,0:T(8,128)(2,1)S(1)}, u32[]{:S(2)}, u32[]{:S(2)}) collective-permute-start(bf16[2048,512]{1,0:T(8,128)(2,1)} %bitcast.3.values_ref), channel_id=1, source_target_pairs={{0,4},{4,0},{8,12},{12,8},{16,20},{20,16},{24,28},{28,24},{1,5},{5... | collective-permute-start | bytes 6291464 | tf_op jit(solution)/shard_map/ppermute | solution.py:349
  16.4 46.7 %collective-permute-start.2 = (bf16[1280,512]{1,0:T(8,128)(2,1)}, bf16[1280,512]{1,0:T(8,128)(2,1)}, u32[]{:S(2)}, u32[]{:S(2)}) collective-permute-start(bf16[1280,512]{1,0:T(8,128)(2,1)} %get-tuple-element.15), channel_id=1, source_target_pairs={{0,28},{4,8},{8,4},{12,16},{16,12},{20,24},{24,20},{28,0},{1,29},{... | collective-permute-start | bytes 3932168 | tf_op jit(solution)/shard_map/ppermute | solution.py:348
  18.9 11.3 %collective-permute-start.6 = (f32[2,2,32,512]{3,2,1,0:T(8,128)}, f32[2,2,32,512]{3,2,1,0:T(8,128)}, u32[]{:S(2)}, u32[]{:S(2)}) collective-permute-start(f32[2,2,32,512]{3,2,1,0:T(8,128)} %select_bitcast_fusion), channel_id=1, source_target_pairs={{0,4},{4,0},{8,12},{12,8},{16,20},{20,16},{24,28},{28,24},{1,5},{5... | collective-permute-start | bytes 786440 | tf_op jit(solution)/shard_map/ppermute | solution.py:308
  22.0 31.4 %collective-permute-start.1 = (bf16[256,512]{1,0:T(8,128)(2,1)}, bf16[256,512]{1,0:T(8,128)(2,1)S(1)}, u32[]{:S(2)}, u32[]{:S(2)}) collective-permute-start(bf16[256,512]{1,0:T(8,128)(2,1)} %slice_bitcast_fusion.2), channel_id=1, source_target_pairs={{0,28},{4,8},{8,4},{12,16},{16,12},{20,24},{24,20},{28,0},{1,29},{... | collective-permute-start | bytes 786440 | tf_op jit(solution)/shard_map/ppermute | solution.py:348
  22.2 47.2 %collective-permute-start.10 = (bf16[512,384]{1,0:T(8,128)(2,1)}, bf16[512,384]{1,0:T(8,128)(2,1)S(1)}, u32[]{:S(2)}, u32[]{:S(2)}) collective-permute-start(bf16[512,384]{1,0:T(8,128)(2,1)} %get-tuple-element.18), channel_id=1, source_target_pairs={{0,28},{4,8},{8,4},{12,16},{16,12},{20,24},{24,20},{28,0},{1,29},{... | collective-permute-start | bytes 1179656 | tf_op jit(solution)/shard_map/ppermute | solution.py:348
  31.3 9.2 %copy-start.4 = (bf16[512,128]{1,0:T(8,128)(2,1)S(1)}, bf16[512,128]{1,0:T(8,128)(2,1)}, u32[]{:S(2)}) copy-start(bf16[512,128]{1,0:T(8,128)(2,1)} %get-tuple-element.17) | copy-start | bytes 393220
  31.3 7.1 %collective-permute-start.7 = (f32[2,32,512]{2,1,0:T(8,128)S(1)}, f32[2,32,512]{2,1,0:T(8,128)S(1)}, u32[]{:S(2)}, u32[]{:S(2)}) collective-permute-start(f32[2,32,512]{2,1,0:T(8,128)S(1)} %select_bitcast_fusion.1), channel_id=1, source_target_pairs={{0,16},{4,20},{8,24},{12,28},{16,0},{20,4},{24,8},{28,12},{1,17},{... | collective-permute-start | bytes 393224 | tf_op jit(solution)/shard_map/ppermute | solution.py:308
  38.4 24.7 %collective-permute-start.8 = (bf16[32,512]{1,0:T(8,128)(2,1)S(1)}, bf16[32,512]{1,0:T(8,128)(2,1)S(1)}, u32[]{:S(2)}, u32[]{:S(2)}) collective-permute-start(bf16[32,512]{1,0:T(8,128)(2,1)S(1)} %fusion.27), channel_id=1, source_target_pairs={{0,8},{4,12},{8,0},{12,4},{16,24},{20,28},{24,16},{28,20},{1,9},{5... | collective-permute-start | bytes 98312 | tf_op jit(solution)/shard_map/ppermute | solution.py:308
  40.5 1.4 %copy-start.2 = (bf16[2048,512]{1,0:T(8,128)(2,1)}, bf16[2048,512]{1,0:T(8,128)(2,1)S(1)}, u32[]{:S(2)}) copy-start(bf16[2048,512]{1,0:T(8,128)(2,1)S(1)} %collective-permute-done.near_ref) | copy-start | bytes 6291460
  40.5 31.1 %collective-permute-start.9 = (bf16[512,128]{1,0:T(8,128)(2,1)S(1)}, bf16[512,128]{1,0:T(8,128)(2,1)S(1)}, u32[]{:S(2)}, u32[]{:S(2)}) collective-permute-start(bf16[512,128]{1,0:T(8,128)(2,1)S(1)} %copy-done.4), channel_id=1, source_target_pairs={{0,28},{4,8},{8,4},{12,16},{16,12},{20,24},{24,20},{28,0},{1,29},{... | collective-permute-start | bytes 393224 | tf_op jit(solution)/shard_map/ppermute | solution.py:348
  41.9 21.2 %copy-start.1 = (bf16[1,1,2048,32]{2,3,1,0:T(8,128)(2,1)S(1)}, bf16[1,1,2048,32]{2,3,1,0:T(8,128)(2,1)}, u32[]{:S(2)}) copy-start(bf16[1,1,2048,32]{2,3,1,0:T(8,128)(2,1)} %param.14) | copy-start | bytes 393220
  53.4 9.7 %copy-start.3 = (bf16[256,512]{1,0:T(8,128)(2,1)}, bf16[256,512]{1,0:T(8,128)(2,1)S(1)}, u32[]{:S(2)}) copy-start(bf16[256,512]{1,0:T(8,128)(2,1)S(1)} %collective-permute-done.1.rest_0_) | copy-start | bytes 786436

commit v5 on v4

--- a/solution.py
+++ b/solution.py
@@ -31,36 +31,44 @@
     return pltpu.CompilerParams(vmem_limit_bytes=GRANT)
 
 
-def split(values, bounds):
+def split(values, bounds, basis=None):
     def kernel(values_ref, *rest):
-        outs, held, sems = rest[: len(bounds)], rest[len(bounds) : -1], rest[-1]
-        reads = [
+        count, sems = len(bounds), rest[-1]
+        outs = rest[:count] if basis is None else rest[1 : 1 + count]
+        copies = [
             pltpu.make_async_copy(
-                values_ref.at[pl.ds(row, size), pl.ds(column, width)], ref, sems.at[c]
+                values_ref.at[pl.ds(row, size), pl.ds(column, width)], out, sems.at[c]
             )
-            for c, ((row, size, column, width), ref) in enumerate(zip(bounds, held))
+            for c, ((row, size, column, width), out) in enumerate(zip(bounds, outs))
         ]
-        for read in reads:
-            read.start()
-        writes = []
-        for c, read in enumerate(reads):
-            read.wait()
-            write = pltpu.make_async_copy(held[c], outs[c], sems.at[c + len(bounds)])
-            write.start()
-            writes.append(write)
-        for write in writes:
-            write.wait()
+        if basis is not None:
+            copies.append(pltpu.make_async_copy(values_ref, rest[-3], sems.at[count]))
+            copies.append(pltpu.make_async_copy(rest[0], rest[-2], sems.at[count + 1]))
+        for copy in copies:
+            copy.start()
+        for copy in copies:
+            copy.wait()
+        if basis is not None:
+            sums_ref = rest[1 + count]
+            sums_ref[...] = jnp.dot(
+                rest[-2][...], rest[-3][...], preferred_element_type=jnp.float32
+            ).astype(sums_ref.dtype)
 
     shapes = [(size, width) for _, size, _, width in bounds]
-    scratch = [pltpu.VMEM(shape, values.dtype) for shape in shapes]
+    arguments = [in_hbm(values)]
+    scratch = []
+    if basis is not None:
+        arguments.append(in_hbm(basis))
+        shapes.append((basis.shape[0], values.shape[1]))
+        scratch = [pltpu.VMEM(value.shape, value.dtype) for value in (values, basis)]
     return pl.pallas_call(
         kernel,
-        in_specs=[pl.BlockSpec(memory_space=pltpu.HBM)],
-        out_specs=[pl.BlockSpec(memory_space=pltpu.HBM) for _ in bounds],
-        out_shape=[pltpu.HBM(shape, values.dtype) for shape in shapes],
-        scratch_shapes=scratch + [pltpu.SemaphoreType.DMA((2 * len(bounds),))],
+        in_specs=[pl.BlockSpec(memory_space=pltpu.HBM) for _ in arguments],
+        out_specs=[whole() for _ in shapes],
+        out_shape=[pltpu.VMEM(shape, values.dtype) for shape in shapes],
+        scratch_shapes=scratch + [pltpu.SemaphoreType.DMA((len(bounds) + 2,))],
         compiler_params=grant(),
-    )(in_hbm(values))
+    )(*arguments)
 
 
 def own_product(tile, values, part, parts, total=None):
@@ -74,9 +82,9 @@
 
     in_specs = [
         pl.BlockSpec((tile.shape[0], block), lambda i: (0, first + i)),
-        whole(),
+        pl.BlockSpec(values.shape, lambda i: (0, 0)),
     ]
-    arguments = [in_hbm(tile), in_vmem(values)]
+    arguments = [in_hbm(tile), in_hbm(values)]
     if total is not None:
         in_specs.append(pl.BlockSpec(memory_space=pltpu.HBM))
         arguments.append(in_hbm(total))
@@ -165,8 +173,10 @@
         here = step_rows(block)
 
         def fetch():
-            row, copies = 0, []
-            for c, far_ref in enumerate(rest[:count]):
+            lead = rest[0].shape[0]
+            row, copies = lead, []
+            values_ref[0:lead, :] = rest[0][...]
+            for c, far_ref in enumerate(rest[1:count]):
                 rows = pl.ds(row, far_ref.shape[0])
                 copies.append(pltpu.make_async_copy(far_ref, values_ref.at[rows], sems.at[c]))
                 copies[-1].start()
@@ -183,9 +193,11 @@
         out_ref[here, :] = result + contract(basis_ref[:, here], dual)
 
     arguments = [which] + [in_vmem(value) for value in (total, tile, near)]
-    arguments += [in_hbm(piece) for piece in far] + [in_vmem(value) for value in extra]
+    arguments += [in_vmem(far[0])] + [in_hbm(piece) for piece in far[1:]]
+    arguments += [in_vmem(value) for value in extra]
     in_specs = [pl.BlockSpec(memory_space=pltpu.SMEM)] + [whole() for _ in range(3)]
-    in_specs += [pl.BlockSpec(memory_space=pltpu.HBM) for _ in far] + [whole() for _ in extra]
+    in_specs += [whole()] + [pl.BlockSpec(memory_space=pltpu.HBM) for _ in far[1:]]
+    in_specs += [whole() for _ in extra]
     return pl.pallas_call(
         kernel,
         grid=(points // block,),
@@ -335,19 +347,21 @@
     ).astype(jnp.int32).reshape(1)
 
     unit = points // 8
+    lead = unit * 2
     width = local.shape[1]
     early = width * 3 // 4
     bounds = [
-        (unit, 5 * unit, 0, width),
+        (lead, 6 * unit - lead, 0, width),
         (6 * unit, 2 * unit, 0, early),
         (6 * unit, 2 * unit, early, width - early),
     ]
-    pieces = [lax.slice_in_dim(local, 0, unit), *split(local, bounds)]
+    pieces = list(split(local, [(0, lead, 0, width)]))
+    *rest, coefficients = split(local, bounds, row_cluster_basis[0, 0].T)
+    pieces += rest
     far = []
     for piece in pieces:
         far.append(lax.ppermute(piece, "row", far_pairs))
     near = lax.ppermute(local, "row", near_pairs)
-    coefficients = contract(row_cluster_basis[0, 0], local).astype(jnp.bfloat16)
     blocks = coupling_blocks(
         couplings[0, 0], adm_targets[0, 0], adm_ranks[0, 0], adm_count[0, 0], rows, cols
     )

time: 73.4 us -> 77.7 us (1.059)
  waiting for transfers between devices: 17 us -> 24.9 us
  matrix products: 3.48 us -> 1.44 us
  local copies, waits for them, and re-layouts: 2.88 us -> 1.18 us
  Pallas kernels: 29.3 us -> 30.1 us
    ppermute x3, waiting for transfers between devices: 10.7 us -> 20.1 us  [dual_of(): lax.ppermute(outgoing, 'row', [(i, i ^ 1 << bit) for i in range(rows)])]
    ppermute x4, waiting for transfers between devices: 6.25 us -> 0.01 us  [on_device(): far.append(lax.ppermute(piece, 'row', far_pairs))]
    ppermute x3, waiting for transfers between devices: 0.01 us -> 4.77 us  [dual_of(): lax.ppermute(outgoing, 'col', [(i, (i + shift) % cols) for i in range(col...]
    dot_general x4 -> x3, matrix products: 3.48 us -> 1.44 us  [contract(): lax.dot_general(tile, values, (((0,), (0,)), ((), ())), preferred_element...]
    slice x1 -> x0, local copies, waits for them, and re-layouts: 1.67 us -> none  [on_device(): pieces = [lax.slice_in_dim(local, 0, unit), *split(local, bounds)]]
    pallas_call x1 -> x2, Pallas kernels: 2.6 us -> 3.66 us  [split(): pl.pallas_call(kernel, in_specs=[pl.BlockSpec(memory_space=pltpu.HBM) for...]
    ppermute x3, starting transfers between devices: 3.76 us -> 4.69 us  [dual_of(): lax.ppermute(outgoing, 'row', [(i, i ^ 1 << bit) for i in range(rows)])]
    ppermute x3, starting transfers between devices: 5.54 us -> 4.65 us  [dual_of(): lax.ppermute(outgoing, 'col', [(i, (i + shift) % cols) for i in range(col...]
  transfers between devices with their start and end apart: 11 -> 11, of which waited for: 3 -> 2; matrix products, arithmetic and copies ran while one was open for 5% -> 3% of each run, Pallas kernels for 38% -> 34%
where the time goes in v5:
time: 77.7 us; the launch traced here: 77.4 us
  Pallas kernels  30.1 us (39%)
  waiting for transfers between devices  24.9 us (32%)
  starting transfers between devices  14.6 us (19%)
  other arithmetic  3.65 us (5%)
  between operations  1.54 us (2%)
  matrix products  1.44 us (2%)
  local copies, waits for them, and re-layouts  1.18 us (2%)
    ppermute x3, waiting for transfers between devices, dual_of(): lax.ppermute(outgoing, 'row', [(i, i ^ 1 << bit) for i in range(rows)])  20.1 us
    pallas_call x2, Pallas kernels, own_product(): pl.pallas_call(kernel, grid=(steps,), in_specs=in_specs, out_specs=pl.Blo...  11.6 us
    pallas_call x1, Pallas kernels, add_rows(): pl.pallas_call(kernel, grid=(points // block,), in_specs=in_specs, out_sp...  6.05 us
    pallas_call x1, Pallas kernels, stage(): pl.pallas_call(kernel, in_specs=[pl.BlockSpec(memory_space=pltpu.HBM) for...  5.27 us
    ppermute x3, waiting for transfers between devices, dual_of(): lax.ppermute(outgoing, 'col', [(i, (i + shift) % cols) for i in range(col...  4.77 us
    ppermute x3, starting transfers between devices, dual_of(): lax.ppermute(outgoing, 'row', [(i, i ^ 1 << bit) for i in range(rows)])  4.69 us
    ppermute x3, starting transfers between devices, dual_of(): lax.ppermute(outgoing, 'col', [(i, (i + shift) % cols) for i in range(col...  4.65 us
    ppermute x4, starting transfers between devices, on_device(): far.append(lax.ppermute(piece, 'row', far_pairs))  3.71 us
  transfers between devices with their start and end apart: 11, of which 2 were waited for; matrix products, arithmetic and copies ran while one was open for 3% of the time, Pallas kernels for 34%

profile of v5, /device:TPU:1, one launch (start us, length us, event | category | flops | bytes accessed | tf_op | source)
XLA Modules:
  0.0 77.4 jit_solution(14564317106958769717)
XLA Ops:
  0.7 0.7 fusion.32
  1.3 1.0 %bitcast_multiply_fusion = bf16[64,1024]{0,1:T(8,128)(2,1)S(1)} fusion(bf16[1,1,64,32,32]{2,4,3,1,0:T(8,128)(2,1)} %param.15, bf16[64,32]{0,1:T(8,128)(2,1)S(1)} %fusion.32), kind=kLoop, calls=%fused_computation.14 | loop fusion | flops 131072 | bytes 266240 | tf_op jit(solution)/shard_map/mul | solution.py:280
  2.3 0.9 %reduce-precision_convert_fusion = (bf16[32,1024]{1,0:T(8,128)(2,1)S(1)}, bf16[32,1024]{1,0:T(8,128)(2,1)S(1)}) fusion(bf16[64,1024]{0,1:T(8,128)(2,1)S(1)} %bitcast_multiply_fusion, s32[64]{0:T(128)} %bitcast.76), kind=kOutput, calls=%fused_computation.18 | convolution fusion | flops 4329472 | bytes 262400 | tf_op jit(solution)/shard_map/dot_general | solution.py:13
  3.3 0.2 stack.10
  3.5 0.2 copy.15
  3.6 0.2 stack.9
  3.8 0.2 copy.14
  4.1 0.4 reshape.110
  4.6 2.6 %shard_map.104 = (bf16[1024,512]{1,0:T(8,128)(2,1)S(1)}, bf16[512,384]{1,0:T(8,128)(2,1)S(1)}, bf16[512,128]{1,0:T(8,128)(2,1)S(1)}, bf16[32,512]{1,0:T(8,128)(2,1)S(1)}) custom-call(bf16[2048,512]{1,0:T(8,128)(2,1)} %bitcast.65, bf16[32,2048]{1,0:T(8,128)(2,1)} %bitcast.75), custom_call_target="tpu_custom_call" | custom-call | tf_op jit(solution)/shard_map/pallas_call | solution.py:64
  7.3 4.2 %collective-permute-start.5 = (bf16[32,1024]{1,0:T(8,128)(2,1)S(1)}, bf16[32,1024]{1,0:T(8,128)(2,1)S(1)}, u32[]{:S(2)}, u32[]{:S(2)}) collective-permute-start(bf16[32,1024]{1,0:T(8,128)(2,1)S(1)} %get-tuple-element.24), channel_id=1, source_target_pairs={{0,3},{1,0},{2,1},{3,2},{4,7},{5,4},{6,5},{7,6},{8,11},{9,8},{10,9... | collective-permute-start | bytes 196616 | tf_op jit(solution)/shard_map/ppermute | solution.py:300
  11.5 0.5 collective-permute-start.3
  11.9 1.5 %collective-permute-start = (bf16[2048,512]{1,0:T(8,128)(2,1)}, bf16[2048,512]{1,0:T(8,128)(2,1)}, u32[]{:S(2)}, u32[]{:S(2)}) collective-permute-start(bf16[2048,512]{1,0:T(8,128)(2,1)} %bitcast.66), channel_id=1, source_target_pairs={{0,4},{4,0},{8,12},{12,8},{16,20},{20,16},{24,28},{28,24},{1,5},{5... | collective-permute-start | bytes 6291464 | tf_op jit(solution)/shard_map/ppermute | solution.py:364
  13.4 4.8 %collective-permute-done.4 = bf16[32,1024]{1,0:T(8,128)(2,1)S(1)} collective-permute-done((bf16[32,1024]{1,0:T(8,128)(2,1)S(1)}, bf16[32,1024]{1,0:T(8,128)(2,1)S(1)}, u32[]{:S(2)}, u32[]{:S(2)}) %collective-permute-start.4) | collective-permute-done | bytes 65568 | tf_op jit(solution)/shard_map/ppermute | solution.py:300
  18.2 0.2 fusion.1
  18.5 0.3 convolution_add_fusion
  18.7 0.8 select_bitcast_fusion
  19.5 0.7 collective-permute-start.6
  20.2 1.1 %shard_map.103 = bf16[512,512]{1,0:T(8,128)(2,1)S(1)} custom-call(bf16[2048,512]{1,0:T(8,128)(2,1)} %bitcast.67), custom_call_target="tpu_custom_call" | custom-call | tf_op jit(solution)/shard_map/pallas_call | solution.py:64
  21.3 1.2 %collective-permute-start.1 = (bf16[512,512]{1,0:T(8,128)(2,1)S(1)}, bf16[512,512]{1,0:T(8,128)(2,1)S(1)}, u32[]{:S(2)}, u32[]{:S(2)}) collective-permute-start(bf16[512,512]{1,0:T(8,128)(2,1)S(1)} %shard_map.103), channel_id=1, source_target_pairs={{0,28},{4,8},{8,4},{12,16},{16,12},{20,24},{24,20},{28,0},{1,29},{... | collective-permute-start | bytes 1572872 | tf_op jit(solution)/shard_map/ppermute | solution.py:363
  22.4 0.6 collective-permute-start.2
  23.1 1.1 %collective-permute-start.10 = (bf16[512,384]{1,0:T(8,128)(2,1)S(1)}, bf16[512,384]{1,0:T(8,128)(2,1)S(1)}, u32[]{:S(2)}, u32[]{:S(2)}) collective-permute-start(bf16[512,384]{1,0:T(8,128)(2,1)S(1)} %get-tuple-element.20), channel_id=1, source_target_pairs={{0,28},{4,8},{8,4},{12,16},{16,12},{20,24},{24,20},{28,0},{1,29},{... | collective-permute-start | bytes 1179656 | tf_op jit(solution)/shard_map/ppermute | solution.py:363
  24.8 5.8 %shard_map.100.rest_0_ = f32[2048,512]{1,0:T(8,128)} custom-call(bf16[2048,2048]{1,0:T(8,128)(2,1)} %bitcast.70, bf16[2048,512]{1,0:T(8,128)(2,1)} %bitcast.68), custom_call_target="tpu_custom_call" | custom-call | flops 2147483648 | bytes 8388608 | tf_op jit(solution)/shard_map/pallas_call | solution.py:91
  30.6 1.0 %bitcast_add_fusion = f32[2,2,32,512]{3,2,1,0:T(8,128)S(1)} fusion(f32[2,2,32,512]{3,2,1,0:T(8,128)} %collective-permute-done.6, f32[2,2,2,32,512]{4,3,2,1,0:T(8,128)S(1)} %bitcast.74, pred[]{:T(512)S(6)} %eq.41), kind=kLoop, calls=%fused_computation.13 | loop fusion | flops 131072 | bytes 1048577 | tf_op jit(solution)/shard_map/add | solution.py:322
  31.7 1.3 %collective-permute-start.7 = (f32[2,32,512]{2,1,0:T(8,128)S(1)}, f32[2,32,512]{2,1,0:T(8,128)S(1)}, u32[]{:S(2)}, u32[]{:S(2)}) collective-permute-start(f32[2,32,512]{2,1,0:T(8,128)S(1)} %select_bitcast_fusion.1), channel_id=1, source_target_pairs={{0,16},{4,20},{8,24},{12,28},{16,0},{20,4},{24,8},{28,12},{1,17},{... | collective-permute-start | bytes 393224 | tf_op jit(solution)/shard_map/ppermute | solution.py:320
  33.0 5.8 %shard_map.101.total_ref = f32[2048,512]{1,0:T(8,128)} custom-call(bf16[2048,2048]{1,0:T(8,128)(2,1)} %bitcast.71, bf16[2048,512]{1,0:T(8,128)(2,1)} %bitcast.69, f32[2048,512]{1,0:T(8,128)} %shard_map.100.rest_0_), custom_call_target="tpu_custom_call", output_to_operand_aliasing={{}: (2, {})} | custom-call | flops 2147483648 | bytes 8388608 | tf_op jit(solution)/shard_map/pallas_call | solution.py:91
  38.8 2.7 %collective-permute-start.8 = (bf16[32,512]{1,0:T(8,128)(2,1)S(1)}, bf16[32,512]{1,0:T(8,128)(2,1)S(1)}, u32[]{:S(2)}, u32[]{:S(2)}) collective-permute-start(bf16[32,512]{1,0:T(8,128)(2,1)S(1)} %fusion.26), channel_id=1, source_target_pairs={{0,8},{4,12},{8,0},{12,4},{16,24},{20,28},{24,16},{28,20},{1,9},{5... | collective-permute-start | bytes 98312 | tf_op jit(solution)/shard_map/ppermute | solution.py:320
  41.5 0.8 %collective-permute-start.9 = (bf16[512,128]{1,0:T(8,128)(2,1)S(1)}, bf16[512,128]{1,0:T(8,128)(2,1)S(1)}, u32[]{:S(2)}, u32[]{:S(2)}) collective-permute-start(bf16[512,128]{1,0:T(8,128)(2,1)S(1)} %get-tuple-element.19), channel_id=1, source_target_pairs={{0,28},{4,8},{8,4},{12,16},{16,12},{20,24},{24,20},{28,0},{1,29},{... | collective-permute-start | bytes 393224 | tf_op jit(solution)/shard_map/ppermute | solution.py:363
  42.3 5.3 %shard_map.102 = (bf16[1536,2048]{1,0:T(8,128)(2,1)S(1)}, bf16[2048,512]{1,0:T(8,128)(2,1)S(1)}, bf16[2048,512]{1,0:T(8,128)(2,1)S(1)}, f32[2048,512]{1,0:T(8,128)S(1)}) custom-call(bf16[2048,2048]{1,0:T(8,128)(2,1)} %bitcast.72, bf16[2048,512]{1,0:T(8,128)(2,1)} %collective-permute-done.near_ref, f32[2048,512]{1,0:T(8,128)} %shard_map.101.total_ref), custom_call_target="tpu_custom_call" | custom-call | tf_op jit(solution)/shard_map/pallas_call | solution.py:146
  47.6 20.1 %collective-permute-done.8.rest_4_ = bf16[32,512]{1,0:T(8,128)(2,1)S(1)} collective-permute-done((bf16[32,512]{1,0:T(8,128)(2,1)S(1)}, bf16[32,512]{1,0:T(8,128)(2,1)S(1)}, u32[]{:S(2)}, u32[]{:S(2)}) %collective-permute-start.8) | collective-permute-done | bytes 32800 | tf_op jit(solution)/shard_map/ppermute | solution.py:320
  67.7 6.0 %shard_map.105.total_ref = f32[2048,512]{1,0:T(8,128)S(1)} custom-call(s32[1]{0:T(128)} %bitcast.1.which_ref, f32[2048,512]{1,0:T(8,128)S(1)} %get-tuple-element.13.total_ref, bf16[1536,2048]{1,0:T(8,128)(2,1)S(1)} %get-tuple-element.14.tile_ref, bf16[2048,512]{1,0:T(8,128)(2,1)S(1)} %get-tuple-element.15.near_ref, ...), custom_call_target="tpu_custom_call", output_to_operand_aliasing={{}: (1, {})} | custom-call | flops 3221225472 | bytes 1572864 | tf_op jit(solution)/shard_map/pallas_call | solution.py:201
  73.8 2.1 %shard_map.106.rest_0_ = f32[2048,512]{1,0:T(8,128)} custom-call(s32[1]{0:T(128)} %bitcast.1.which_ref, f32[2048,512]{1,0:T(8,128)S(1)} %shard_map.105.total_ref, bf16[2048,512]{1,0:T(8,128)(2,1)S(1)} %get-tuple-element.18.flipped_ref, bf16[512,384]{1,0:T(8,128)(2,1)S(1)} %collective-permute-done.10.far_ref, bf16[2048,512]{1,0:T(8,128)(2,1)S(1)} %get-tuple-element.15.near_ref), custom_call_target="tpu_custom_call" | custom-call | flops 805306368 | bytes 8388608 | tf_op jit(solution)/shard_map/pallas_call | solution.py:254
  75.9 1.5 %shard_map.107 = f32[2048,512]{1,0:T(8,128)} custom-call(s32[1]{0:T(128)} %bitcast.1.which_ref, f32[2048,512]{1,0:T(8,128)S(1)} %shard_map.105.total_ref, bf16[2048,512]{1,0:T(8,128)(2,1)S(1)} %get-tuple-element.18.flipped_ref, bf16[512,128]{1,0:T(8,128)(2,1)S(1)} %collective-permute-done.9.far_ref, ...), custom_call_target="tpu_custom_call", output_to_operand_aliasing={{}: (5, {})} | custom-call | flops 268435456 | bytes 4194304 | tf_op jit(solution)/shard_map/pallas_call | solution.py:254
  (21 shorter events, 0.3 us)
Async XLA Ops:
  7.3 6.2 %collective-permute-start.5 = (bf16[32,1024]{1,0:T(8,128)(2,1)S(1)}, bf16[32,1024]{1,0:T(8,128)(2,1)S(1)}, u32[]{:S(2)}, u32[]{:S(2)}) collective-permute-start(bf16[32,1024]{1,0:T(8,128)(2,1)S(1)} %get-tuple-element.24), channel_id=1, source_target_pairs={{0,3},{1,0},{2,1},{3,2},{4,7},{5,4},{6,5},{7,6},{8,11},{9,8},{10,9... | collective-permute-start | bytes 196616 | tf_op jit(solution)/shard_map/ppermute | solution.py:300
  11.5 6.7 %collective-permute-start.4 = (bf16[32,1024]{1,0:T(8,128)(2,1)S(1)}, bf16[32,1024]{1,0:T(8,128)(2,1)S(1)}, u32[]{:S(2)}, u32[]{:S(2)}) collective-permute-start(bf16[32,1024]{1,0:T(8,128)(2,1)S(1)} %get-tuple-element.23), channel_id=1, source_target_pairs={{0,2},{1,3},{2,0},{3,1},{4,6},{5,7},{6,4},{7,5},{8,10},{9,11},{10,... | collective-permute-start | bytes 196616 | tf_op jit(solution)/shard_map/ppermute | solution.py:300
  11.5 6.7 %collective-permute-start.3 = (bf16[32,1024]{1,0:T(8,128)(2,1)S(1)}, bf16[32,1024]{1,0:T(8,128)(2,1)S(1)}, u32[]{:S(2)}, u32[]{:S(2)}) collective-permute-start(bf16[32,1024]{1,0:T(8,128)(2,1)S(1)} %get-tuple-element.22), channel_id=1, source_target_pairs={{0,1},{1,2},{2,3},{3,0},{4,5},{5,6},{6,7},{7,4},{8,9},{9,10},{10,1... | collective-permute-start | bytes 196616 | tf_op jit(solution)/shard_map/ppermute | solution.py:300
  11.9 29.6 %collective-permute-start = (bf16[2048,512]{1,0:T(8,128)(2,1)}, bf16[2048,512]{1,0:T(8,128)(2,1)}, u32[]{:S(2)}, u32[]{:S(2)}) collective-permute-start(bf16[2048,512]{1,0:T(8,128)(2,1)} %bitcast.66), channel_id=1, source_target_pairs={{0,4},{4,0},{8,12},{12,8},{16,20},{20,16},{24,28},{28,24},{1,5},{5... | collective-permute-start | bytes 6291464 | tf_op jit(solution)/shard_map/ppermute | solution.py:364
  19.5 11.1 %collective-permute-start.6 = (f32[2,2,32,512]{3,2,1,0:T(8,128)}, f32[2,2,32,512]{3,2,1,0:T(8,128)}, u32[]{:S(2)}, u32[]{:S(2)}) collective-permute-start(f32[2,2,32,512]{3,2,1,0:T(8,128)} %select_bitcast_fusion), channel_id=1, source_target_pairs={{0,4},{4,0},{8,12},{12,8},{16,20},{20,16},{24,28},{28,24},{1,5},{5... | collective-permute-start | bytes 786440 | tf_op jit(solution)/shard_map/ppermute | solution.py:320
  21.3 46.5 %collective-permute-start.1 = (bf16[512,512]{1,0:T(8,128)(2,1)S(1)}, bf16[512,512]{1,0:T(8,128)(2,1)S(1)}, u32[]{:S(2)}, u32[]{:S(2)}) collective-permute-start(bf16[512,512]{1,0:T(8,128)(2,1)S(1)} %shard_map.103), channel_id=1, source_target_pairs={{0,28},{4,8},{8,4},{12,16},{16,12},{20,24},{24,20},{28,0},{1,29},{... | collective-permute-start | bytes 1572872 | tf_op jit(solution)/shard_map/ppermute | solution.py:363
  22.4 45.3 %collective-permute-start.2 = (bf16[1024,512]{1,0:T(8,128)(2,1)S(1)}, bf16[1024,512]{1,0:T(8,128)(2,1)}, u32[]{:S(2)}, u32[]{:S(2)}) collective-permute-start(bf16[1024,512]{1,0:T(8,128)(2,1)S(1)} %get-tuple-element.16), channel_id=1, source_target_pairs={{0,28},{4,8},{8,4},{12,16},{16,12},{20,24},{24,20},{28,0},{1,29},{... | collective-permute-start | bytes 3145736 | tf_op jit(solution)/shard_map/ppermute | solution.py:363
  23.1 50.7 %collective-permute-start.10 = (bf16[512,384]{1,0:T(8,128)(2,1)S(1)}, bf16[512,384]{1,0:T(8,128)(2,1)S(1)}, u32[]{:S(2)}, u32[]{:S(2)}) collective-permute-start(bf16[512,384]{1,0:T(8,128)(2,1)S(1)} %get-tuple-element.20), channel_id=1, source_target_pairs={{0,28},{4,8},{8,4},{12,16},{16,12},{20,24},{24,20},{28,0},{1,29},{... | collective-permute-start | bytes 1179656 | tf_op jit(solution)/shard_map/ppermute | solution.py:363
  31.7 7.1 %collective-permute-start.7 = (f32[2,32,512]{2,1,0:T(8,128)S(1)}, f32[2,32,512]{2,1,0:T(8,128)S(1)}, u32[]{:S(2)}, u32[]{:S(2)}) collective-permute-start(f32[2,32,512]{2,1,0:T(8,128)S(1)} %select_bitcast_fusion.1), channel_id=1, source_target_pairs={{0,16},{4,20},{8,24},{12,28},{16,0},{20,4},{24,8},{28,12},{1,17},{... | collective-permute-start | bytes 393224 | tf_op jit(solution)/shard_map/ppermute | solution.py:320
  38.8 28.9 %collective-permute-start.8 = (bf16[32,512]{1,0:T(8,128)(2,1)S(1)}, bf16[32,512]{1,0:T(8,128)(2,1)S(1)}, u32[]{:S(2)}, u32[]{:S(2)}) collective-permute-start(bf16[32,512]{1,0:T(8,128)(2,1)S(1)} %fusion.26), channel_id=1, source_target_pairs={{0,8},{4,12},{8,0},{12,4},{16,24},{20,28},{24,16},{28,20},{1,9},{5... | collective-permute-start | bytes 98312 | tf_op jit(solution)/shard_map/ppermute | solution.py:320
  41.5 34.4 %collective-permute-start.9 = (bf16[512,128]{1,0:T(8,128)(2,1)S(1)}, bf16[512,128]{1,0:T(8,128)(2,1)S(1)}, u32[]{:S(2)}, u32[]{:S(2)}) collective-permute-start(bf16[512,128]{1,0:T(8,128)(2,1)S(1)} %get-tuple-element.19), channel_id=1, source_target_pairs={{0,28},{4,8},{8,4},{12,16},{16,12},{20,24},{24,20},{28,0},{1,29},{... | collective-permute-start | bytes 393224 | tf_op jit(solution)/shard_map/ppermute | solution.py:363
  42.3 25.4 %copy-start = (bf16[1,1,2048,32]{2,3,1,0:T(8,128)(2,1)S(1)}, bf16[1,1,2048,32]{2,3,1,0:T(8,128)(2,1)}, u32[]{:S(2)}) copy-start(bf16[1,1,2048,32]{2,3,1,0:T(8,128)(2,1)} %param.14) | copy-start | bytes 393220

commit v6 on v5

--- a/solution.py
+++ b/solution.py
@@ -108,44 +108,40 @@
     return pl.ds(pl.multiple_of(pl.program_id(0) * block, block), block)
 
 
-def choose(which_ref, fetch, near_ref, values_ref):
-    @pl.when(which_ref[0] == 2)
-    def _():
-        fetch()
-
-    @pl.when(which_ref[0] == 1)
-    def _():
-        values_ref[...] = near_ref[...]
-
-    @pl.when(which_ref[0] == 0)
-    def _():
-        values_ref[...] = jnp.zeros_like(values_ref)
-
-
-def stage(tile, near, total, start):
+def stage(tile, near, total, which, start):
     rows, points = tile.shape
     size = rows - start
     block = min(BLOCK, points)
 
-    def kernel(tile_ref, near_ref, total_ref, first_ref, flipped_ref, near_out, total_out, *scratch):
-        last_ref, sems = scratch
+    def kernel(which_ref, tile_ref, near_ref, total_ref, first_ref, flipped_ref, *rest):
+        near_out, total_out, last_ref, sems = rest
+        near_copy = pltpu.make_async_copy(near_ref, near_out, sems.at[3])
         copies = [
             pltpu.make_async_copy(tile_ref.at[pl.ds(start, size)], last_ref, sems.at[0]),
             pltpu.make_async_copy(tile_ref.at[pl.ds(0, start)], first_ref, sems.at[1]),
             pltpu.make_async_copy(total_ref, total_out, sems.at[2]),
-            pltpu.make_async_copy(near_ref, near_out, sems.at[3]),
         ]
         for copy in copies:
             copy.start()
+
+        @pl.when(which_ref[0] == 1)
+        def _():
+            near_copy.start()
+
         copies[0].wait()
         for at in range(0, points, block):
             flipped_ref[at : at + block, :] = last_ref[:, at : at + block].T
         for copy in copies[1:]:
             copy.wait()
 
+        @pl.when(which_ref[0] == 1)
+        def _():
+            near_copy.wait()
+
     return pl.pallas_call(
         kernel,
-        in_specs=[pl.BlockSpec(memory_space=pltpu.HBM) for _ in range(3)],
+        in_specs=[pl.BlockSpec(memory_space=pltpu.SMEM)]
+        + [pl.BlockSpec(memory_space=pltpu.HBM) for _ in range(3)],
         out_specs=[whole() for _ in range(4)],
         out_shape=[
             pltpu.VMEM((start, points), tile.dtype),
@@ -158,18 +154,19 @@
             pltpu.VMEM((size, points), tile.dtype),
             pltpu.SemaphoreType.DMA((4,)),
         ],
-    )(in_hbm(tile), in_hbm(near), in_hbm(total))
-
-
-def add_rows(total, tile, far, near, which, extra):
+    )(which, in_hbm(tile), in_hbm(near), in_hbm(total))
+
+
+def add_rows(total, tile, flipped, far, near, which, extra):
     points, columns = total.shape
     size = tile.shape[0]
     block = min(BLOCK, points)
     count = len(far)
-
-    def kernel(which_ref, total_ref, tile_ref, near_ref, *rest):
-        out_ref, values_ref, sems = rest[-3:]
-        basis_ref, kept_ref, incoming_ref = rest[count:-3]
+    steps = points // block
+
+    def kernel(which_ref, total_ref, tile_ref, flipped_ref, near_ref, *rest):
+        out_ref, final_ref, values_ref, sems, out_sems = rest[-5:]
+        basis_ref, kept_ref, incoming_ref = rest[count:-5]
         here = step_rows(block)
 
         def fetch():
@@ -184,31 +181,62 @@
             for copy in copies:
                 copy.wait()
 
-        @pl.when(pl.program_id(0) == 0)
-        def _():
-            choose(which_ref, fetch, near_ref.at[:size], values_ref)
+        @pl.when((pl.program_id(0) == 0) & (which_ref[0] == 2))
+        def _():
+            fetch()
 
         dual = (kept_ref[...] + incoming_ref[...].astype(jnp.float32)).astype(jnp.bfloat16)
-        result = total_ref[here, :] + contract(tile_ref[:, here], values_ref[...])
-        out_ref[here, :] = result + contract(basis_ref[:, here], dual)
-
-    arguments = [which] + [in_vmem(value) for value in (total, tile, near)]
+        out_ref[here, :] = total_ref[here, :] + contract(basis_ref[:, here], dual)
+
+        @pl.when(which_ref[0] == 2)
+        def _():
+            out_ref[here, :] += contract(tile_ref[:, here], values_ref[...])
+
+        @pl.when(which_ref[0] == 1)
+        def _():
+            result = contract(tile_ref[:, here], near_ref[:size, :])
+            out_ref[here, :] += result + jnp.dot(
+                flipped_ref[here, :], near_ref[size:, :], preferred_element_type=jnp.float32
+            )
+
+        def finished(step):
+            rows = pl.ds(step * block, block)
+            return pltpu.make_async_copy(
+                out_ref.at[rows], final_ref.at[rows], out_sems.at[step]
+            )
+
+        @pl.when(which_ref[0] != 2)
+        def _():
+            pltpu.make_async_copy(
+                out_ref.at[here], final_ref.at[here], out_sems.at[pl.program_id(0)]
+            ).start()
+
+        @pl.when((which_ref[0] != 2) & (pl.program_id(0) == steps - 1))
+        def _():
+            for step in range(steps):
+                finished(step).wait()
+
+    arguments = [which] + [in_vmem(value) for value in (total, tile, flipped, near)]
     arguments += [in_vmem(far[0])] + [in_hbm(piece) for piece in far[1:]]
     arguments += [in_vmem(value) for value in extra]
-    in_specs = [pl.BlockSpec(memory_space=pltpu.SMEM)] + [whole() for _ in range(3)]
+    in_specs = [pl.BlockSpec(memory_space=pltpu.SMEM)] + [whole() for _ in range(4)]
     in_specs += [whole()] + [pl.BlockSpec(memory_space=pltpu.HBM) for _ in far[1:]]
     in_specs += [whole() for _ in extra]
     return pl.pallas_call(
         kernel,
-        grid=(points // block,),
+        grid=(steps,),
         in_specs=in_specs,
-        out_specs=whole(),
-        out_shape=pltpu.VMEM((points, columns), jnp.float32),
+        out_specs=[whole(), pl.BlockSpec(memory_space=pltpu.HBM)],
+        out_shape=[
+            pltpu.VMEM((points, columns), jnp.float32),
+            pltpu.HBM((points, columns), jnp.float32),
+        ],
         input_output_aliases={1: 0},
         compiler_params=grant(),
         scratch_shapes=[
             pltpu.VMEM((size, columns), jnp.bfloat16),
             pltpu.SemaphoreType.DMA((count,)),
+            pltpu.SemaphoreType.DMA((steps,)),
         ],
         cost_estimate=pl.CostEstimate(
             flops=2 * size * points * columns,
@@ -218,48 +246,44 @@
     )(*arguments)
 
 
-def add_last(total, flipped, far, near, which, column, out=None):
+def add_last(total, flipped, far, which, column, out):
     points, columns = total.shape
     size, width = far.shape
     block = min(BLOCK // 2, points)
     steps = points // block
     here = pl.ds(column, width)
 
-    def kernel(which_ref, total_ref, flipped_ref, far_ref, near_ref, *rest):
-        out_ref, values_ref, staged_ref, sems = rest[-4:]
-
-        def fetch():
-            values_ref[...] = far_ref[...]
-
-        choose(which_ref, fetch, near_ref.at[points - size :, here], values_ref)
-        copies = []
-        for step in range(steps):
-            rows = pl.ds(step * block, block)
-            staged_ref[rows, :] = total_ref[rows, here] + jnp.dot(
-                flipped_ref[rows, :], values_ref[...], preferred_element_type=jnp.float32
-            )
-            copy = pltpu.make_async_copy(
-                staged_ref.at[rows], out_ref.at[rows, here], sems.at[step]
-            )
-            copy.start()
-            copies.append(copy)
-        for copy in copies:
-            copy.wait()
-
-    arguments = [which] + [in_vmem(value) for value in (total, flipped, far, near)]
-    in_specs = [pl.BlockSpec(memory_space=pltpu.SMEM)] + [whole() for _ in range(4)]
-    if out is not None:
-        arguments.append(in_hbm(out))
-        in_specs.append(pl.BlockSpec(memory_space=pltpu.HBM))
+    def kernel(which_ref, total_ref, flipped_ref, far_ref, *rest):
+        out_ref, staged_ref, sems = rest[-3:]
+
+        @pl.when(which_ref[0] == 2)
+        def _():
+            copies = []
+            for step in range(steps):
+                rows = pl.ds(step * block, block)
+                staged_ref[rows, :] = total_ref[rows, here] + jnp.dot(
+                    flipped_ref[rows, :], far_ref[...], preferred_element_type=jnp.float32
+                )
+                copy = pltpu.make_async_copy(
+                    staged_ref.at[rows], out_ref.at[rows, here], sems.at[step]
+                )
+                copy.start()
+                copies.append(copy)
+            for copy in copies:
+                copy.wait()
+
+    arguments = [which] + [in_vmem(value) for value in (total, flipped, far)]
+    in_specs = [pl.BlockSpec(memory_space=pltpu.SMEM)] + [whole() for _ in range(3)]
+    arguments.append(in_hbm(out))
+    in_specs.append(pl.BlockSpec(memory_space=pltpu.HBM))
     return pl.pallas_call(
         kernel,
         in_specs=in_specs,
         out_specs=pl.BlockSpec(memory_space=pltpu.HBM),
         out_shape=jax.ShapeDtypeStruct((points, columns), jnp.float32),
-        input_output_aliases={} if out is None else {5: 0},
+        input_output_aliases={4: 0},
         compiler_params=grant(),
         scratch_shapes=[
-            pltpu.VMEM((size, width), jnp.bfloat16),
             pltpu.VMEM((points, width), jnp.float32),
             pltpu.SemaphoreType.DMA((steps,)),
         ],
@@ -369,11 +393,11 @@
     total = own_product(self_tiles[0, 0], local, 0, 2)
     total = own_product(self_tiles[0, 0], local, 1, 2, total)
     side = side_tiles[0, 0]
-    first, flipped, near, total = stage(side, near, total, 6 * unit)
+    first, flipped, near, total = stage(side, near, total, which, 6 * unit)
     extra = (column_cluster_basis[0, 0].T, kept, incoming)
-    total = add_rows(total, first, far[:2], near, which, extra)
-    out = add_last(total, flipped, far[2], near, which, 0)
-    out = add_last(total, flipped, far[3], near, which, early, out)
+    total, out = add_rows(total, first, flipped, far[:2], near, which, extra)
+    out = add_last(total, flipped, far[2], which, 0, out)
+    out = add_last(total, flipped, far[3], which, early, out)
     return out[None, None]
 
 

time: 77.7 us -> 77.3 us (level)
  waiting for transfers between devices: 24.9 us -> 23.2 us
  starting transfers between devices: 14.6 us -> 15.7 us
    ppermute x3, waiting for transfers between devices: 4.77 us -> 2.44 us  [dual_of(): lax.ppermute(outgoing, 'col', [(i, (i + shift) % cols) for i in range(col...]
    ppermute x3, starting transfers between devices: 4.65 us -> 5.54 us  [dual_of(): lax.ppermute(outgoing, 'col', [(i, (i + shift) % cols) for i in range(col...]
where the time goes in v6:
time: 77.3 us; the launch traced here: 77 us
  Pallas kernels  30.3 us (39%)
  waiting for transfers between devices  23.2 us (30%)
  starting transfers between devices  15.7 us (20%)
  other arithmetic  3.64 us (5%)
  between operations  1.53 us (2%)
  matrix products  1.44 us (2%)
  local copies, waits for them, and re-layouts  1.18 us (2%)
    ppermute x3, waiting for transfers between devices, dual_of(): lax.ppermute(outgoing, 'row', [(i, i ^ 1 << bit) for i in range(rows)])  20.7 us
    pallas_call x2, Pallas kernels, own_product(): pl.pallas_call(kernel, grid=(steps,), in_specs=in_specs, out_specs=pl.Blo...  11.6 us
    pallas_call x1, Pallas kernels, add_rows(): pl.pallas_call(kernel, grid=(steps,), in_specs=in_specs, out_specs=[whole...  6.92 us
    ppermute x3, starting transfers between devices, dual_of(): lax.ppermute(outgoing, 'col', [(i, (i + shift) % cols) for i in range(col...  5.54 us
    ppermute x3, starting transfers between devices, dual_of(): lax.ppermute(outgoing, 'row', [(i, i ^ 1 << bit) for i in range(rows)])  4.84 us
    pallas_call x1, Pallas kernels, stage(): pl.pallas_call(kernel, in_specs=[pl.BlockSpec(memory_space=pltpu.SMEM)] +...  4.68 us
    ppermute x4, starting transfers between devices, on_device(): far.append(lax.ppermute(piece, 'row', far_pairs))  3.77 us
    pallas_call x2, Pallas kernels, split(): pl.pallas_call(kernel, in_specs=[pl.BlockSpec(memory_space=pltpu.HBM) for...  3.66 us
  transfers between devices with their start and end apart: 11, of which 2 were waited for; matrix products, arithmetic and copies ran while one was open for 3% of the time, Pallas kernels for 34%

profile of v6, /device:TPU:1, one launch (start us, length us, event | category | flops | bytes accessed | tf_op | source)
XLA Modules:
  0.0 77.0 jit_solution(97487602352154031)
XLA Ops:
  0.7 0.7 fusion.32
  1.3 1.0 %bitcast_multiply_fusion = bf16[64,1024]{0,1:T(8,128)(2,1)S(1)} fusion(bf16[1,1,64,32,32]{2,4,3,1,0:T(8,128)(2,1)} %param.15, bf16[64,32]{0,1:T(8,128)(2,1)S(1)} %fusion.32), kind=kLoop, calls=%fused_computation.14 | loop fusion | flops 131072 | bytes 266240 | tf_op jit(solution)/shard_map/mul | solution.py:304
  2.3 0.9 %reduce-precision_convert_fusion = (bf16[32,1024]{1,0:T(8,128)(2,1)S(1)}, bf16[32,1024]{1,0:T(8,128)(2,1)S(1)}) fusion(bf16[64,1024]{0,1:T(8,128)(2,1)S(1)} %bitcast_multiply_fusion, s32[64]{0:T(128)} %bitcast.76), kind=kOutput, calls=%fused_computation.18 | convolution fusion | flops 4329472 | bytes 262400 | tf_op jit(solution)/shard_map/dot_general | solution.py:13
  3.3 0.2 stack.9
  3.5 0.2 copy.15
  3.6 0.2 stack.10
  4.1 0.4 reshape.110
  4.6 2.6 %shard_map.104 = (bf16[1024,512]{1,0:T(8,128)(2,1)S(1)}, bf16[512,384]{1,0:T(8,128)(2,1)S(1)}, bf16[512,128]{1,0:T(8,128)(2,1)S(1)}, bf16[32,512]{1,0:T(8,128)(2,1)S(1)}) custom-call(bf16[2048,512]{1,0:T(8,128)(2,1)} %bitcast.65, bf16[32,2048]{1,0:T(8,128)(2,1)} %bitcast.75), custom_call_target="tpu_custom_call" | custom-call | tf_op jit(solution)/shard_map/pallas_call | solution.py:64
  7.3 2.2 %collective-permute-start.3 = (bf16[32,1024]{1,0:T(8,128)(2,1)S(1)}, bf16[32,1024]{1,0:T(8,128)(2,1)S(1)}, u32[]{:S(2)}, u32[]{:S(2)}) collective-permute-start(bf16[32,1024]{1,0:T(8,128)(2,1)S(1)} %get-tuple-element.26), channel_id=1, source_target_pairs={{0,1},{1,2},{2,3},{3,0},{4,5},{5,6},{6,7},{7,4},{8,9},{9,10},{10,1... | collective-permute-start | bytes 196616 | tf_op jit(solution)/shard_map/ppermute | solution.py:324
  9.4 2.3 %collective-permute-start.4 = (bf16[32,1024]{1,0:T(8,128)(2,1)S(1)}, bf16[32,1024]{1,0:T(8,128)(2,1)S(1)}, u32[]{:S(2)}, u32[]{:S(2)}) collective-permute-start(bf16[32,1024]{1,0:T(8,128)(2,1)S(1)} %get-tuple-element.27), channel_id=1, source_target_pairs={{0,2},{1,3},{2,0},{3,1},{4,6},{5,7},{6,4},{7,5},{8,10},{9,11},{10,... | collective-permute-start | bytes 196616 | tf_op jit(solution)/shard_map/ppermute | solution.py:324
  11.8 1.1 %collective-permute-start.5 = (bf16[32,1024]{1,0:T(8,128)(2,1)S(1)}, bf16[32,1024]{1,0:T(8,128)(2,1)S(1)}, u32[]{:S(2)}, u32[]{:S(2)}) collective-permute-start(bf16[32,1024]{1,0:T(8,128)(2,1)S(1)} %get-tuple-element.28), channel_id=1, source_target_pairs={{0,3},{1,0},{2,1},{3,2},{4,7},{5,4},{6,5},{7,6},{8,11},{9,8},{10,9... | collective-permute-start | bytes 196616 | tf_op jit(solution)/shard_map/ppermute | solution.py:324
  12.8 1.5 %collective-permute-start = (bf16[2048,512]{1,0:T(8,128)(2,1)}, bf16[2048,512]{1,0:T(8,128)(2,1)}, u32[]{:S(2)}, u32[]{:S(2)}) collective-permute-start(bf16[2048,512]{1,0:T(8,128)(2,1)} %bitcast.66), channel_id=1, source_target_pairs={{0,4},{4,0},{8,12},{12,8},{16,20},{20,16},{24,28},{28,24},{1,5},{5... | collective-permute-start | bytes 6291464 | tf_op jit(solution)/shard_map/ppermute | solution.py:388
  14.3 2.4 %collective-permute-done.4 = bf16[32,1024]{1,0:T(8,128)(2,1)S(1)} collective-permute-done((bf16[32,1024]{1,0:T(8,128)(2,1)S(1)}, bf16[32,1024]{1,0:T(8,128)(2,1)S(1)}, u32[]{:S(2)}, u32[]{:S(2)}) %collective-permute-start.4) | collective-permute-done | bytes 65568 | tf_op jit(solution)/shard_map/ppermute | solution.py:324
  16.8 0.2 fusion.1
  17.1 0.3 convolution_add_fusion
  17.3 0.7 select_bitcast_fusion
  18.1 0.9 %collective-permute-start.6 = (f32[2,2,32,512]{3,2,1,0:T(8,128)}, f32[2,2,32,512]{3,2,1,0:T(8,128)}, u32[]{:S(2)}, u32[]{:S(2)}) collective-permute-start(f32[2,2,32,512]{3,2,1,0:T(8,128)} %select_bitcast_fusion), channel_id=1, source_target_pairs={{0,4},{4,0},{8,12},{12,8},{16,20},{20,16},{24,28},{28,24},{1,5},{5... | collective-permute-start | bytes 786440 | tf_op jit(solution)/shard_map/ppermute | solution.py:344
  19.0 1.1 %shard_map.103 = bf16[512,512]{1,0:T(8,128)(2,1)S(1)} custom-call(bf16[2048,512]{1,0:T(8,128)(2,1)} %bitcast.67), custom_call_target="tpu_custom_call" | custom-call | tf_op jit(solution)/shard_map/pallas_call | solution.py:64
  20.1 1.2 %collective-permute-start.1 = (bf16[512,512]{1,0:T(8,128)(2,1)S(1)}, bf16[512,512]{1,0:T(8,128)(2,1)S(1)}, u32[]{:S(2)}, u32[]{:S(2)}) collective-permute-start(bf16[512,512]{1,0:T(8,128)(2,1)S(1)} %shard_map.103), channel_id=1, source_target_pairs={{0,28},{4,8},{8,4},{12,16},{16,12},{20,24},{24,20},{28,0},{1,29},{... | collective-permute-start | bytes 1572872 | tf_op jit(solution)/shard_map/ppermute | solution.py:387
  21.2 0.7 collective-permute-start.10
  21.9 1.1 %collective-permute-start.2 = (bf16[1024,512]{1,0:T(8,128)(2,1)S(1)}, bf16[1024,512]{1,0:T(8,128)(2,1)}, u32[]{:S(2)}, u32[]{:S(2)}) collective-permute-start(bf16[1024,512]{1,0:T(8,128)(2,1)S(1)} %get-tuple-element.19), channel_id=1, source_target_pairs={{0,28},{4,8},{8,4},{12,16},{16,12},{20,24},{24,20},{28,0},{1,29},{... | collective-permute-start | bytes 3145736 | tf_op jit(solution)/shard_map/ppermute | solution.py:387
  23.6 5.8 %shard_map.100.rest_0_ = f32[2048,512]{1,0:T(8,128)} custom-call(bf16[2048,2048]{1,0:T(8,128)(2,1)} %bitcast.70, bf16[2048,512]{1,0:T(8,128)(2,1)} %bitcast.68), custom_call_target="tpu_custom_call" | custom-call | flops 2147483648 | bytes 8388608 | tf_op jit(solution)/shard_map/pallas_call | solution.py:91
  29.4 1.0 %bitcast_add_fusion = f32[2,2,32,512]{3,2,1,0:T(8,128)S(1)} fusion(f32[2,2,32,512]{3,2,1,0:T(8,128)} %collective-permute-done.6, f32[2,2,2,32,512]{4,3,2,1,0:T(8,128)S(1)} %bitcast.74, pred[]{:T(512)S(6)} %eq.41), kind=kLoop, calls=%fused_computation.13 | loop fusion | flops 131072 | bytes 1048577 | tf_op jit(solution)/shard_map/add | solution.py:346
  30.4 1.3 %collective-permute-start.7 = (f32[2,32,512]{2,1,0:T(8,128)S(1)}, f32[2,32,512]{2,1,0:T(8,128)S(1)}, u32[]{:S(2)}, u32[]{:S(2)}) collective-permute-start(f32[2,32,512]{2,1,0:T(8,128)S(1)} %select_bitcast_fusion.1), channel_id=1, source_target_pairs={{0,16},{4,20},{8,24},{12,28},{16,0},{20,4},{24,8},{28,12},{1,17},{... | collective-permute-start | bytes 393224 | tf_op jit(solution)/shard_map/ppermute | solution.py:344
  31.7 5.8 %shard_map.101.total_ref = f32[2048,512]{1,0:T(8,128)} custom-call(bf16[2048,2048]{1,0:T(8,128)(2,1)} %bitcast.71, bf16[2048,512]{1,0:T(8,128)(2,1)} %bitcast.69, f32[2048,512]{1,0:T(8,128)} %shard_map.100.rest_0_), custom_call_target="tpu_custom_call", output_to_operand_aliasing={{}: (2, {})} | custom-call | flops 2147483648 | bytes 8388608 | tf_op jit(solution)/shard_map/pallas_call | solution.py:91
  37.6 2.6 %collective-permute-start.8 = (bf16[32,512]{1,0:T(8,128)(2,1)S(1)}, bf16[32,512]{1,0:T(8,128)(2,1)S(1)}, u32[]{:S(2)}, u32[]{:S(2)}) collective-permute-start(bf16[32,512]{1,0:T(8,128)(2,1)S(1)} %fusion.26), channel_id=1, source_target_pairs={{0,8},{4,12},{8,0},{12,4},{16,24},{20,28},{24,16},{28,20},{1,9},{5... | collective-permute-start | bytes 98312 | tf_op jit(solution)/shard_map/ppermute | solution.py:344
  40.2 0.9 %collective-permute-start.9 = (bf16[512,128]{1,0:T(8,128)(2,1)S(1)}, bf16[512,128]{1,0:T(8,128)(2,1)S(1)}, u32[]{:S(2)}, u32[]{:S(2)}) collective-permute-start(bf16[512,128]{1,0:T(8,128)(2,1)S(1)} %get-tuple-element.22), channel_id=1, source_target_pairs={{0,28},{4,8},{8,4},{12,16},{16,12},{20,24},{24,20},{28,0},{1,29},{... | collective-permute-start | bytes 393224 | tf_op jit(solution)/shard_map/ppermute | solution.py:387
  41.1 4.7 %shard_map.102 = (bf16[1536,2048]{1,0:T(8,128)(2,1)S(1)}, bf16[2048,512]{1,0:T(8,128)(2,1)S(1)}, bf16[2048,512]{1,0:T(8,128)(2,1)S(1)}, f32[2048,512]{1,0:T(8,128)S(1)}) custom-call(s32[1]{0:T(128)} %bitcast.1.which_ref, bf16[2048,2048]{1,0:T(8,128)(2,1)} %bitcast.72, bf16[2048,512]{1,0:T(8,128)(2,1)} %collective-permute-done.near_ref, ...), custom_call_target="tpu_custom_call" | custom-call | tf_op jit(solution)/shard_map/pallas_call | solution.py:141
  45.8 20.7 %collective-permute-done.8.rest_4_ = bf16[32,512]{1,0:T(8,128)(2,1)S(1)} collective-permute-done((bf16[32,512]{1,0:T(8,128)(2,1)S(1)}, bf16[32,512]{1,0:T(8,128)(2,1)S(1)}, u32[]{:S(2)}, u32[]{:S(2)}) %collective-permute-start.8) | collective-permute-done | bytes 32800 | tf_op jit(solution)/shard_map/ppermute | solution.py:344
  66.5 6.9 %shard_map.105 = (f32[2048,512]{1,0:T(8,128)S(1)}, f32[2048,512]{1,0:T(8,128)}) custom-call(s32[1]{0:T(128)} %bitcast.1.which_ref, f32[2048,512]{1,0:T(8,128)S(1)} %get-tuple-element.15.total_ref, bf16[1536,2048]{1,0:T(8,128)(2,1)S(1)} %get-tuple-element.16.tile_ref, ...), custom_call_target="tpu_custom_call", output_to_operand_aliasing={{0}: (1, {})} | custom-call | flops 3221225472 | bytes 1572864 | tf_op jit(solution)/shard_map/pallas_call | solution.py:225
  73.5 2.1 %shard_map.106.rest_0_ = f32[2048,512]{1,0:T(8,128)} custom-call(s32[1]{0:T(128)} %bitcast.1.which_ref, f32[2048,512]{1,0:T(8,128)S(1)} %get-tuple-element.21.total_ref, bf16[2048,512]{1,0:T(8,128)(2,1)S(1)} %get-tuple-element.17.flipped_ref, bf16[512,384]{1,0:T(8,128)(2,1)S(1)} %collective-permute-done.10.far_ref, ...), custom_call_target="tpu_custom_call", output_to_operand_aliasing={{}: (4, {})} | custom-call | flops 805306368 | bytes 8388608 | tf_op jit(solution)/shard_map/pallas_call | solution.py:279
  75.5 1.4 %shard_map.107 = f32[2048,512]{1,0:T(8,128)} custom-call(s32[1]{0:T(128)} %bitcast.1.which_ref, f32[2048,512]{1,0:T(8,128)S(1)} %get-tuple-element.21.total_ref, bf16[2048,512]{1,0:T(8,128)(2,1)S(1)} %get-tuple-element.17.flipped_ref, bf16[512,128]{1,0:T(8,128)(2,1)S(1)} %collective-permute-done.9.far_ref, ...), custom_call_target="tpu_custom_call", output_to_operand_aliasing={{}: (4, {})} | custom-call | flops 268435456 | bytes 4194304 | tf_op jit(solution)/shard_map/pallas_call | solution.py:279
  (21 shorter events, 0.5 us)
Async XLA Ops:
  7.3 7.1 %collective-permute-start.3 = (bf16[32,1024]{1,0:T(8,128)(2,1)S(1)}, bf16[32,1024]{1,0:T(8,128)(2,1)S(1)}, u32[]{:S(2)}, u32[]{:S(2)}) collective-permute-start(bf16[32,1024]{1,0:T(8,128)(2,1)S(1)} %get-tuple-element.26), channel_id=1, source_target_pairs={{0,1},{1,2},{2,3},{3,0},{4,5},{5,6},{6,7},{7,4},{8,9},{9,10},{10,1... | collective-permute-start | bytes 196616 | tf_op jit(solution)/shard_map/ppermute | solution.py:324
  9.4 7.3 %collective-permute-start.4 = (bf16[32,1024]{1,0:T(8,128)(2,1)S(1)}, bf16[32,1024]{1,0:T(8,128)(2,1)S(1)}, u32[]{:S(2)}, u32[]{:S(2)}) collective-permute-start(bf16[32,1024]{1,0:T(8,128)(2,1)S(1)} %get-tuple-element.27), channel_id=1, source_target_pairs={{0,2},{1,3},{2,0},{3,1},{4,6},{5,7},{6,4},{7,5},{8,10},{9,11},{10,... | collective-permute-start | bytes 196616 | tf_op jit(solution)/shard_map/ppermute | solution.py:324
  11.8 5.0 %collective-permute-start.5 = (bf16[32,1024]{1,0:T(8,128)(2,1)S(1)}, bf16[32,1024]{1,0:T(8,128)(2,1)S(1)}, u32[]{:S(2)}, u32[]{:S(2)}) collective-permute-start(bf16[32,1024]{1,0:T(8,128)(2,1)S(1)} %get-tuple-element.28), channel_id=1, source_target_pairs={{0,3},{1,0},{2,1},{3,2},{4,7},{5,4},{6,5},{7,6},{8,11},{9,8},{10,9... | collective-permute-start | bytes 196616 | tf_op jit(solution)/shard_map/ppermute | solution.py:324
  12.8 27.4 %collective-permute-start = (bf16[2048,512]{1,0:T(8,128)(2,1)}, bf16[2048,512]{1,0:T(8,128)(2,1)}, u32[]{:S(2)}, u32[]{:S(2)}) collective-permute-start(bf16[2048,512]{1,0:T(8,128)(2,1)} %bitcast.66), channel_id=1, source_target_pairs={{0,4},{4,0},{8,12},{12,8},{16,20},{20,16},{24,28},{28,24},{1,5},{5... | collective-permute-start | bytes 6291464 | tf_op jit(solution)/shard_map/ppermute | solution.py:388
  18.1 11.3 %collective-permute-start.6 = (f32[2,2,32,512]{3,2,1,0:T(8,128)}, f32[2,2,32,512]{3,2,1,0:T(8,128)}, u32[]{:S(2)}, u32[]{:S(2)}) collective-permute-start(f32[2,2,32,512]{3,2,1,0:T(8,128)} %select_bitcast_fusion), channel_id=1, source_target_pairs={{0,4},{4,0},{8,12},{12,8},{16,20},{20,16},{24,28},{28,24},{1,5},{5... | collective-permute-start | bytes 786440 | tf_op jit(solution)/shard_map/ppermute | solution.py:344
  20.1 46.4 %collective-permute-start.1 = (bf16[512,512]{1,0:T(8,128)(2,1)S(1)}, bf16[512,512]{1,0:T(8,128)(2,1)S(1)}, u32[]{:S(2)}, u32[]{:S(2)}) collective-permute-start(bf16[512,512]{1,0:T(8,128)(2,1)S(1)} %shard_map.103), channel_id=1, source_target_pairs={{0,28},{4,8},{8,4},{12,16},{16,12},{20,24},{24,20},{28,0},{1,29},{... | collective-permute-start | bytes 1572872 | tf_op jit(solution)/shard_map/ppermute | solution.py:387
  21.2 52.2 %collective-permute-start.10 = (bf16[512,384]{1,0:T(8,128)(2,1)S(1)}, bf16[512,384]{1,0:T(8,128)(2,1)S(1)}, u32[]{:S(2)}, u32[]{:S(2)}) collective-permute-start(bf16[512,384]{1,0:T(8,128)(2,1)S(1)} %get-tuple-element.23), channel_id=1, source_target_pairs={{0,28},{4,8},{8,4},{12,16},{16,12},{20,24},{24,20},{28,0},{1,29},{... | collective-permute-start | bytes 1179656 | tf_op jit(solution)/shard_map/ppermute | solution.py:387
  21.9 44.6 %collective-permute-start.2 = (bf16[1024,512]{1,0:T(8,128)(2,1)S(1)}, bf16[1024,512]{1,0:T(8,128)(2,1)}, u32[]{:S(2)}, u32[]{:S(2)}) collective-permute-start(bf16[1024,512]{1,0:T(8,128)(2,1)S(1)} %get-tuple-element.19), channel_id=1, source_target_pairs={{0,28},{4,8},{8,4},{12,16},{16,12},{20,24},{24,20},{28,0},{1,29},{... | collective-permute-start | bytes 3145736 | tf_op jit(solution)/shard_map/ppermute | solution.py:387
  30.4 7.1 %collective-permute-start.7 = (f32[2,32,512]{2,1,0:T(8,128)S(1)}, f32[2,32,512]{2,1,0:T(8,128)S(1)}, u32[]{:S(2)}, u32[]{:S(2)}) collective-permute-start(f32[2,32,512]{2,1,0:T(8,128)S(1)} %select_bitcast_fusion.1), channel_id=1, source_target_pairs={{0,16},{4,20},{8,24},{12,28},{16,0},{20,4},{24,8},{28,12},{1,17},{... | collective-permute-start | bytes 393224 | tf_op jit(solution)/shard_map/ppermute | solution.py:344
  37.6 28.9 %collective-permute-start.8 = (bf16[32,512]{1,0:T(8,128)(2,1)S(1)}, bf16[32,512]{1,0:T(8,128)(2,1)S(1)}, u32[]{:S(2)}, u32[]{:S(2)}) collective-permute-start(bf16[32,512]{1,0:T(8,128)(2,1)S(1)} %fusion.26), channel_id=1, source_target_pairs={{0,8},{4,12},{8,0},{12,4},{16,24},{20,28},{24,16},{28,20},{1,9},{5... | collective-permute-start | bytes 98312 | tf_op jit(solution)/shard_map/ppermute | solution.py:344
  40.2 35.3 %collective-permute-start.9 = (bf16[512,128]{1,0:T(8,128)(2,1)S(1)}, bf16[512,128]{1,0:T(8,128)(2,1)S(1)}, u32[]{:S(2)}, u32[]{:S(2)}) collective-permute-start(bf16[512,128]{1,0:T(8,128)(2,1)S(1)} %get-tuple-element.22), channel_id=1, source_target_pairs={{0,28},{4,8},{8,4},{12,16},{16,12},{20,24},{24,20},{28,0},{1,29},{... | collective-permute-start | bytes 393224 | tf_op jit(solution)/shard_map/ppermute | solution.py:387
  41.1 25.4 %copy-start = (bf16[1,1,2048,32]{2,3,1,0:T(8,128)(2,1)S(1)}, bf16[1,1,2048,32]{2,3,1,0:T(8,128)(2,1)}, u32[]{:S(2)}) copy-start(bf16[1,1,2048,32]{2,3,1,0:T(8,128)(2,1)} %param.14) | copy-start | bytes 393220

commit v7 on v6

--- a/solution.py
+++ b/solution.py
@@ -186,18 +186,24 @@
             fetch()
 
         dual = (kept_ref[...] + incoming_ref[...].astype(jnp.float32)).astype(jnp.bfloat16)
-        out_ref[here, :] = total_ref[here, :] + contract(basis_ref[:, here], dual)
+
+        def base():
+            return total_ref[here, :] + contract(basis_ref[:, here], dual)
 
         @pl.when(which_ref[0] == 2)
         def _():
-            out_ref[here, :] += contract(tile_ref[:, here], values_ref[...])
+            out_ref[here, :] = base() + contract(tile_ref[:, here], values_ref[...])
 
         @pl.when(which_ref[0] == 1)
         def _():
-            result = contract(tile_ref[:, here], near_ref[:size, :])
-            out_ref[here, :] += result + jnp.dot(
+            result = base() + contract(tile_ref[:, here], near_ref[:size, :])
+            out_ref[here, :] = result + jnp.dot(
                 flipped_ref[here, :], near_ref[size:, :], preferred_element_type=jnp.float32
             )
+
+        @pl.when(which_ref[0] == 0)
+        def _():
+            out_ref[here, :] = base()
 
         def finished(step):
             rows = pl.ds(step * block, block)

time: 77.3 us -> 76.5 us (0.990)
  Pallas kernels: 30.3 us -> 29.5 us
    pallas_call x1, Pallas kernels: 6.92 us -> 6.12 us  [add_rows(): pl.pallas_call(kernel, grid=(steps,), in_specs=in_specs, out_specs=[whole...]
  transfers between devices with their start and end apart: 11 -> 11, of which waited for: 2 -> 2; matrix products, arithmetic and copies ran while one was open for 3% -> 3% of each run, Pallas kernels for 34% -> 33%
where the time goes in v7:
time: 76.5 us; the launch traced here: 76.2 us
  Pallas kernels  29.5 us (39%)
  waiting for transfers between devices  23.2 us (30%)
  starting transfers between devices  15.7 us (21%)
  other arithmetic  3.64 us (5%)
  between operations  1.53 us (2%)
  matrix products  1.44 us (2%)
  local copies, waits for them, and re-layouts  1.18 us (2%)
    ppermute x3, waiting for transfers between devices, dual_of(): lax.ppermute(outgoing, 'row', [(i, i ^ 1 << bit) for i in range(rows)])  20.7 us
    pallas_call x2, Pallas kernels, own_product(): pl.pallas_call(kernel, grid=(steps,), in_specs=in_specs, out_specs=pl.Blo...  11.6 us
    pallas_call x1, Pallas kernels, add_rows(): pl.pallas_call(kernel, grid=(steps,), in_specs=in_specs, out_specs=[whole...  6.12 us
    ppermute x3, starting transfers between devices, dual_of(): lax.ppermute(outgoing, 'col', [(i, (i + shift) % cols) for i in range(col...  5.54 us
    ppermute x3, starting transfers between devices, dual_of(): lax.ppermute(outgoing, 'row', [(i, i ^ 1 << bit) for i in range(rows)])  4.84 us
    pallas_call x1, Pallas kernels, stage(): pl.pallas_call(kernel, in_specs=[pl.BlockSpec(memory_space=pltpu.SMEM)] +...  4.68 us
    ppermute x4, starting transfers between devices, on_device(): far.append(lax.ppermute(piece, 'row', far_pairs))  3.77 us
    pallas_call x2, Pallas kernels, split(): pl.pallas_call(kernel, in_specs=[pl.BlockSpec(memory_space=pltpu.HBM) for...  3.66 us
  transfers between devices with their start and end apart: 11, of which 2 were waited for; matrix products, arithmetic and copies ran while one was open for 3% of the time, Pallas kernels for 33%

profile of v7, /device:TPU:1, one launch (start us, length us, event | category | flops | bytes accessed | tf_op | source)
XLA Modules:
  0.0 76.2 jit_solution(1158494022208565528)
XLA Ops:
  0.7 0.7 fusion.32
  1.3 1.0 %bitcast_multiply_fusion = bf16[64,1024]{0,1:T(8,128)(2,1)S(1)} fusion(bf16[1,1,64,32,32]{2,4,3,1,0:T(8,128)(2,1)} %param.15, bf16[64,32]{0,1:T(8,128)(2,1)S(1)} %fusion.32), kind=kLoop, calls=%fused_computation.14 | loop fusion | flops 131072 | bytes 266240 | tf_op jit(solution)/shard_map/mul | solution.py:310
  2.3 0.9 %reduce-precision_convert_fusion = (bf16[32,1024]{1,0:T(8,128)(2,1)S(1)}, bf16[32,1024]{1,0:T(8,128)(2,1)S(1)}) fusion(bf16[64,1024]{0,1:T(8,128)(2,1)S(1)} %bitcast_multiply_fusion, s32[64]{0:T(128)} %bitcast.76), kind=kOutput, calls=%fused_computation.18 | convolution fusion | flops 4329472 | bytes 262400 | tf_op jit(solution)/shard_map/dot_general | solution.py:13
  3.3 0.2 stack.9
  3.5 0.2 copy.15
  3.6 0.2 stack.10
  4.1 0.4 reshape.110
  4.6 2.6 %shard_map.104 = (bf16[1024,512]{1,0:T(8,128)(2,1)S(1)}, bf16[512,384]{1,0:T(8,128)(2,1)S(1)}, bf16[512,128]{1,0:T(8,128)(2,1)S(1)}, bf16[32,512]{1,0:T(8,128)(2,1)S(1)}) custom-call(bf16[2048,512]{1,0:T(8,128)(2,1)} %bitcast.65, bf16[32,2048]{1,0:T(8,128)(2,1)} %bitcast.75), custom_call_target="tpu_custom_call" | custom-call | tf_op jit(solution)/shard_map/pallas_call | solution.py:64
  7.3 2.2 %collective-permute-start.3 = (bf16[32,1024]{1,0:T(8,128)(2,1)S(1)}, bf16[32,1024]{1,0:T(8,128)(2,1)S(1)}, u32[]{:S(2)}, u32[]{:S(2)}) collective-permute-start(bf16[32,1024]{1,0:T(8,128)(2,1)S(1)} %get-tuple-element.26), channel_id=1, source_target_pairs={{0,1},{1,2},{2,3},{3,0},{4,5},{5,6},{6,7},{7,4},{8,9},{9,10},{10,1... | collective-permute-start | bytes 196616 | tf_op jit(solution)/shard_map/ppermute | solution.py:330
  9.4 2.3 %collective-permute-start.4 = (bf16[32,1024]{1,0:T(8,128)(2,1)S(1)}, bf16[32,1024]{1,0:T(8,128)(2,1)S(1)}, u32[]{:S(2)}, u32[]{:S(2)}) collective-permute-start(bf16[32,1024]{1,0:T(8,128)(2,1)S(1)} %get-tuple-element.27), channel_id=1, source_target_pairs={{0,2},{1,3},{2,0},{3,1},{4,6},{5,7},{6,4},{7,5},{8,10},{9,11},{10,... | collective-permute-start | bytes 196616 | tf_op jit(solution)/shard_map/ppermute | solution.py:330
  11.8 1.1 %collective-permute-start.5 = (bf16[32,1024]{1,0:T(8,128)(2,1)S(1)}, bf16[32,1024]{1,0:T(8,128)(2,1)S(1)}, u32[]{:S(2)}, u32[]{:S(2)}) collective-permute-start(bf16[32,1024]{1,0:T(8,128)(2,1)S(1)} %get-tuple-element.28), channel_id=1, source_target_pairs={{0,3},{1,0},{2,1},{3,2},{4,7},{5,4},{6,5},{7,6},{8,11},{9,8},{10,9... | collective-permute-start | bytes 196616 | tf_op jit(solution)/shard_map/ppermute | solution.py:330
  12.8 1.5 %collective-permute-start = (bf16[2048,512]{1,0:T(8,128)(2,1)}, bf16[2048,512]{1,0:T(8,128)(2,1)}, u32[]{:S(2)}, u32[]{:S(2)}) collective-permute-start(bf16[2048,512]{1,0:T(8,128)(2,1)} %bitcast.66), channel_id=1, source_target_pairs={{0,4},{4,0},{8,12},{12,8},{16,20},{20,16},{24,28},{28,24},{1,5},{5... | collective-permute-start | bytes 6291464 | tf_op jit(solution)/shard_map/ppermute | solution.py:394
  14.3 2.4 %collective-permute-done.4 = bf16[32,1024]{1,0:T(8,128)(2,1)S(1)} collective-permute-done((bf16[32,1024]{1,0:T(8,128)(2,1)S(1)}, bf16[32,1024]{1,0:T(8,128)(2,1)S(1)}, u32[]{:S(2)}, u32[]{:S(2)}) %collective-permute-start.4) | collective-permute-done | bytes 65568 | tf_op jit(solution)/shard_map/ppermute | solution.py:330
  16.8 0.2 fusion.1
  17.1 0.3 convolution_add_fusion
  17.3 0.7 select_bitcast_fusion
  18.1 0.9 %collective-permute-start.6 = (f32[2,2,32,512]{3,2,1,0:T(8,128)}, f32[2,2,32,512]{3,2,1,0:T(8,128)}, u32[]{:S(2)}, u32[]{:S(2)}) collective-permute-start(f32[2,2,32,512]{3,2,1,0:T(8,128)} %select_bitcast_fusion), channel_id=1, source_target_pairs={{0,4},{4,0},{8,12},{12,8},{16,20},{20,16},{24,28},{28,24},{1,5},{5... | collective-permute-start | bytes 786440 | tf_op jit(solution)/shard_map/ppermute | solution.py:350
  19.0 1.1 %shard_map.103 = bf16[512,512]{1,0:T(8,128)(2,1)S(1)} custom-call(bf16[2048,512]{1,0:T(8,128)(2,1)} %bitcast.67), custom_call_target="tpu_custom_call" | custom-call | tf_op jit(solution)/shard_map/pallas_call | solution.py:64
  20.1 1.2 %collective-permute-start.1 = (bf16[512,512]{1,0:T(8,128)(2,1)S(1)}, bf16[512,512]{1,0:T(8,128)(2,1)S(1)}, u32[]{:S(2)}, u32[]{:S(2)}) collective-permute-start(bf16[512,512]{1,0:T(8,128)(2,1)S(1)} %shard_map.103), channel_id=1, source_target_pairs={{0,28},{4,8},{8,4},{12,16},{16,12},{20,24},{24,20},{28,0},{1,29},{... | collective-permute-start | bytes 1572872 | tf_op jit(solution)/shard_map/ppermute | solution.py:393
  21.2 0.7 collective-permute-start.10
  21.9 1.1 %collective-permute-start.2 = (bf16[1024,512]{1,0:T(8,128)(2,1)S(1)}, bf16[1024,512]{1,0:T(8,128)(2,1)}, u32[]{:S(2)}, u32[]{:S(2)}) collective-permute-start(bf16[1024,512]{1,0:T(8,128)(2,1)S(1)} %get-tuple-element.19), channel_id=1, source_target_pairs={{0,28},{4,8},{8,4},{12,16},{16,12},{20,24},{24,20},{28,0},{1,29},{... | collective-permute-start | bytes 3145736 | tf_op jit(solution)/shard_map/ppermute | solution.py:393
  23.6 5.8 %shard_map.100.rest_0_ = f32[2048,512]{1,0:T(8,128)} custom-call(bf16[2048,2048]{1,0:T(8,128)(2,1)} %bitcast.70, bf16[2048,512]{1,0:T(8,128)(2,1)} %bitcast.68), custom_call_target="tpu_custom_call" | custom-call | flops 2147483648 | bytes 8388608 | tf_op jit(solution)/shard_map/pallas_call | solution.py:91
  29.4 1.0 %bitcast_add_fusion = f32[2,2,32,512]{3,2,1,0:T(8,128)S(1)} fusion(f32[2,2,32,512]{3,2,1,0:T(8,128)} %collective-permute-done.6, f32[2,2,2,32,512]{4,3,2,1,0:T(8,128)S(1)} %bitcast.74, pred[]{:T(512)S(6)} %eq.41), kind=kLoop, calls=%fused_computation.13 | loop fusion | flops 131072 | bytes 1048577 | tf_op jit(solution)/shard_map/add | solution.py:352
  30.4 1.3 %collective-permute-start.7 = (f32[2,32,512]{2,1,0:T(8,128)S(1)}, f32[2,32,512]{2,1,0:T(8,128)S(1)}, u32[]{:S(2)}, u32[]{:S(2)}) collective-permute-start(f32[2,32,512]{2,1,0:T(8,128)S(1)} %select_bitcast_fusion.1), channel_id=1, source_target_pairs={{0,16},{4,20},{8,24},{12,28},{16,0},{20,4},{24,8},{28,12},{1,17},{... | collective-permute-start | bytes 393224 | tf_op jit(solution)/shard_map/ppermute | solution.py:350
  31.7 5.8 %shard_map.101.total_ref = f32[2048,512]{1,0:T(8,128)} custom-call(bf16[2048,2048]{1,0:T(8,128)(2,1)} %bitcast.71, bf16[2048,512]{1,0:T(8,128)(2,1)} %bitcast.69, f32[2048,512]{1,0:T(8,128)} %shard_map.100.rest_0_), custom_call_target="tpu_custom_call", output_to_operand_aliasing={{}: (2, {})} | custom-call | flops 2147483648 | bytes 8388608 | tf_op jit(solution)/shard_map/pallas_call | solution.py:91
  37.6 2.6 %collective-permute-start.8 = (bf16[32,512]{1,0:T(8,128)(2,1)S(1)}, bf16[32,512]{1,0:T(8,128)(2,1)S(1)}, u32[]{:S(2)}, u32[]{:S(2)}) collective-permute-start(bf16[32,512]{1,0:T(8,128)(2,1)S(1)} %fusion.26), channel_id=1, source_target_pairs={{0,8},{4,12},{8,0},{12,4},{16,24},{20,28},{24,16},{28,20},{1,9},{5... | collective-permute-start | bytes 98312 | tf_op jit(solution)/shard_map/ppermute | solution.py:350
  40.2 0.9 %collective-permute-start.9 = (bf16[512,128]{1,0:T(8,128)(2,1)S(1)}, bf16[512,128]{1,0:T(8,128)(2,1)S(1)}, u32[]{:S(2)}, u32[]{:S(2)}) collective-permute-start(bf16[512,128]{1,0:T(8,128)(2,1)S(1)} %get-tuple-element.22), channel_id=1, source_target_pairs={{0,28},{4,8},{8,4},{12,16},{16,12},{20,24},{24,20},{28,0},{1,29},{... | collective-permute-start | bytes 393224 | tf_op jit(solution)/shard_map/ppermute | solution.py:393
  41.1 4.7 %shard_map.102 = (bf16[1536,2048]{1,0:T(8,128)(2,1)S(1)}, bf16[2048,512]{1,0:T(8,128)(2,1)S(1)}, bf16[2048,512]{1,0:T(8,128)(2,1)S(1)}, f32[2048,512]{1,0:T(8,128)S(1)}) custom-call(s32[1]{0:T(128)} %bitcast.1.which_ref, bf16[2048,2048]{1,0:T(8,128)(2,1)} %bitcast.72, bf16[2048,512]{1,0:T(8,128)(2,1)} %collective-permute-done.near_ref, ...), custom_call_target="tpu_custom_call" | custom-call | tf_op jit(solution)/shard_map/pallas_call | solution.py:141
  45.8 20.7 %collective-permute-done.8.rest_4_ = bf16[32,512]{1,0:T(8,128)(2,1)S(1)} collective-permute-done((bf16[32,512]{1,0:T(8,128)(2,1)S(1)}, bf16[32,512]{1,0:T(8,128)(2,1)S(1)}, u32[]{:S(2)}, u32[]{:S(2)}) %collective-permute-start.8) | collective-permute-done | bytes 32800 | tf_op jit(solution)/shard_map/ppermute | solution.py:350
  66.5 6.1 %shard_map.105 = (f32[2048,512]{1,0:T(8,128)S(1)}, f32[2048,512]{1,0:T(8,128)}) custom-call(s32[1]{0:T(128)} %bitcast.1.which_ref, f32[2048,512]{1,0:T(8,128)S(1)} %get-tuple-element.15.total_ref, bf16[1536,2048]{1,0:T(8,128)(2,1)S(1)} %get-tuple-element.16.tile_ref, ...), custom_call_target="tpu_custom_call", output_to_operand_aliasing={{0}: (1, {})} | custom-call | flops 3221225472 | bytes 1572864 | tf_op jit(solution)/shard_map/pallas_call | solution.py:231
  72.6 2.1 %shard_map.106.rest_0_ = f32[2048,512]{1,0:T(8,128)} custom-call(s32[1]{0:T(128)} %bitcast.1.which_ref, f32[2048,512]{1,0:T(8,128)S(1)} %get-tuple-element.21.total_ref, bf16[2048,512]{1,0:T(8,128)(2,1)S(1)} %get-tuple-element.17.flipped_ref, bf16[512,384]{1,0:T(8,128)(2,1)S(1)} %collective-permute-done.10.far_ref, ...), custom_call_target="tpu_custom_call", output_to_operand_aliasing={{}: (4, {})} | custom-call | flops 805306368 | bytes 8388608 | tf_op jit(solution)/shard_map/pallas_call | solution.py:285
  74.7 1.4 %shard_map.107 = f32[2048,512]{1,0:T(8,128)} custom-call(s32[1]{0:T(128)} %bitcast.1.which_ref, f32[2048,512]{1,0:T(8,128)S(1)} %get-tuple-element.21.total_ref, bf16[2048,512]{1,0:T(8,128)(2,1)S(1)} %get-tuple-element.17.flipped_ref, bf16[512,128]{1,0:T(8,128)(2,1)S(1)} %collective-permute-done.9.far_ref, ...), custom_call_target="tpu_custom_call", output_to_operand_aliasing={{}: (4, {})} | custom-call | flops 268435456 | bytes 4194304 | tf_op jit(solution)/shard_map/pallas_call | solution.py:285
  (21 shorter events, 0.5 us)
Async XLA Ops:
  7.3 7.1 %collective-permute-start.3 = (bf16[32,1024]{1,0:T(8,128)(2,1)S(1)}, bf16[32,1024]{1,0:T(8,128)(2,1)S(1)}, u32[]{:S(2)}, u32[]{:S(2)}) collective-permute-start(bf16[32,1024]{1,0:T(8,128)(2,1)S(1)} %get-tuple-element.26), channel_id=1, source_target_pairs={{0,1},{1,2},{2,3},{3,0},{4,5},{5,6},{6,7},{7,4},{8,9},{9,10},{10,1... | collective-permute-start | bytes 196616 | tf_op jit(solution)/shard_map/ppermute | solution.py:330
  9.4 7.3 %collective-permute-start.4 = (bf16[32,1024]{1,0:T(8,128)(2,1)S(1)}, bf16[32,1024]{1,0:T(8,128)(2,1)S(1)}, u32[]{:S(2)}, u32[]{:S(2)}) collective-permute-start(bf16[32,1024]{1,0:T(8,128)(2,1)S(1)} %get-tuple-element.27), channel_id=1, source_target_pairs={{0,2},{1,3},{2,0},{3,1},{4,6},{5,7},{6,4},{7,5},{8,10},{9,11},{10,... | collective-permute-start | bytes 196616 | tf_op jit(solution)/shard_map/ppermute | solution.py:330
  11.8 5.0 %collective-permute-start.5 = (bf16[32,1024]{1,0:T(8,128)(2,1)S(1)}, bf16[32,1024]{1,0:T(8,128)(2,1)S(1)}, u32[]{:S(2)}, u32[]{:S(2)}) collective-permute-start(bf16[32,1024]{1,0:T(8,128)(2,1)S(1)} %get-tuple-element.28), channel_id=1, source_target_pairs={{0,3},{1,0},{2,1},{3,2},{4,7},{5,4},{6,5},{7,6},{8,11},{9,8},{10,9... | collective-permute-start | bytes 196616 | tf_op jit(solution)/shard_map/ppermute | solution.py:330
  12.8 27.4 %collective-permute-start = (bf16[2048,512]{1,0:T(8,128)(2,1)}, bf16[2048,512]{1,0:T(8,128)(2,1)}, u32[]{:S(2)}, u32[]{:S(2)}) collective-permute-start(bf16[2048,512]{1,0:T(8,128)(2,1)} %bitcast.66), channel_id=1, source_target_pairs={{0,4},{4,0},{8,12},{12,8},{16,20},{20,16},{24,28},{28,24},{1,5},{5... | collective-permute-start | bytes 6291464 | tf_op jit(solution)/shard_map/ppermute | solution.py:394
  18.1 11.3 %collective-permute-start.6 = (f32[2,2,32,512]{3,2,1,0:T(8,128)}, f32[2,2,32,512]{3,2,1,0:T(8,128)}, u32[]{:S(2)}, u32[]{:S(2)}) collective-permute-start(f32[2,2,32,512]{3,2,1,0:T(8,128)} %select_bitcast_fusion), channel_id=1, source_target_pairs={{0,4},{4,0},{8,12},{12,8},{16,20},{20,16},{24,28},{28,24},{1,5},{5... | collective-permute-start | bytes 786440 | tf_op jit(solution)/shard_map/ppermute | solution.py:350
  20.1 46.4 %collective-permute-start.1 = (bf16[512,512]{1,0:T(8,128)(2,1)S(1)}, bf16[512,512]{1,0:T(8,128)(2,1)S(1)}, u32[]{:S(2)}, u32[]{:S(2)}) collective-permute-start(bf16[512,512]{1,0:T(8,128)(2,1)S(1)} %shard_map.103), channel_id=1, source_target_pairs={{0,28},{4,8},{8,4},{12,16},{16,12},{20,24},{24,20},{28,0},{1,29},{... | collective-permute-start | bytes 1572872 | tf_op jit(solution)/shard_map/ppermute | solution.py:393
  21.2 51.4 %collective-permute-start.10 = (bf16[512,384]{1,0:T(8,128)(2,1)S(1)}, bf16[512,384]{1,0:T(8,128)(2,1)S(1)}, u32[]{:S(2)}, u32[]{:S(2)}) collective-permute-start(bf16[512,384]{1,0:T(8,128)(2,1)S(1)} %get-tuple-element.23), channel_id=1, source_target_pairs={{0,28},{4,8},{8,4},{12,16},{16,12},{20,24},{24,20},{28,0},{1,29},{... | collective-permute-start | bytes 1179656 | tf_op jit(solution)/shard_map/ppermute | solution.py:393
  21.9 44.6 %collective-permute-start.2 = (bf16[1024,512]{1,0:T(8,128)(2,1)S(1)}, bf16[1024,512]{1,0:T(8,128)(2,1)}, u32[]{:S(2)}, u32[]{:S(2)}) collective-permute-start(bf16[1024,512]{1,0:T(8,128)(2,1)S(1)} %get-tuple-element.19), channel_id=1, source_target_pairs={{0,28},{4,8},{8,4},{12,16},{16,12},{20,24},{24,20},{28,0},{1,29},{... | collective-permute-start | bytes 3145736 | tf_op jit(solution)/shard_map/ppermute | solution.py:393
  30.4 7.1 %collective-permute-start.7 = (f32[2,32,512]{2,1,0:T(8,128)S(1)}, f32[2,32,512]{2,1,0:T(8,128)S(1)}, u32[]{:S(2)}, u32[]{:S(2)}) collective-permute-start(f32[2,32,512]{2,1,0:T(8,128)S(1)} %select_bitcast_fusion.1), channel_id=1, source_target_pairs={{0,16},{4,20},{8,24},{12,28},{16,0},{20,4},{24,8},{28,12},{1,17},{... | collective-permute-start | bytes 393224 | tf_op jit(solution)/shard_map/ppermute | solution.py:350
  37.6 28.9 %collective-permute-start.8 = (bf16[32,512]{1,0:T(8,128)(2,1)S(1)}, bf16[32,512]{1,0:T(8,128)(2,1)S(1)}, u32[]{:S(2)}, u32[]{:S(2)}) collective-permute-start(bf16[32,512]{1,0:T(8,128)(2,1)S(1)} %fusion.26), channel_id=1, source_target_pairs={{0,8},{4,12},{8,0},{12,4},{16,24},{20,28},{24,16},{28,20},{1,9},{5... | collective-permute-start | bytes 98312 | tf_op jit(solution)/shard_map/ppermute | solution.py:350
  40.2 34.5 %collective-permute-start.9 = (bf16[512,128]{1,0:T(8,128)(2,1)S(1)}, bf16[512,128]{1,0:T(8,128)(2,1)S(1)}, u32[]{:S(2)}, u32[]{:S(2)}) collective-permute-start(bf16[512,128]{1,0:T(8,128)(2,1)S(1)} %get-tuple-element.22), channel_id=1, source_target_pairs={{0,28},{4,8},{8,4},{12,16},{16,12},{20,24},{24,20},{28,0},{1,29},{... | collective-permute-start | bytes 393224 | tf_op jit(solution)/shard_map/ppermute | solution.py:393
  41.1 25.4 %copy-start = (bf16[1,1,2048,32]{2,3,1,0:T(8,128)(2,1)S(1)}, bf16[1,1,2048,32]{2,3,1,0:T(8,128)(2,1)}, u32[]{:S(2)}) copy-start(bf16[1,1,2048,32]{2,3,1,0:T(8,128)(2,1)} %param.14) | copy-start | bytes 393220
